TPU v7x, 32 devices: a whole 2x2x4 slice. The times are simulated.
32 devices in a mesh: seq: 8 (over y, x, core), head: 4 (over z).
Axes of the slice: x: 2, y: 2, z: 4, core: 2. Of those that a mesh axis runs over, the one named last changes fastest.
Arguments:
- query: bfloat16 [2, 1024, 4096], P(None, 'seq', 'head'), may hold values from -5 to 5
- keys: bfloat16 [2, 1024, 1024], P(None, 'seq', 'head'), may hold values from -5 to 5
- values: bfloat16 [2, 1024, 1024], P(None, 'seq', 'head'), may hold values from -12 to 12
- norm_gain: float32 [4096], P('head'), may hold values from 0.25 to 1.75
- in_b: bfloat16 [2048, 128], P('seq'), may hold values from -0.25 to 0.25
- out_c: bfloat16 [2048, 128], P('seq'), may hold values from -0.25 to 0.25
- step: float32 [64, 2048], P('head', 'seq'), may hold values from 0.2 to 1
- log_decay: float32 [64, 2048], P('head', 'seq'), may hold values from -2 to 0
- skip: float32 [64], P('head'), may hold values from 0.5 to 1.5
Outputs:
- mixed: bfloat16 [2048, 4096], P('seq', 'head')
All inputs are finite; a program needn't handle non-finite values.
Results may differ from a plain program's by a relative error of at most 0.012.
Values may be sent and summed in bfloat16 or wider, within the bound.
No kernel may reach another device: no remote copies, remote signals or barrier semaphores. Data moves between devices by JAX's collectives and lax.ppermute only.
A program may use at most 128 MiB of HBM per device.

v0:
```python
import math

import jax
import jax.numpy as jnp
from jax import lax
from jax.sharding import PartitionSpec as P

HEADS = 32
HDIM = 128
SDIM = 64
STATE = 128
SPAN = 256


def from_behind(block, axis, distance):
    devices = range(lax.axis_size(axis))
    route = [((i - distance) % len(devices), i) for i in devices]
    return lax.ppermute(block, axis, route)


def partner(block, axis, stride):
    count = lax.axis_size(axis)
    route = []
    for low in range(count):
        high = low | 1 << stride
        if high != low and high < count:
            route += [(low, high), (high, low)]
    return lax.ppermute(block, axis, route)


def entering_2(value, axis, join, neutral):
    place = lax.axis_index(axis)
    gathered = jax.tree.map(
        lambda a, kind: lax.all_gather(a.astype(kind), axis), value, (jnp.bfloat16, jnp.bfloat16)
    )
    state = jax.tree.map(lambda a, e: jnp.zeros_like(a) + jnp.asarray(e, a.dtype), value, neutral)

    def one(turn, state):
        return join(
            state,
            jax.tree.map(
                lambda a, own: lax.dynamic_index_in_dim(a, turn, 0, False).astype(own.dtype),
                gathered,
                value,
            ),
        )

    return lax.fori_loop(0, place, one, state)


def combine_states(earlier, later):
    return (earlier[0] + later[0], jnp.exp(later[0])[:, None, None] * earlier[1] + later[1])


def body(query, keys, values, norm_gain, in_b, out_c, step, log_decay, skip):
    seq_count = lax.axis_size("seq")
    seq_index = lax.axis_index("seq")
    blk_rows = query.shape[1]
    feat_local = query.shape[2]
    kv_local = keys.shape[2] // HDIM
    group_size = feat_local // HDIM // kv_local
    score_scale = 1.0 / math.sqrt(HDIM)
    near_kv = from_behind((keys, values), "seq", 1)
    far_kv = from_behind((near_kv[0], near_kv[1]), "seq", 1)
    near_kv = tuple((jnp.where(seq_index == 0, member[::-1], member) for member in near_kv))
    far_kv = tuple((jnp.where(seq_index < 2, member[::-1], member) for member in far_kv))
    outputs = []
    for slot_id in range(2):
        block_id = seq_index + seq_count * slot_id
        key_rows = jnp.concatenate([far_kv[0][slot_id], near_kv[0][slot_id], keys[slot_id]], 0)
        val_rows = jnp.concatenate([far_kv[1][slot_id], near_kv[1][slot_id], values[slot_id]], 0)
        query_heads = query[slot_id].reshape(blk_rows, kv_local, group_size, HDIM)
        key_heads = key_rows.reshape(3 * blk_rows, kv_local, HDIM)
        val_heads = val_rows.reshape(3 * blk_rows, kv_local, HDIM)
        scores = (
            jnp.einsum("qgjd,kgd->gjqk", query_heads, key_heads, preferred_element_type=jnp.float32)
            * score_scale
        )
        query_pos = block_id * blk_rows + jnp.arange(blk_rows, dtype=jnp.int32)
        key_pos = (block_id - 2) * blk_rows + jnp.arange(3 * blk_rows, dtype=jnp.int32)
        window = 2 * blk_rows
        allowed = (
            (key_pos[None, :] <= query_pos[:, None])
            & (key_pos[None, :] > query_pos[:, None] - window)
            & (key_pos[None, :] >= 0)
        )
        scores = jnp.where(allowed, scores, -jnp.inf)
        row_peak = jnp.max(scores, axis=-1, keepdims=True)
        exp_terms = jnp.exp(scores - row_peak)
        row_total = jnp.sum(exp_terms, axis=-1)
        weights = exp_terms.astype(jnp.bfloat16)
        result = jnp.einsum(
            "gjqk,kgd->qgjd", weights, val_heads, preferred_element_type=jnp.float32
        )
        result = result / jnp.transpose(row_total, (2, 0, 1))[..., None]
        outputs.append(result.reshape(blk_rows, feat_local).astype(jnp.bfloat16))
    lead_slot = outputs[0]
    tail_slot = outputs[1]
    for bit_pos in reversed(range(seq_count.bit_length() - 1)):
        upper_half = jnp.right_shift(seq_index, bit_pos) % 2 == 1
        outgoing = jnp.where(upper_half, lead_slot, tail_slot)
        incoming = partner(outgoing, "seq", bit_pos)
        lead_slot = jnp.where(upper_half, incoming, lead_slot)
        tail_slot = jnp.where(upper_half, tail_slot, incoming)
    attended = jnp.concatenate([lead_slot, tail_slot], 0)
    widened = attended.astype(jnp.float32)
    row_sums = lax.psum(jnp.sum(widened * widened, axis=-1), "head")
    meansq = row_sums / (HEADS * HDIM)
    normed = (widened * norm_gain[None, :] * lax.rsqrt(meansq + 1e-06)[:, None]).astype(
        jnp.bfloat16
    )
    highest = lax.Precision.HIGHEST
    tok_rows = normed.shape[0]
    heads_ssm = step.shape[0]
    span_count = tok_rows // SPAN
    inputs_low = normed.reshape(span_count, SPAN, heads_ssm, SDIM)
    inputs = inputs_low.astype(jnp.float32)
    in_low = in_b.reshape(span_count, SPAN, STATE)
    out_low = out_c.reshape(span_count, SPAN, STATE)
    in_rows = in_low.astype(jnp.float32)
    out_rows = out_low.astype(jnp.float32)
    step_rows = step.reshape(heads_ssm, span_count, SPAN).transpose(1, 0, 2)
    decay_rows = log_decay.reshape(heads_ssm, span_count, SPAN).transpose(1, 0, 2)
    cum_log = jnp.cumsum(decay_rows, axis=2)
    causal = jnp.arange(SPAN)[:, None] >= jnp.arange(SPAN)[None, :]
    decay_mat = jnp.exp(
        jnp.where(causal[None, None], cum_log[:, :, :, None] - cum_log[:, :, None, :], -jnp.inf)
    )
    cross_terms = jnp.einsum("ctn,cun->ctu", out_low, in_low, preferred_element_type=jnp.float32)
    mixing = (decay_mat * cross_terms[:, None] * step_rows[:, :, None, :]).astype(jnp.bfloat16)
    local_out = jnp.einsum(
        "chtu,cuhe->cthe", mixing, inputs_low, preferred_element_type=jnp.float32
    )
    span_totals = cum_log[:, :, -1]
    end_weights = jnp.exp(span_totals[:, :, None] - cum_log) * step_rows
    weighted = end_weights.transpose(0, 2, 1)[..., None] * inputs
    span_states = jnp.einsum("cuhe,cun->chen", weighted, in_rows, precision=highest)
    incl_log = jnp.cumsum(span_totals, axis=0)
    excl_log = incl_log - span_totals
    dev_total = incl_log[-1]
    dev_state = jnp.einsum(
        "ch,chen->hen", jnp.exp(dev_total[None, :] - incl_log), span_states, precision=highest
    )
    earlier_mask = jnp.arange(span_count)[:, None] > jnp.arange(span_count)[None, :]
    pair_weights = jnp.exp(
        jnp.where(earlier_mask[:, :, None], excl_log[:, None, :] - incl_log[None, :, :], -jnp.inf)
    )
    local_start = jnp.einsum("kjh,jhen->khen", pair_weights, span_states, precision=highest)
    entry_scale = jnp.exp(cum_log).transpose(0, 2, 1)[..., None]
    identity = (
        jnp.zeros((heads_ssm,), jnp.float32),
        jnp.zeros((heads_ssm, SDIM, STATE), jnp.float32),
    )
    entry_term = (
        jnp.einsum("ctn,chen->cthe", out_rows, local_start, precision=highest) * entry_scale
    )
    partial_value = local_out + entry_term
    entering = entering_2((dev_total, dev_state), "seq", combine_states, identity)[1]
    correction = jnp.einsum("ctn,hen->cthe", out_rows, entering, precision=highest)
    offset_scale = jnp.exp(excl_log[:, None, :] + cum_log.transpose(0, 2, 1))[..., None]
    result = partial_value + correction * offset_scale
    result = result + skip[None, None, :, None] * inputs
    return result.reshape(tok_rows, heads_ssm * SDIM).astype(jnp.bfloat16)


def solution(mesh):
    placed = (
        P(None, "seq", "head"),
        P(None, "seq", "head"),
        P(None, "seq", "head"),
        P("head"),
        P("seq", None),
        P("seq", None),
        P("head", "seq"),
        P("head", "seq"),
        P("head"),
    )
    return jax.shard_map(
        body, mesh=mesh, in_specs=placed, out_specs=P("seq", "head"), check_vma=False
    )
```

profile of v0, /device:TPU:7, one launch (start us, length us, event | category | flops | bytes accessed | tf_op | source)
XLA Modules:
  0.0 94.2 jit_solution(1609227975789895635)
XLA Ops:
  6.5 1.1 %copy.121 = bf16[2,128,256]{1,2,0:T(8,128)(2,1)S(1)} copy(bf16[2,128,256]{2,1,0:T(8,128)(2,1)} %param.12) | data formatting | bytes 262144 | tf_op args[1]
  7.7 1.0 %copy.119 = bf16[2,128,256]{1,2,0:T(8,128)(2,1)S(1)} copy(bf16[2,128,256]{2,1,0:T(8,128)(2,1)} %param.13) | data formatting | bytes 262144 | tf_op args[2]
  11.4 2.4 %collective-permute-start.3 = (bf16[2,128,256]{1,2,0:T(8,128)(2,1)S(1)}, bf16[2,128,256]{1,2,0:T(8,128)(2,1)S(1)}, u32[]{:S(2)}, u32[]{:S(2)}) collective-permute-start(bf16[2,128,256]{1,2,0:T(8,128)(2,1)S(1)} %collective-permute-done.2), channel_id=1, source_target_pairs={{28,0},{0,4},{4,8},{8,12},{12,16},{16,20},{20,24},{24,28},{29,1},{... | collective-permute-start | bytes 393224 | tf_op jit(solution)/shard_map/ppermute | solution.py:18
  14.4 1.3 %collective-permute-done.3 = bf16[2,128,256]{1,2,0:T(8,128)(2,1)S(1)} collective-permute-done((bf16[2,128,256]{1,2,0:T(8,128)(2,1)S(1)}, bf16[2,128,256]{1,2,0:T(8,128)(2,1)S(1)}, u32[]{:S(2)}, u32[]{:S(2)}) %collective-permute-start.3) | collective-permute-done | bytes 131104 | tf_op jit(solution)/shard_map/ppermute | solution.py:18
  15.7 1.4 %collective-permute-done.1 = bf16[2,128,256]{1,2,0:T(8,128)(2,1)S(1)} collective-permute-done((bf16[2,128,256]{1,2,0:T(8,128)(2,1)S(1)}, bf16[2,128,256]{1,2,0:T(8,128)(2,1)S(1)}, u32[]{:S(2)}, u32[]{:S(2)}) %collective-permute-start.1) | collective-permute-done | bytes 131104 | tf_op jit(solution)/shard_map/ppermute | solution.py:18
  19.6 1.6 %collective-permute-start.4 = (bf16[128,1024]{0,1:T(8,128)(2,1)S(1)}, bf16[128,1024]{0,1:T(8,128)(2,1)S(1)}, u32[]{:S(2)}, u32[]{:S(2)}) collective-permute-start(bf16[128,1024]{0,1:T(8,128)(2,1)S(1)} %bitcast_select_fusion.3), channel_id=1, source_target_pairs={{0,16},{16,0},{4,20},{20,4},{8,24},{24,8},{12,28},{28,12},{1,17},{... | collective-permute-start | bytes 786440 | tf_op jit(solution)/shard_map/ppermute | solution.py:28
  22.0 3.9 %collective-permute-done.4 = bf16[128,1024]{0,1:T(8,128)(2,1)S(1)} collective-permute-done((bf16[128,1024]{0,1:T(8,128)(2,1)S(1)}, bf16[128,1024]{0,1:T(8,128)(2,1)S(1)}, u32[]{:S(2)}, u32[]{:S(2)}) %collective-permute-start.4) | collective-permute-done | bytes 262176 | tf_op jit(solution)/shard_map/ppermute | solution.py:28
  26.3 5.0 %collective-permute-done.5 = bf16[128,1024]{0,1:T(8,128)(2,1)S(1)} collective-permute-done((bf16[128,1024]{0,1:T(8,128)(2,1)S(1)}, bf16[128,1024]{0,1:T(8,128)(2,1)S(1)}, u32[]{:S(2)}, u32[]{:S(2)}) %collective-permute-start.5) | collective-permute-done | bytes 262176 | tf_op jit(solution)/shard_map/ppermute | solution.py:28
  31.3 3.8 %collective-permute-start.6 = (bf16[128,1024]{0,1:T(8,128)(2,1)S(1)}, bf16[128,1024]{0,1:T(8,128)(2,1)S(1)}, u32[]{:S(2)}, u32[]{:S(2)}) collective-permute-start(bf16[128,1024]{0,1:T(8,128)(2,1)S(1)} %broadcast_select_fusion.5), channel_id=1, source_target_pairs={{0,4},{4,0},{8,12},{12,8},{16,20},{20,16},{24,28},{28,24},{1,5},{5... | collective-permute-start | bytes 786440 | tf_op jit(solution)/shard_map/ppermute | solution.py:28
  35.4 0.9 collective-permute-done.6
  36.5 10.2 %psum.7 = f32[256]{0:T(256)S(1)} all-reduce(f32[256]{0:T(256)S(1)} %multiply_reduce_fusion), channel_id=1, replica_groups=mesh['seq'=8,'head'=4] {'head'}, use_global_device_ids=true, to_apply=%region_5.6 | all-reduce | flops 256 | bytes 2048 | tf_op jit(solution)/shard_map/psum | solution.py:107
  46.7 1.5 %multiply_convert_fusion.14 = (bf16[16,64,128]{2,1,0:T(8,128)(2,1)}, f32[16,64,128]{2,1,0:T(8,128)S(1)}) fusion(f32[16]{0:T(128)S(1)} %get-tuple-element.72, bf16[256,128]{1,0:T(8,128)(2,1)S(1)} %copy-done.2, f32[256,16]{0,1:T(8,128)S(1)} %get-tuple-element.65, f32[256]{0:T(256)S(1)} %add_rsqrt_fusion, f32[16,64]{1,0:T(8,128)S(1)} %mul.192, ...), kind=kOutput, calls=%fused_computation.43 | convolution fusion | flops 405274624 | bytes 1397824 | tf_op jit(solution)/shard_map/cuhe,cun->chen/dot_general | solution.py:137
  48.2 11.5 %all-gather = bf16[8,16,1]{1,2,0:T(2,128)(2,1)S(1)} all-gather(bf16[1,16,1]{1,2,0:T(2,128)(2,1)S(1)} %slice.88), channel_id=2, replica_groups=mesh['seq'=8,'head'=4] {'seq'}, dimensions={0}, use_global_device_ids=true | all-gather | bytes 288 | tf_op jit(solution)/shard_map/all_gather | solution.py:34
  60.7 15.3 %all-gather.4.cloned.1.call-done = bf16[128,64,128]{2,1,0:T(8,128)(2,1)} async-done(((bf16[16,64,128]{2,1,0:T(8,128)(2,1)}), bf16[128,64,128]{2,1,0:T(8,128)(2,1)}) %all-gather.4.cloned.1.call-update) | async-done | bytes 2097168 | tf_op jit(solution)/shard_map/all_gather | solution.py:34
  76.0 8.1 %while.12 = (s32[]{:T(128)}, f32[16,64,128]{2,1,0:T(8,128)S(1)}, s32[]{:T(128)}, bf16[8,16]{1,0:T(8,128)(2,1)S(1)}, bf16[8,16,64,128]{3,2,1,0:T(8,128)(2,1)}, /*index=5*/s32[]{:T(128)}, s32[]{:T(128)}, s32[]{:T(128)}) while((s32[]{:T(128)}, f32[16,64,128]{2,1,0:T(8,128)S(1)}, s32[]{:T(128)}, bf16[8,16]{1,0:T(8,128)(2,1)S(1)}, ...), condition=%wide.region_9.10_spmd, body=%wide.region_8.9_spmd.sunk | while | flops 393237 | bytes 1311007 | solution.py:48
  76.0 1.1 %convert_add_fusion.2 = f32[16,64,128]{2,1,0:T(8,128)S(1)} fusion(f32[16,64,128]{2,1,0:T(8,128)S(1)} %get-tuple-element.138, bf16[8,16,64,128]{3,2,1,0:T(8,128)(2,1)} %get-tuple-element.149, s32[]{:T(128)S(6)} %select_n.192, f32[16]{0:T(128)S(1)} %exponential_bitcast_fusion.4), kind=kLoop, calls=%fused_computation.clone.1 | loop fusion | flops 393216 | bytes 1310788 | tf_op jit(solution)/shard_map/while/body/add | solution.py:52
  77.2 1.1 %convert_add_fusion.2 = f32[16,64,128]{2,1,0:T(8,128)S(1)} fusion(f32[16,64,128]{2,1,0:T(8,128)S(1)} %get-tuple-element.138, bf16[8,16,64,128]{3,2,1,0:T(8,128)(2,1)} %get-tuple-element.149, s32[]{:T(128)S(6)} %select_n.192, f32[16]{0:T(128)S(1)} %exponential_bitcast_fusion.4), kind=kLoop, calls=%fused_computation.clone.1 | loop fusion | flops 393216 | bytes 1310788 | tf_op jit(solution)/shard_map/while/body/add | solution.py:52
  78.4 1.1 %convert_add_fusion.2 = f32[16,64,128]{2,1,0:T(8,128)S(1)} fusion(f32[16,64,128]{2,1,0:T(8,128)S(1)} %get-tuple-element.138, bf16[8,16,64,128]{3,2,1,0:T(8,128)(2,1)} %get-tuple-element.149, s32[]{:T(128)S(6)} %select_n.192, f32[16]{0:T(128)S(1)} %exponential_bitcast_fusion.4), kind=kLoop, calls=%fused_computation.clone.1 | loop fusion | flops 393216 | bytes 1310788 | tf_op jit(solution)/shard_map/while/body/add | solution.py:52
  79.5 1.1 %convert_add_fusion.2 = f32[16,64,128]{2,1,0:T(8,128)S(1)} fusion(f32[16,64,128]{2,1,0:T(8,128)S(1)} %get-tuple-element.138, bf16[8,16,64,128]{3,2,1,0:T(8,128)(2,1)} %get-tuple-element.149, s32[]{:T(128)S(6)} %select_n.192, f32[16]{0:T(128)S(1)} %exponential_bitcast_fusion.4), kind=kLoop, calls=%fused_computation.clone.1 | loop fusion | flops 393216 | bytes 1310788 | tf_op jit(solution)/shard_map/while/body/add | solution.py:52
  80.7 1.1 %convert_add_fusion.2 = f32[16,64,128]{2,1,0:T(8,128)S(1)} fusion(f32[16,64,128]{2,1,0:T(8,128)S(1)} %get-tuple-element.138, bf16[8,16,64,128]{3,2,1,0:T(8,128)(2,1)} %get-tuple-element.149, s32[]{:T(128)S(6)} %select_n.192, f32[16]{0:T(128)S(1)} %exponential_bitcast_fusion.4), kind=kLoop, calls=%fused_computation.clone.1 | loop fusion | flops 393216 | bytes 1310788 | tf_op jit(solution)/shard_map/while/body/add | solution.py:52
  81.8 1.1 %convert_add_fusion.2 = f32[16,64,128]{2,1,0:T(8,128)S(1)} fusion(f32[16,64,128]{2,1,0:T(8,128)S(1)} %get-tuple-element.138, bf16[8,16,64,128]{3,2,1,0:T(8,128)(2,1)} %get-tuple-element.149, s32[]{:T(128)S(6)} %select_n.192, f32[16]{0:T(128)S(1)} %exponential_bitcast_fusion.4), kind=kLoop, calls=%fused_computation.clone.1 | loop fusion | flops 393216 | bytes 1310788 | tf_op jit(solution)/shard_map/while/body/add | solution.py:52
  83.0 1.1 %convert_add_fusion.2 = f32[16,64,128]{2,1,0:T(8,128)S(1)} fusion(f32[16,64,128]{2,1,0:T(8,128)S(1)} %get-tuple-element.138, bf16[8,16,64,128]{3,2,1,0:T(8,128)(2,1)} %get-tuple-element.149, s32[]{:T(128)S(6)} %select_n.192, f32[16]{0:T(128)S(1)} %exponential_bitcast_fusion.4), kind=kLoop, calls=%fused_computation.clone.1 | loop fusion | flops 393216 | bytes 1310788 | tf_op jit(solution)/shard_map/while/body/add | solution.py:52
  84.8 1.6 %fusion.19 = bf16[1,256,16,64]{1,3,2,0:T(8,128)(2,1)S(1)} fusion(f32[1,256,16,64]{1,3,2,0:T(8,128)S(1)} %fusion.15, f32[1,256,16,64]{1,3,2,0:T(8,128)S(1)} %fusion.13, f32[16,256]{1,0:T(8,128)S(1)} %copy-done.3, f32[256,256]{1,0:T(8,128)S(1)} %fusion.72, f32[16,256]{1,0:T(8,128)S(1)} %get-tuple-element.66, pred[256,256]{1,0:T(8,128)(4,1)S(1)} %iota_compare_fusion, ...), kind=kOutput, calls=%fused_computation.28 | convolution fusion | flops 144703488 | bytes 4035648 | tf_op jit(solution)/shard_map/chtu,cuhe->cthe/dot_general | solution.py:131
  86.4 1.0 %copy.144 = bf16[256,1024]{1,0:T(8,128)(2,1)} copy(bf16[256,1024]{0,1:T(8,128)(2,1)S(1)} %bitcast.165) | data formatting | bytes 1048576 | tf_op jit(solution)/shard_map/convert_element_type | solution.py:163
  (95 shorter events, 9.0 us)
Async XLA Ops:
  6.5 53.3 %copy-start = (bf16[256,128]{1,0:T(8,128)(2,1)S(1)}, bf16[256,128]{1,0:T(8,128)(2,1)}, u32[]{:S(2)}) copy-start(bf16[256,128]{1,0:T(8,128)(2,1)} %param.16) | copy-start | bytes 196612
  6.5 3.4 %copy-start.1 = (bf16[2,128,1024]{2,1,0:T(8,128)(2,1)S(1)}, bf16[2,128,1024]{2,1,0:T(8,128)(2,1)}, u32[]{:S(2)}) copy-start(bf16[2,128,1024]{2,1,0:T(8,128)(2,1)} %param.11) | copy-start | bytes 1572868
  6.5 69.4 %all-gather.4.cloned.1.call-start = ((), (), s32[]{:S(2)}) async-start(), calls=%async_computation | async-start | bytes 2359296 | tf_op jit(solution)/shard_map/all_gather | solution.py:34
  7.6 3.4 %collective-permute-start.2 = (bf16[2,128,256]{1,2,0:T(8,128)(2,1)S(1)}, bf16[2,128,256]{1,2,0:T(8,128)(2,1)S(1)}, u32[]{:S(2)}, u32[]{:S(2)}) collective-permute-start(bf16[2,128,256]{1,2,0:T(8,128)(2,1)S(1)} %copy.121), channel_id=1, source_target_pairs={{28,0},{0,4},{4,8},{8,12},{12,16},{16,20},{20,24},{24,28},{29,1},{... | collective-permute-start | bytes 393224 | tf_op jit(solution)/shard_map/ppermute | solution.py:18
  8.7 5.0 %collective-permute-start = (bf16[2,128,256]{1,2,0:T(8,128)(2,1)S(1)}, bf16[2,128,256]{1,2,0:T(8,128)(2,1)S(1)}, u32[]{:S(2)}, u32[]{:S(2)}) collective-permute-start(bf16[2,128,256]{1,2,0:T(8,128)(2,1)S(1)} %copy.119), channel_id=1, source_target_pairs={{28,0},{0,4},{4,8},{8,12},{12,16},{16,20},{20,24},{24,28},{29,1},{... | collective-permute-start | bytes 393224 | tf_op jit(solution)/shard_map/ppermute | solution.py:18
  11.4 4.3 %collective-permute-start.3 = (bf16[2,128,256]{1,2,0:T(8,128)(2,1)S(1)}, bf16[2,128,256]{1,2,0:T(8,128)(2,1)S(1)}, u32[]{:S(2)}, u32[]{:S(2)}) collective-permute-start(bf16[2,128,256]{1,2,0:T(8,128)(2,1)S(1)} %collective-permute-done.2), channel_id=1, source_target_pairs={{28,0},{0,4},{4,8},{8,12},{12,16},{16,20},{20,24},{24,28},{29,1},{... | collective-permute-start | bytes 393224 | tf_op jit(solution)/shard_map/ppermute | solution.py:18
  13.8 3.3 %collective-permute-start.1 = (bf16[2,128,256]{1,2,0:T(8,128)(2,1)S(1)}, bf16[2,128,256]{1,2,0:T(8,128)(2,1)S(1)}, u32[]{:S(2)}, u32[]{:S(2)}) collective-permute-start(bf16[2,128,256]{1,2,0:T(8,128)(2,1)S(1)} %collective-permute-done), channel_id=1, source_target_pairs={{28,0},{0,4},{4,8},{8,12},{12,16},{16,20},{20,24},{24,28},{29,1},{... | collective-permute-start | bytes 393224 | tf_op jit(solution)/shard_map/ppermute | solution.py:18
  19.1 2.1 %copy-start.4 = (f32[16,256]{1,0:T(8,128)S(1)}, f32[16,256]{1,0:T(8,128)}, u32[]{:S(2)}) copy-start(f32[16,256]{1,0:T(8,128)} %param.18) | copy-start | bytes 49156
  19.6 6.3 %collective-permute-start.4 = (bf16[128,1024]{0,1:T(8,128)(2,1)S(1)}, bf16[128,1024]{0,1:T(8,128)(2,1)S(1)}, u32[]{:S(2)}, u32[]{:S(2)}) collective-permute-start(bf16[128,1024]{0,1:T(8,128)(2,1)S(1)} %bitcast_select_fusion.3), channel_id=1, source_target_pairs={{0,16},{16,0},{4,20},{20,4},{8,24},{24,8},{12,28},{28,12},{1,17},{... | collective-permute-start | bytes 786440 | tf_op jit(solution)/shard_map/ppermute | solution.py:28
  22.0 13.2 %copy-start.5 = (f32[1024]{0:T(1024)S(1)}, f32[1024]{0:T(1024)}, u32[]{:S(2)}) copy-start(f32[1024]{0:T(1024)} %param.14) | copy-start | bytes 12292
  22.0 13.3 %copy-start.3 = (f32[16,256]{1,0:T(8,128)S(1)}, f32[16,256]{1,0:T(8,128)}, u32[]{:S(2)}) copy-start(f32[16,256]{1,0:T(8,128)} %param.17) | copy-start | bytes 49156
  26.0 5.3 %collective-permute-start.5 = (bf16[128,1024]{0,1:T(8,128)(2,1)S(1)}, bf16[128,1024]{0,1:T(8,128)(2,1)S(1)}, u32[]{:S(2)}, u32[]{:S(2)}) collective-permute-start(bf16[128,1024]{0,1:T(8,128)(2,1)S(1)} %get-tuple-element.62), channel_id=1, source_target_pairs={{0,8},{8,0},{4,12},{12,4},{16,24},{24,16},{20,28},{28,20},{1,9},{9... | collective-permute-start | bytes 786440 | tf_op jit(solution)/shard_map/ppermute | solution.py:28
  31.3 15.4 %copy-start.2 = (bf16[256,128]{1,0:T(8,128)(2,1)S(1)}, bf16[256,128]{1,0:T(8,128)(2,1)}, u32[]{:S(2)}) copy-start(bf16[256,128]{1,0:T(8,128)(2,1)} %param.15) | copy-start | bytes 196612
  31.3 4.9 %collective-permute-start.6 = (bf16[128,1024]{0,1:T(8,128)(2,1)S(1)}, bf16[128,1024]{0,1:T(8,128)(2,1)S(1)}, u32[]{:S(2)}, u32[]{:S(2)}) collective-permute-start(bf16[128,1024]{0,1:T(8,128)(2,1)S(1)} %broadcast_select_fusion.5), channel_id=1, source_target_pairs={{0,4},{4,0},{8,12},{12,8},{16,20},{20,16},{24,28},{28,24},{1,5},{5... | collective-permute-start | bytes 786440 | tf_op jit(solution)/shard_map/ppermute | solution.py:28
  84.1 0.7 copy-start.6
Sparse Core Ops, SparseCore 0:
  48.3 27.5 all-gather.3
where the time goes:
time: 94.6 us; the launch traced here: 94.2 us
  waiting for transfers between devices  27.7 us (29%)
  blocking collectives  21.6 us (23%)
  between operations  13.9 us (15%)
  other arithmetic  10 us (11%)
  starting transfers between devices  8.6 us (9%)
  local copies, waits for them, and re-layouts  6.09 us (6%)
  matrix products  5.98 us (6%)
    all_gather x1, waiting for transfers between devices, entering_2(): lax.all_gather(a.astype(kind), axis)  15.3 us
    all_gather x1, blocking collectives, entering_2(): lax.all_gather(a.astype(kind), axis)  11.5 us
    psum x1, blocking collectives, body(): row_sums = lax.psum(jnp.sum(widened * widened, axis=-1), 'head')  10.2 us
    ppermute x3, waiting for transfers between devices, partner(): return lax.ppermute(block, axis, route)  9.79 us
    add x7, other arithmetic, combine_states(): jnp.exp(later[0])[:, None, None] * earlier[1] + later[1]  7.78 us
    ppermute x3, starting transfers between devices, partner(): return lax.ppermute(block, axis, route)  5.49 us
    ppermute x4, starting transfers between devices, from_behind(): return lax.ppermute(block, axis, route)  3.1 us
    ppermute x4, waiting for transfers between devices, from_behind(): return lax.ppermute(block, axis, route)  2.65 us
  transfers between devices with their start and end apart: 8, of which 6 were waited for; matrix products, arithmetic and copies ran while one was open for 6% of the time, Pallas kernels for 0%

commit v1 on v0

v1 whole, which is shorter than its diff:
```python
import functools
import math

import jax
import jax.numpy as jnp
from jax import lax
from jax.experimental import pallas as pl
from jax.experimental.pallas import tpu as pltpu
from jax.sharding import PartitionSpec as P


HEADS = 32
HDIM = 128
SDIM = 64
STATE = 128

F32 = jnp.float32
BF16 = jnp.bfloat16
VMEM = pltpu.VMEM
GRANT = 12 << 20


def dot(a, b, contract=(1, 0), precision=None):
    return lax.dot_general(
        a,
        b,
        (((contract[0],), (contract[1],)), ((), ())),
        precision=precision,
        preferred_element_type=F32,
    )


def call(kernel, outs, args, flops=1, spaces=None):
    spaces = spaces or [VMEM] * len(args)
    return pl.pallas_call(
        kernel,
        out_shape=[jax.ShapeDtypeStruct(s, d) for s, d in outs],
        in_specs=[pl.BlockSpec(memory_space=m) for m in spaces],
        out_specs=[pl.BlockSpec(memory_space=VMEM)] * len(outs),
        compiler_params=pltpu.CompilerParams(vmem_limit_bytes=GRANT),
        cost_estimate=pl.CostEstimate(flops=flops, bytes_accessed=1 << 20, transcendentals=0),
    )(*args)


def pack_kernel(k_ref, v_ref, out_ref):
    width = k_ref.shape[2]

    def inner(sems):
        copies = [
            pltpu.make_async_copy(ref, out_ref.at[:, :, i * width : (i + 1) * width], sems.at[i])
            for i, ref in enumerate((k_ref, v_ref))
        ]
        for copy in copies:
            copy.start()
        for copy in copies:
            copy.wait()

    pl.run_scoped(inner, pltpu.SemaphoreType.DMA((2,)))


def prepare_kernel(step_ref, log_ref, b_ref, c_ref, skip_ref, mix_ref, bw_ref, scale_ref, tot_ref, pass_ref):
    heads, toks = step_ref.shape
    half = toks // 2
    highest = lax.Precision.HIGHEST
    log = log_ref[...]
    step = step_ref[...]
    rows = lax.broadcasted_iota(jnp.int32, (toks, toks), 0)
    cols = lax.broadcasted_iota(jnp.int32, (toks, toks), 1)
    lower = (rows >= cols).astype(F32)
    cum = dot(log, lower, (1, 1), highest)
    cum_cols = dot(lower, log, (1, 1), highest)
    total = cum[:, toks - 1 :]
    weight = jnp.exp(total - cum) * step
    cross = dot(c_ref[...], b_ref[...], (1, 1))
    b_t = jnp.transpose(b_ref[...].astype(F32))
    causal = (
        lax.broadcasted_iota(jnp.int32, (half, half), 0)
        >= lax.broadcasted_iota(jnp.int32, (half, half), 1)
    )
    lanes = lax.broadcasted_iota(jnp.int32, (toks, HDIM), 1)
    for pair in range(heads // 2):
        for side in range(2):
            k = 2 * pair + side
            at = side * toks
            for r in range(2):
                for c in range(2):
                    dst = (pair, slice(r * half, (r + 1) * half), slice(at + c * half, at + (c + 1) * half))
                    if c > r:
                        mix_ref[dst] = jnp.zeros((half, half), BF16)
                        continue
                    rs, cs = slice(r * half, (r + 1) * half), slice(c * half, (c + 1) * half)
                    gap = cum_cols[rs, k : k + 1] - cum[k : k + 1, cs]
                    if r == c:
                        gap = jnp.where(causal, gap, -jnp.inf)
                    mix_ref[dst] = (jnp.exp(gap) * cross[rs, cs] * step[k : k + 1, cs]).astype(BF16)
            bw_ref[pair, :, at : at + toks] = (b_t * weight[k : k + 1, :]).astype(BF16)
        both = jnp.where(
            lanes < SDIM,
            cum_cols[:, 2 * pair : 2 * pair + 1],
            cum_cols[:, 2 * pair + 1 : 2 * pair + 2],
        )
        both = jnp.exp(both)
        scale_ref[:, pair * HDIM : (pair + 1) * HDIM] = both
        tot_ref[:, pair * HDIM : (pair + 1) * HDIM] = both[toks - 1 :, :]
        pass_ref[:, pair * HDIM : (pair + 1) * HDIM] = jnp.where(
            lanes[:1] < SDIM, skip_ref[2 * pair], skip_ref[2 * pair + 1]
        )


def attention_kernel(second, q_ref, kv_ref, near_ref, far_even_ref, far_odd_ref, *refs):
    if second:
        before_ref, out_ref, sums_ref = refs
    else:
        out_ref, sums_ref = refs
    me, count = lax.axis_index("seq"), lax.axis_size("seq")
    blk, feat = q_ref.shape[1:]
    kv_local = kv_ref.shape[2] // (2 * HDIM)
    group = feat // HDIM // kv_local
    odd = me % 2
    slot = 1 - odd if second else odd
    near_slot = jnp.where(me < 1, 0, slot)
    far_slot = jnp.where(me < 2, 0, slot)
    block = slot * count + me
    rows = lax.broadcasted_iota(jnp.int32, (group * blk, blk), 0) % blk
    cols = lax.broadcasted_iota(jnp.int32, (group * blk, blk), 1)
    own_ok = cols <= rows
    far_ok = (cols > rows) & (block >= 2)
    near_ok = (cols >= 0) & (block >= 1)
    factor = math.log2(math.e) / math.sqrt(HDIM)
    squares = jnp.zeros((blk, 1), F32)

    def take(column):
        at = slice(column * HDIM, (column + 1) * HDIM)
        far = jnp.where(odd == 1, far_odd_ref[far_slot, :, at], far_even_ref[far_slot, :, at])
        return jnp.concatenate([far, near_ref[near_slot, :, at], kv_ref[slot, :, at]], 0)

    for g in range(kv_local):
        heads = [
            q_ref[slot, :, (g * group + i) * HDIM : (g * group + i + 1) * HDIM] for i in range(group)
        ]
        query = jnp.concatenate(heads, 0)
        score = dot(query, take(g), (1, 1))
        ok = jnp.concatenate([far_ok, near_ok, own_ok], 1)
        score = jnp.where(ok, score, -jnp.inf)
        peak = jnp.max(score, axis=1, keepdims=True)
        terms = jnp.exp2((score - peak) * factor)
        total = jnp.sum(terms, axis=1, keepdims=True)
        result = dot(terms.astype(BF16), take(kv_local + g)) / total
        result = result.astype(BF16)
        wide = result.astype(F32)
        part = jnp.sum(wide * wide, axis=1, keepdims=True)
        for i in range(group):
            out_ref[:, (g * group + i) * HDIM : (g * group + i + 1) * HDIM] = result[
                i * blk : (i + 1) * blk
            ]
            squares = squares + part[i * blk : (i + 1) * blk]
    turned = jnp.transpose(jnp.broadcast_to(squares, (blk, blk)))[:8]
    if second:
        sums_ref[:8] = before_ref[...]
        sums_ref[8:] = turned
    else:
        sums_ref[...] = turned


def home_kernel(xa_ref, xb_ref, ra_ref, rb_ref, gain_ref, bw_ref, x_ref, keep_ref, send_ref):
    me, count = lax.axis_index("seq"), lax.axis_size("seq")
    blk, feat = xa_ref.shape
    upper = me >= count // 2
    pairs = feat // HDIM
    mine = me % 2
    gain = gain_ref[...]
    for part in range(2):
        swap = upper if part == 0 else jnp.logical_not(upper)
        sums = jnp.where(swap, rb_ref[...], ra_ref[...])
        mean = jnp.transpose(jnp.broadcast_to(sums[:1], (blk, blk))) / (HEADS * HDIM)
        inv = lax.rsqrt(mean + 1e-06)[:, :1]
        rows = jnp.where(swap, xb_ref[...], xa_ref[...]).astype(F32)
        x_ref[part * blk : (part + 1) * blk, :] = (rows * gain * inv).astype(BF16)
    lanes = lax.broadcasted_iota(jnp.int32, (2 * blk, HDIM), 1)
    zero = jnp.zeros((2 * blk, HDIM), BF16)
    for p in range(pairs):
        x = x_ref[:, p * HDIM : (p + 1) * HDIM]
        spread = jnp.concatenate([jnp.where(lanes < SDIM, x, zero), jnp.where(lanes < SDIM, zero, x)], 0)
        state = dot(bw_ref[p], spread)
        side = 0 if p < pairs // 2 else 1
        at = (p % (pairs // 2)) * HDIM

        @pl.when(mine == side)
        def _():
            keep_ref[:, at : at + HDIM] = state

        @pl.when(mine != side)
        def _():
            send_ref[:, at : at + HDIM] = state.astype(BF16)


def local_kernel(x_ref, mix_ref, skip_ref, out_ref):
    toks, feat = x_ref.shape
    lanes = lax.broadcasted_iota(jnp.int32, (toks, HDIM), 1)
    zero = jnp.zeros((toks, HDIM), BF16)
    for p in range(feat // HDIM):
        at = slice(p * HDIM, (p + 1) * HDIM)
        x = x_ref[:, at]
        spread = jnp.concatenate([jnp.where(lanes < SDIM, x, zero), jnp.where(lanes < SDIM, zero, x)], 0)
        out_ref[:, at] = dot(mix_ref[p], spread) + skip_ref[:, at] * x.astype(F32)


def final_kernel(local_ref, scale_ref, c_ref, own_ref, other_ref, out_ref):
    mine = lax.axis_index("seq") % 2
    half = own_ref.shape[1]
    for ref, side in ((own_ref, mine), (other_ref, 1 - mine)):
        at = pl.ds(pl.multiple_of(side * half, half), half)
        part = dot(c_ref[...], ref[...])
        out_ref[:, at] = (local_ref[:, at] + part * scale_ref[:, at]).astype(BF16)


def add_kernel(a_ref, b_ref, *out_refs):
    rows = a_ref.shape[0] // len(out_refs)
    for i, ref in enumerate(out_refs):
        at = slice(i * rows, (i + 1) * rows)
        ref[...] = a_ref[at] + b_ref[at]


def half_of(ref, side):
    half = ref.shape[1] // 2
    return ref[:, pl.ds(pl.multiple_of(side * half, half), half)]


def decay_kernel(tot_ref, core_ref, out_ref):
    mine = lax.axis_index("seq") % 2
    out_ref[...] = half_of(tot_ref, mine) * half_of(core_ref, mine)


def times_kernel(a_ref, b_ref, out_ref):
    out_ref[...] = a_ref[...] * b_ref[...]


def chip_kernel(keep_ref, got_ref, tot_ref, core_ref, early_ref, total_ref, low_ref):
    mine = lax.axis_index("seq") % 2
    late = mine == 1
    keep, got = keep_ref[...], got_ref[...].astype(F32)
    second = jnp.where(late, half_of(tot_ref, mine), half_of(core_ref, mine))
    early = jnp.where(late, got, keep)
    total = second * early + jnp.where(late, keep, got)
    early_ref[...] = early
    total_ref[...] = total
    low_ref[...] = total.astype(BF16)


def stage_kernel(bit, total_ref, theirs_ref, mine_ref, decay_ref, enter_in_ref, carried_in_ref, *outs):
    upper = (lax.axis_index("seq") >> bit) % 2 == 1
    theirs = theirs_ref[...].astype(F32)
    enter_ref, carried_ref, next_ref, low_ref = outs
    carried = carried_in_ref[...]
    enter_ref[...] = enter_in_ref[...] + jnp.where(upper, carried * theirs, 0.0)
    carried_ref[...] = jnp.where(upper, carried * decay_ref[...], carried)
    total = total_ref[...]
    total = jnp.where(upper, mine_ref[...] * theirs + total, decay_ref[...] * total + theirs)
    next_ref[...] = total
    low_ref[...] = total.astype(BF16)


def last_kernel(bit, theirs_ref, enter_in_ref, carried_ref, early_ref, tot_ref, core_ref, own_ref, give_ref):
    me = lax.axis_index("seq")
    mine = me % 2
    late = mine == 1
    upper = (me >> bit) % 2 == 1
    enter = enter_in_ref[...]
    enter = enter + jnp.where(upper, carried_ref[...] * theirs_ref[...].astype(F32), 0.0)
    first = jnp.where(late, half_of(core_ref, mine), half_of(tot_ref, mine))
    after = first * enter + early_ref[...]
    own_ref[...] = jnp.where(late, after, enter).astype(BF16)
    give_ref[...] = jnp.where(late, enter, after).astype(BF16)


def layer(query, keys, values, norm_gain, in_b, out_c, step, log_decay, skip):
    seq_count = lax.axis_size("seq")
    head_count = lax.axis_size("head")
    blk, feat = query.shape[1:]
    heads, toks = step.shape
    kv_width = keys.shape[2]
    pairs = heads // 2
    half = feat // 2
    every = range(seq_count)
    any_space = pltpu.HBM

    def swap(block, bit):
        return lax.ppermute(block, "seq", [(i, i ^ (1 << bit)) for i in every])

    (kv,) = call(pack_kernel, [((2, blk, 2 * kv_width), BF16)], (keys, values), spaces=[any_space] * 2)
    near = lax.ppermute(kv, "seq", [(i, (i + 1) % seq_count) for i in every])
    far_even = lax.ppermute(kv, "seq", [(i, (i + 2) % seq_count) for i in every if i % 2 == 0])
    far_odd = lax.ppermute(near, "seq", [(i, i + 1) for i in every if i % 2 == 0])

    mix, b_weighted, scale, tot, skip_row = call(
        prepare_kernel,
        [
            ((pairs, toks, 2 * toks), BF16),
            ((pairs, STATE, 2 * toks), BF16),
            ((toks, feat), F32),
            ((1, feat), F32),
            ((1, feat), F32),
        ],
        (step, log_decay, in_b, out_c, skip),
        flops=1 << 30,
        spaces=[VMEM] * 4 + [pltpu.SMEM],
    )
    bits = seq_count.bit_length() - 1
    core = swap(tot, 0)
    (chip,) = call(decay_kernel, [((1, half), F32)], (tot, core))

    args = (query, kv, near, far_even, far_odd)
    first, sums = call(
        functools.partial(attention_kernel, False), [((blk, feat), BF16), ((8, blk), F32)], args, flops=1 << 28
    )
    to_a = [(i, i // 2 + (i % 2) * (seq_count // 2)) for i in every]
    to_b = [(i, i // 2 + (1 - i % 2) * (seq_count // 2)) for i in every]
    home_a = lax.ppermute(first, "seq", to_a)
    second, sums = call(
        functools.partial(attention_kernel, True),
        [((blk, feat), BF16), ((16, blk), F32)],
        args + (sums,),
        flops=1 << 28,
    )
    home_b = lax.ppermute(second, "seq", to_b)
    z_bits = head_count.bit_length() - 1
    for bit in range(z_bits):
        other = lax.ppermute(sums, "head", [(i, i ^ (1 << bit)) for i in range(head_count)])
        parts = 2 if bit == z_bits - 1 else 1
        added = call(add_kernel, [((16 // parts, blk), F32)] * parts, (sums, other))
        sums = added[0]
    sums_a = lax.ppermute(added[0], "seq", to_a)
    sums_b = lax.ppermute(added[1], "seq", to_b)
    decays = []
    running = [chip]
    for bit in range(1, bits - 1):
        decays.append(swap(running[-1], bit))
        if bit < bits - 2:
            running += call(times_kernel, [((1, half), F32)], (running[-1], decays[-1]))

    x, keep, send = call(
        home_kernel,
        [((toks, feat), BF16), ((STATE, half), F32), ((STATE, half), BF16)],
        (home_a, home_b, sums_a, sums_b, norm_gain[None, :], b_weighted),
        flops=1 << 28,
    )
    (local,) = call(local_kernel, [((toks, feat), F32)], (x, mix, skip_row), flops=1 << 29)
    got = swap(send, 0)
    state = ((STATE, half), F32)
    row = ((1, half), F32)
    early, total, low = call(chip_kernel, [state, state, ((STATE, half), BF16)], (keep, got, tot, core))
    enter, carried = jnp.zeros(*state), jnp.ones(*row)
    for bit in range(1, bits):
        theirs = swap(low, bit)
        if bit < bits - 1:
            enter, carried, total, low = call(
                functools.partial(stage_kernel, bit),
                [state, row, state, ((STATE, half), BF16)],
                (total, theirs, running[bit - 1], decays[bit - 1], enter, carried),
            )
    own, give = call(
        functools.partial(last_kernel, bits - 1),
        [((STATE, half), BF16)] * 2,
        (theirs, enter, carried, early, tot, core),
    )
    other = swap(give, 0)
    (out,) = call(final_kernel, [((toks, feat), BF16)], (local, scale, out_c, own, other), flops=1 << 28)
    return out


def solution(mesh):
    placed = (
        P(None, "seq", "head"),
        P(None, "seq", "head"),
        P(None, "seq", "head"),
        P("head"),
        P("seq", None),
        P("seq", None),
        P("head", "seq"),
        P("head", "seq"),
        P("head"),
    )
    return jax.shard_map(layer, mesh=mesh, in_specs=placed, out_specs=P("seq", "head"), check_vma=False)
```

time: 94.6 us -> 52.6 us (0.56)
  the two profiles are of different devices: /device:TPU:7 before, /device:TPU:0 now
where the time goes in v1:
time: 52.6 us; the launch traced here: 52.3 us
  starting transfers between devices  23.6 us (45%)
  waiting for transfers between devices  17 us (32%)
  Pallas kernels  8.57 us (16%)
  local copies, waits for them, and re-layouts  2.89 us (5%)
    ppermute x6, waiting for transfers between devices, swap(): return lax.ppermute(block, 'seq', [(i, i ^ 1 << bit) for i in every])  8.93 us
    pallas_call x13, Pallas kernels, call(): pl.pallas_call(kernel, out_shape=[jax.ShapeDtypeStruct(s, d) for s, d in...  8.57 us
    ppermute x1, starting transfers between devices, layer(): sums_b = lax.ppermute(added[1], 'seq', to_b)  5.39 us
    ppermute x1, starting transfers between devices, layer(): lax.ppermute(kv, 'seq', [(i, (i + 2) % seq_count) for i in every if i % 2...  4.4 us
    ppermute x2, starting transfers between devices, layer(): lax.ppermute(sums, 'head', [(i, i ^ 1 << bit) for i in range(head_count)])  4.23 us
    ppermute x6, starting transfers between devices, swap(): return lax.ppermute(block, 'seq', [(i, i ^ 1 << bit) for i in every])  4.14 us
    ppermute x2, waiting for transfers between devices, layer(): lax.ppermute(sums, 'head', [(i, i ^ 1 << bit) for i in range(head_count)])  4.03 us
    unnamed x18, local copies, waits for them, and re-layouts  2.87 us
  transfers between devices with their start and end apart: 15, of which 8 were waited for; matrix products, arithmetic and copies ran while one was open for 0% of the time, Pallas kernels for 5%

profile of v1, /device:TPU:0, one launch (start us, length us, event | category | flops | bytes accessed | tf_op | source)
XLA Modules:
  0.0 52.3 jit_solution(17801048371150346042)
XLA Ops:
  0.0 0.9 %copy-done.1 = bf16[2,128,256]{2,1,0:T(8,128)(2,1)S(1)} copy-done((bf16[2,128,256]{2,1,0:T(8,128)(2,1)S(1)}, bf16[2,128,256]{2,1,0:T(8,128)(2,1)}, u32[]{:S(2)}) %copy-start.1) | copy-done | bytes 131096
  0.9 0.9 %copy-done.2 = bf16[2,128,256]{2,1,0:T(8,128)(2,1)S(1)} copy-done((bf16[2,128,256]{2,1,0:T(8,128)(2,1)S(1)}, bf16[2,128,256]{2,1,0:T(8,128)(2,1)}, u32[]{:S(2)}) %copy-start.2) | copy-done | bytes 131096
  2.4 4.4 %collective-permute-start.1 = (bf16[2,128,512]{2,1,0:T(8,128)(2,1)S(1)}, bf16[2,128,512]{2,1,0:T(8,128)(2,1)S(1)}, u32[]{:S(2)}, u32[]{:S(2)}) collective-permute-start(bf16[2,128,512]{2,1,0:T(8,128)(2,1)S(1)} %shard_map.91.kv_ref), channel_id=1, source_target_pairs={{0,8},{8,16},{16,24},{24,0},{1,9},{9,17},{17,25},{25,1},{2,10},{10... | collective-permute-start | bytes 786440 | tf_op jit(solution)/shard_map/ppermute | solution.py:292
  6.8 2.6 %collective-permute-done.near_ref = bf16[2,128,512]{2,1,0:T(8,128)(2,1)S(1)} collective-permute-done((bf16[2,128,512]{2,1,0:T(8,128)(2,1)S(1)}, bf16[2,128,512]{2,1,0:T(8,128)(2,1)S(1)}, u32[]{:S(2)}, u32[]{:S(2)}) %collective-permute-start) | collective-permute-done | bytes 262176 | tf_op jit(solution)/shard_map/ppermute | solution.py:291
  9.4 1.3 %collective-permute-start.2 = (bf16[2,128,512]{2,1,0:T(8,128)(2,1)S(1)}, bf16[2,128,512]{2,1,0:T(8,128)(2,1)S(1)}, u32[]{:S(2)}, u32[]{:S(2)}) collective-permute-start(bf16[2,128,512]{2,1,0:T(8,128)(2,1)S(1)} %collective-permute-done.near_ref), channel_id=1, source_target_pairs={{0,4},{8,12},{16,20},{24,28},{1,5},{9,13},{17,21},{25,29},{2,6},{1... | collective-permute-start | bytes 786440 | tf_op jit(solution)/shard_map/ppermute | solution.py:293
  10.7 1.5 %collective-permute-done.1.far_even_ref = bf16[2,128,512]{2,1,0:T(8,128)(2,1)S(1)} collective-permute-done((bf16[2,128,512]{2,1,0:T(8,128)(2,1)S(1)}, bf16[2,128,512]{2,1,0:T(8,128)(2,1)S(1)}, u32[]{:S(2)}, u32[]{:S(2)}) %collective-permute-start.1) | collective-permute-done | bytes 262176 | tf_op jit(solution)/shard_map/ppermute | solution.py:292
  12.1 1.0 %copy-done = bf16[2,128,1024]{2,1,0:T(8,128)(2,1)S(1)} copy-done((bf16[2,128,1024]{2,1,0:T(8,128)(2,1)S(1)}, bf16[2,128,1024]{2,1,0:T(8,128)(2,1)}, u32[]{:S(2)}) %copy-start) | copy-done | bytes 524312
  13.2 1.0 %shard_map.92 = (bf16[128,1024]{1,0:T(8,128)(2,1)S(1)}, f32[8,128]{1,0:T(8,128)S(1)}) custom-call(bf16[2,128,1024]{2,1,0:T(8,128)(2,1)S(1)} %copy-done, bf16[2,128,512]{2,1,0:T(8,128)(2,1)S(1)} %shard_map.91.kv_ref, bf16[2,128,512]{2,1,0:T(8,128)(2,1)S(1)} %collective-permute-done.near_ref, bf16[2,128,512]{2,1,0:T(8,128)(2,1)S(1)} %collective-permute-done.1.far_even_ref, ...), custom_call_target="tpu_custom_call" | custom-call | flops 268435456 | bytes 1048576 | tf_op jit(solution)/shard_map/pallas_call | solution.py:35
  14.2 1.0 %shard_map.93 = (bf16[128,1024]{1,0:T(8,128)(2,1)S(1)}, f32[16,128]{1,0:T(8,128)S(1)}) custom-call(bf16[2,128,1024]{2,1,0:T(8,128)(2,1)S(1)} %copy-done, bf16[2,128,512]{2,1,0:T(8,128)(2,1)S(1)} %shard_map.91.kv_ref, bf16[2,128,512]{2,1,0:T(8,128)(2,1)S(1)} %collective-permute-done.near_ref, bf16[2,128,512]{2,1,0:T(8,128)(2,1)S(1)} %collective-permute-done.1.far_even_ref, ...), custom_call_target="tpu_custom_call" | custom-call | flops 268435456 | bytes 1048576 | tf_op jit(solution)/shard_map/pallas_call | solution.py:35
  15.3 2.3 %collective-permute-start.4 = (bf16[128,1024]{1,0:T(8,128)(2,1)S(1)}, bf16[128,1024]{1,0:T(8,128)(2,1)S(1)}, u32[]{:S(2)}, u32[]{:S(2)}) collective-permute-start(bf16[128,1024]{1,0:T(8,128)(2,1)S(1)} %get-tuple-element.29), channel_id=1, source_target_pairs={{0,16},{4,0},{8,20},{12,4},{16,24},{20,8},{24,28},{28,12},{1,17},{... | collective-permute-start | bytes 786440 | tf_op jit(solution)/shard_map/ppermute | solution.py:325
  18.2 1.6 %collective-permute-start.5 = (f32[16,128]{1,0:T(8,128)S(1)}, f32[16,128]{1,0:T(8,128)S(1)}, u32[]{:S(2)}, u32[]{:S(2)}) collective-permute-start(f32[16,128]{1,0:T(8,128)S(1)} %get-tuple-element.30.a_ref), channel_id=1, source_target_pairs={{0,1},{1,0},{2,3},{3,2},{4,5},{5,4},{6,7},{7,6},{8,9},{9,8},{10,11... | collective-permute-start | bytes 24584 | tf_op jit(solution)/shard_map/ppermute | solution.py:328
  19.9 2.1 %collective-permute-done.5.b_ref = f32[16,128]{1,0:T(8,128)S(1)} collective-permute-done((f32[16,128]{1,0:T(8,128)S(1)}, f32[16,128]{1,0:T(8,128)S(1)}, u32[]{:S(2)}, u32[]{:S(2)}) %collective-permute-start.5) | collective-permute-done | bytes 8224 | tf_op jit(solution)/shard_map/ppermute | solution.py:328
  22.0 2.6 %collective-permute-start.6 = (f32[16,128]{1,0:T(8,128)S(1)}, f32[16,128]{1,0:T(8,128)S(1)}, u32[]{:S(2)}, u32[]{:S(2)}) collective-permute-start(f32[16,128]{1,0:T(8,128)S(1)} %shard_map.94.a_ref), channel_id=1, source_target_pairs={{0,2},{1,3},{2,0},{3,1},{4,6},{5,7},{6,4},{7,5},{8,10},{9,11},{10,... | collective-permute-start | bytes 24584 | tf_op jit(solution)/shard_map/ppermute | solution.py:328
  24.6 2.0 %collective-permute-done.6.b_ref = f32[16,128]{1,0:T(8,128)S(1)} collective-permute-done((f32[16,128]{1,0:T(8,128)S(1)}, f32[16,128]{1,0:T(8,128)S(1)}, u32[]{:S(2)}, u32[]{:S(2)}) %collective-permute-start.6) | collective-permute-done | bytes 8224 | tf_op jit(solution)/shard_map/ppermute | solution.py:328
  27.2 5.4 %collective-permute-start.8 = (f32[8,128]{1,0:T(8,128)S(1)}, f32[8,128]{1,0:T(8,128)S(1)}, u32[]{:S(2)}, u32[]{:S(2)}) collective-permute-start(f32[8,128]{1,0:T(8,128)S(1)} %get-tuple-element.32), channel_id=1, source_target_pairs={{0,16},{4,0},{8,20},{12,4},{16,24},{20,8},{24,28},{28,12},{1,17},{... | collective-permute-start | bytes 12296 | tf_op jit(solution)/shard_map/ppermute | solution.py:333
  32.6 2.0 %shard_map.96 = (bf16[8,256,512]{2,1,0:T(8,128)(2,1)S(1)}, bf16[8,128,512]{2,1,0:T(8,128)(2,1)S(1)}, f32[256,1024]{1,0:T(8,128)S(1)}, f32[1,1024]{1,0:T(1,128)S(1)}, f32[1,1024]{1,0:T(1,128)S(1)}) custom-call(f32[16,256]{1,0:T(8,128)S(1)} %copy-done.6, f32[16,256]{1,0:T(8,128)S(1)} %copy-done.7, bf16[256,128]{1,0:T(8,128)(2,1)S(1)} %copy-done.5, ...), custom_call_target="tpu_custom_call" | custom-call | flops 1073741824 | bytes 1048576 | tf_op jit(solution)/shard_map/pallas_call | solution.py:35
  34.7 1.7 %shard_map.97 = (bf16[256,1024]{1,0:T(8,128)(2,1)S(1)}, f32[128,512]{1,0:T(8,128)S(1)}, bf16[128,512]{1,0:T(8,128)(2,1)S(1)}) custom-call(bf16[128,1024]{1,0:T(8,128)(2,1)S(1)} %collective-permute-done.3.xa_ref, bf16[128,1024]{1,0:T(8,128)(2,1)S(1)} %collective-permute-done.4.xb_ref, f32[8,128]{1,0:T(8,128)S(1)} %collective-permute-done.7.ra_ref, ...), custom_call_target="tpu_custom_call" | custom-call | flops 268435456 | bytes 1048576 | tf_op jit(solution)/shard_map/pallas_call | solution.py:35
  37.0 1.1 %collective-permute-done.10.core_ref = f32[1,1024]{1,0:T(1,128)S(1)} collective-permute-done((f32[1,1024]{1,0:T(1,128)S(1)}, f32[1,1024]{1,0:T(1,128)S(1)}, u32[]{:S(2)}, u32[]{:S(2)}) %collective-permute-start.10) | collective-permute-done | bytes 4128 | tf_op jit(solution)/shard_map/ppermute | solution.py:288
  38.2 1.4 %collective-permute-start.11 = (bf16[128,512]{1,0:T(8,128)(2,1)S(1)}, bf16[128,512]{1,0:T(8,128)(2,1)S(1)}, u32[]{:S(2)}, u32[]{:S(2)}) collective-permute-start(bf16[128,512]{1,0:T(8,128)(2,1)S(1)} %get-tuple-element.42), channel_id=1, source_target_pairs={{0,8},{4,12},{8,0},{12,4},{16,24},{20,28},{24,16},{28,20},{1,9},{5... | collective-permute-start | bytes 393224 | tf_op jit(solution)/shard_map/ppermute | solution.py:288
  40.3 3.6 %collective-permute-done.12.decay_ref = f32[1,512]{1,0:T(1,128)S(1)} collective-permute-done((f32[1,512]{1,0:T(1,128)S(1)}, f32[1,512]{1,0:T(1,128)S(1)}, u32[]{:S(2)}, u32[]{:S(2)}) %collective-permute-start.12) | collective-permute-done | bytes 2080 | tf_op jit(solution)/shard_map/ppermute | solution.py:288
  43.9 0.8 %shard_map.101 = (f32[128,512]{1,0:T(8,128)S(1)}, f32[1,512]{1,0:T(1,128)S(1)}, f32[128,512]{1,0:T(8,128)}, bf16[128,512]{1,0:T(8,128)(2,1)S(1)}) custom-call(f32[128,512]{1,0:T(8,128)S(1)} %get-tuple-element.41.total_ref, bf16[128,512]{1,0:T(8,128)(2,1)S(1)} %collective-permute-done.11.theirs_ref, f32[1,512]{1,0:T(1,128)S(1)} %shard_map.100.mine_ref, ...), custom_call_target="tpu_custom_call" | custom-call | flops 1 | bytes 1048576 | tf_op jit(solution)/shard_map/pallas_call | solution.py:35
  44.7 1.4 %collective-permute-start.13 = (bf16[128,512]{1,0:T(8,128)(2,1)S(1)}, bf16[128,512]{1,0:T(8,128)(2,1)S(1)}, u32[]{:S(2)}, u32[]{:S(2)}) collective-permute-start(bf16[128,512]{1,0:T(8,128)(2,1)S(1)} %get-tuple-element.43), channel_id=1, source_target_pairs={{0,16},{4,20},{8,24},{12,28},{16,0},{20,4},{24,8},{28,12},{1,17},{... | collective-permute-start | bytes 393224 | tf_op jit(solution)/shard_map/ppermute | solution.py:288
  46.1 3.6 %collective-permute-done.13.theirs_ref = bf16[128,512]{1,0:T(8,128)(2,1)S(1)} collective-permute-done((bf16[128,512]{1,0:T(8,128)(2,1)S(1)}, bf16[128,512]{1,0:T(8,128)(2,1)S(1)}, u32[]{:S(2)}, u32[]{:S(2)}) %collective-permute-start.13) | collective-permute-done | bytes 131104 | tf_op jit(solution)/shard_map/ppermute | solution.py:288
  51.2 1.1 %shard_map.103 = bf16[256,1024]{1,0:T(8,128)(2,1)} custom-call(f32[256,1024]{1,0:T(8,128)S(1)} %shard_map.98.local_ref, f32[256,1024]{1,0:T(8,128)S(1)} %get-tuple-element.37.scale_ref, bf16[256,128]{1,0:T(8,128)(2,1)S(1)} %copy-done.3, bf16[128,512]{1,0:T(8,128)(2,1)S(1)} %get-tuple-element.47.own_ref, bf16[128,512]{1,0:T(8,128)(2,1)S(1)} %collective-permute-done.14.other_ref), custom_call_target="tpu_custom_call" | custom-call | flops 268435456 | bytes 1048576 | tf_op jit(solution)/shard_map/pallas_call | solution.py:35
  (39 shorter events, 4.8 us)
Async XLA Ops:
  0.0 0.9 %copy-start.1 = (bf16[2,128,256]{2,1,0:T(8,128)(2,1)S(1)}, bf16[2,128,256]{2,1,0:T(8,128)(2,1)}, u32[]{:S(2)}) copy-start(bf16[2,128,256]{2,1,0:T(8,128)(2,1)} %k_ref.1) | copy-start | bytes 393220
  0.9 0.9 %copy-start.2 = (bf16[2,128,256]{2,1,0:T(8,128)(2,1)S(1)}, bf16[2,128,256]{2,1,0:T(8,128)(2,1)}, u32[]{:S(2)}) copy-start(bf16[2,128,256]{2,1,0:T(8,128)(2,1)} %v_ref.1) | copy-start | bytes 393220
  1.8 30.8 %copy-start.3 = (bf16[256,128]{1,0:T(8,128)(2,1)S(1)}, bf16[256,128]{1,0:T(8,128)(2,1)}, u32[]{:S(2)}) copy-start(bf16[256,128]{1,0:T(8,128)(2,1)} %c_ref.3) | copy-start | bytes 196612
  1.8 30.8 %copy-start.5 = (bf16[256,128]{1,0:T(8,128)(2,1)S(1)}, bf16[256,128]{1,0:T(8,128)(2,1)}, u32[]{:S(2)}) copy-start(bf16[256,128]{1,0:T(8,128)(2,1)} %b_ref.1) | copy-start | bytes 196612
  1.8 30.8 %copy-start.6 = (f32[16,256]{1,0:T(8,128)S(1)}, f32[16,256]{1,0:T(8,128)}, u32[]{:S(2)}) copy-start(f32[16,256]{1,0:T(8,128)} %step_ref.1) | copy-start | bytes 49156
  1.8 30.8 %copy-start.7 = (f32[16,256]{1,0:T(8,128)S(1)}, f32[16,256]{1,0:T(8,128)}, u32[]{:S(2)}) copy-start(f32[16,256]{1,0:T(8,128)} %log_ref.1) | copy-start | bytes 49156
  1.8 30.8 %copy-start.8 = (f32[16]{0:T(128)S(1)}, f32[16]{0:T(128)}, u32[]{:S(2)}) copy-start(f32[16]{0:T(128)} %skip_ref.1) | copy-start | bytes 196
  1.9 7.5 %collective-permute-start = (bf16[2,128,512]{2,1,0:T(8,128)(2,1)S(1)}, bf16[2,128,512]{2,1,0:T(8,128)(2,1)S(1)}, u32[]{:S(2)}, u32[]{:S(2)}) collective-permute-start(bf16[2,128,512]{2,1,0:T(8,128)(2,1)S(1)} %shard_map.91.kv_ref), channel_id=1, source_target_pairs={{0,4},{4,8},{8,12},{12,16},{16,20},{20,24},{24,28},{28,0},{1,5},{5... | collective-permute-start | bytes 786440 | tf_op jit(solution)/shard_map/ppermute | solution.py:291
  2.4 9.7 %collective-permute-start.1 = (bf16[2,128,512]{2,1,0:T(8,128)(2,1)S(1)}, bf16[2,128,512]{2,1,0:T(8,128)(2,1)S(1)}, u32[]{:S(2)}, u32[]{:S(2)}) collective-permute-start(bf16[2,128,512]{2,1,0:T(8,128)(2,1)S(1)} %shard_map.91.kv_ref), channel_id=1, source_target_pairs={{0,8},{8,16},{16,24},{24,0},{1,9},{9,17},{17,25},{25,1},{2,10},{10... | collective-permute-start | bytes 786440 | tf_op jit(solution)/shard_map/ppermute | solution.py:292
  9.4 2.8 %collective-permute-start.2 = (bf16[2,128,512]{2,1,0:T(8,128)(2,1)S(1)}, bf16[2,128,512]{2,1,0:T(8,128)(2,1)S(1)}, u32[]{:S(2)}, u32[]{:S(2)}) collective-permute-start(bf16[2,128,512]{2,1,0:T(8,128)(2,1)S(1)} %collective-permute-done.near_ref), channel_id=1, source_target_pairs={{0,4},{8,12},{16,20},{24,28},{1,5},{9,13},{17,21},{25,29},{2,6},{1... | collective-permute-start | bytes 786440 | tf_op jit(solution)/shard_map/ppermute | solution.py:293
  12.1 1.0 %copy-start = (bf16[2,128,1024]{2,1,0:T(8,128)(2,1)S(1)}, bf16[2,128,1024]{2,1,0:T(8,128)(2,1)}, u32[]{:S(2)}) copy-start(bf16[2,128,1024]{2,1,0:T(8,128)(2,1)} %q_ref.3) | copy-start | bytes 1572868
  15.3 19.4 %copy-start.4 = (f32[1024]{0:T(1024)S(1)}, f32[1024]{0:T(1024)}, u32[]{:S(2)}) copy-start(f32[1024]{0:T(1024)} %param.12) | copy-start | bytes 12292
  15.3 19.4 %collective-permute-start.4 = (bf16[128,1024]{1,0:T(8,128)(2,1)S(1)}, bf16[128,1024]{1,0:T(8,128)(2,1)S(1)}, u32[]{:S(2)}, u32[]{:S(2)}) collective-permute-start(bf16[128,1024]{1,0:T(8,128)(2,1)S(1)} %get-tuple-element.29), channel_id=1, source_target_pairs={{0,16},{4,0},{8,20},{12,4},{16,24},{20,8},{24,28},{28,12},{1,17},{... | collective-permute-start | bytes 786440 | tf_op jit(solution)/shard_map/ppermute | solution.py:325
  17.6 17.1 %collective-permute-start.3 = (bf16[128,1024]{1,0:T(8,128)(2,1)S(1)}, bf16[128,1024]{1,0:T(8,128)(2,1)S(1)}, u32[]{:S(2)}, u32[]{:S(2)}) collective-permute-start(bf16[128,1024]{1,0:T(8,128)(2,1)S(1)} %get-tuple-element.27), channel_id=1, source_target_pairs={{0,0},{4,16},{8,4},{12,20},{16,8},{20,24},{24,12},{28,28},{1,1},{5... | collective-permute-start | bytes 786440 | tf_op jit(solution)/shard_map/ppermute | solution.py:318
  18.2 3.7 %collective-permute-start.5 = (f32[16,128]{1,0:T(8,128)S(1)}, f32[16,128]{1,0:T(8,128)S(1)}, u32[]{:S(2)}, u32[]{:S(2)}) collective-permute-start(f32[16,128]{1,0:T(8,128)S(1)} %get-tuple-element.30.a_ref), channel_id=1, source_target_pairs={{0,1},{1,0},{2,3},{3,2},{4,5},{5,4},{6,7},{7,6},{8,9},{9,8},{10,11... | collective-permute-start | bytes 24584 | tf_op jit(solution)/shard_map/ppermute | solution.py:328
  22.0 4.5 %collective-permute-start.6 = (f32[16,128]{1,0:T(8,128)S(1)}, f32[16,128]{1,0:T(8,128)S(1)}, u32[]{:S(2)}, u32[]{:S(2)}) collective-permute-start(f32[16,128]{1,0:T(8,128)S(1)} %shard_map.94.a_ref), channel_id=1, source_target_pairs={{0,2},{1,3},{2,0},{3,1},{4,6},{5,7},{6,4},{7,5},{8,10},{9,11},{10,... | collective-permute-start | bytes 24584 | tf_op jit(solution)/shard_map/ppermute | solution.py:328
  26.5 8.1 %collective-permute-start.7 = (f32[8,128]{1,0:T(8,128)S(1)}, f32[8,128]{1,0:T(8,128)S(1)}, u32[]{:S(2)}, u32[]{:S(2)}) collective-permute-start(f32[8,128]{1,0:T(8,128)S(1)} %get-tuple-element.31), channel_id=1, source_target_pairs={{0,0},{4,16},{8,4},{12,20},{16,8},{20,24},{24,12},{28,28},{1,1},{5... | collective-permute-start | bytes 12296 | tf_op jit(solution)/shard_map/ppermute | solution.py:332
  27.2 7.5 %collective-permute-start.8 = (f32[8,128]{1,0:T(8,128)S(1)}, f32[8,128]{1,0:T(8,128)S(1)}, u32[]{:S(2)}, u32[]{:S(2)}) collective-permute-start(f32[8,128]{1,0:T(8,128)S(1)} %get-tuple-element.32), channel_id=1, source_target_pairs={{0,16},{4,0},{8,20},{12,4},{16,24},{20,8},{24,28},{28,12},{1,17},{... | collective-permute-start | bytes 12296 | tf_op jit(solution)/shard_map/ppermute | solution.py:333
  36.4 1.7 %collective-permute-start.9 = (bf16[128,512]{1,0:T(8,128)(2,1)S(1)}, bf16[128,512]{1,0:T(8,128)(2,1)S(1)}, u32[]{:S(2)}, u32[]{:S(2)}) collective-permute-start(bf16[128,512]{1,0:T(8,128)(2,1)S(1)} %get-tuple-element.39), channel_id=1, source_target_pairs={{0,4},{4,0},{8,12},{12,8},{16,20},{20,16},{24,28},{28,24},{1,5},{5... | collective-permute-start | bytes 393224 | tf_op jit(solution)/shard_map/ppermute | solution.py:288
  36.9 1.2 %collective-permute-start.10 = (f32[1,1024]{1,0:T(1,128)S(1)}, f32[1,1024]{1,0:T(1,128)S(1)}, u32[]{:S(2)}, u32[]{:S(2)}) collective-permute-start(f32[1,1024]{1,0:T(1,128)S(1)} %get-tuple-element.40.tot_ref), channel_id=1, source_target_pairs={{0,4},{4,0},{8,12},{12,8},{16,20},{20,16},{24,28},{28,24},{1,5},{5... | collective-permute-start | bytes 12296 | tf_op jit(solution)/shard_map/ppermute | solution.py:288
  38.2 5.7 %collective-permute-start.11 = (bf16[128,512]{1,0:T(8,128)(2,1)S(1)}, bf16[128,512]{1,0:T(8,128)(2,1)S(1)}, u32[]{:S(2)}, u32[]{:S(2)}) collective-permute-start(bf16[128,512]{1,0:T(8,128)(2,1)S(1)} %get-tuple-element.42), channel_id=1, source_target_pairs={{0,8},{4,12},{8,0},{12,4},{16,24},{20,28},{24,16},{28,20},{1,9},{5... | collective-permute-start | bytes 393224 | tf_op jit(solution)/shard_map/ppermute | solution.py:288
  39.6 4.2 %collective-permute-start.12 = (f32[1,512]{1,0:T(1,128)S(1)}, f32[1,512]{1,0:T(1,128)S(1)}, u32[]{:S(2)}, u32[]{:S(2)}) collective-permute-start(f32[1,512]{1,0:T(1,128)S(1)} %shard_map.100.mine_ref), channel_id=1, source_target_pairs={{0,8},{4,12},{8,0},{12,4},{16,24},{20,28},{24,16},{28,20},{1,9},{5... | collective-permute-start | bytes 6152 | tf_op jit(solution)/shard_map/ppermute | solution.py:288
  44.7 5.0 %collective-permute-start.13 = (bf16[128,512]{1,0:T(8,128)(2,1)S(1)}, bf16[128,512]{1,0:T(8,128)(2,1)S(1)}, u32[]{:S(2)}, u32[]{:S(2)}) collective-permute-start(bf16[128,512]{1,0:T(8,128)(2,1)S(1)} %get-tuple-element.43), channel_id=1, source_target_pairs={{0,16},{4,20},{8,24},{12,28},{16,0},{20,4},{24,8},{28,12},{1,17},{... | collective-permute-start | bytes 393224 | tf_op jit(solution)/shard_map/ppermute | solution.py:288
  49.8 1.4 %collective-permute-start.14 = (bf16[128,512]{1,0:T(8,128)(2,1)S(1)}, bf16[128,512]{1,0:T(8,128)(2,1)S(1)}, u32[]{:S(2)}, u32[]{:S(2)}) collective-permute-start(bf16[128,512]{1,0:T(8,128)(2,1)S(1)} %get-tuple-element.48), channel_id=1, source_target_pairs={{0,4},{4,0},{8,12},{12,8},{16,20},{20,16},{24,28},{28,24},{1,5},{5... | collective-permute-start | bytes 393224 | tf_op jit(solution)/shard_map/ppermute | solution.py:288

commit v2 on v1

--- a/solution.py
+++ b/solution.py
@@ -39,7 +39,7 @@
         out_specs=[pl.BlockSpec(memory_space=VMEM)] * len(outs),
         compiler_params=pltpu.CompilerParams(vmem_limit_bytes=GRANT),
         cost_estimate=pl.CostEstimate(flops=flops, bytes_accessed=1 << 20, transcendentals=0),
-    )(*args)
+    )(*[pltpu.with_memory_space_constraint(a, m) if m == pltpu.HBM else a for a, m in zip(args, spaces)])
 
 
 def pack_kernel(k_ref, v_ref, out_ref):
@@ -58,7 +58,27 @@
     pl.run_scoped(inner, pltpu.SemaphoreType.DMA((2,)))
 
 
-def prepare_kernel(step_ref, log_ref, b_ref, c_ref, skip_ref, mix_ref, bw_ref, scale_ref, tot_ref, pass_ref):
+def prepare_kernel(*refs):
+    def inner(sems, *inside):
+        copies = [
+            pltpu.make_async_copy(src, dst, sems.at[i])
+            for i, (src, dst) in enumerate(zip(refs[:5], inside))
+        ]
+        for copy in copies:
+            copy.start()
+        for copy in copies:
+            copy.wait()
+        prepare(*inside, *refs[5:])
+
+    pl.run_scoped(
+        inner,
+        pltpu.SemaphoreType.DMA((5,)),
+        *[VMEM(r.shape, r.dtype) for r in refs[:4]],
+        pltpu.SMEM(refs[4].shape, refs[4].dtype),
+    )
+
+
+def prepare(step_ref, log_ref, b_ref, c_ref, skip_ref, mix_ref, bw_ref, scale_ref, tot_ref, pass_ref):
     heads, toks = step_ref.shape
     half = toks // 2
     highest = lax.Precision.HIGHEST
@@ -247,26 +267,38 @@
     low_ref[...] = total.astype(BF16)
 
 
-def stage_kernel(bit, total_ref, theirs_ref, mine_ref, decay_ref, enter_in_ref, carried_in_ref, *outs):
+def arrive(bit, theirs_ref, decay_ref, entered):
     upper = (lax.axis_index("seq") >> bit) % 2 == 1
     theirs = theirs_ref[...].astype(F32)
-    enter_ref, carried_ref, next_ref, low_ref = outs
-    carried = carried_in_ref[...]
-    enter_ref[...] = enter_in_ref[...] + jnp.where(upper, carried * theirs, 0.0)
-    carried_ref[...] = jnp.where(upper, carried * decay_ref[...], carried)
+    enter, carried = (None, None) if entered is None else (entered[0][...], entered[1][...])
+    step = theirs if carried is None else carried * theirs
+    step = jnp.where(upper, step, 0.0)
+    enter = step if enter is None else enter + step
+    if decay_ref is None:
+        return upper, theirs, enter, None
+    ahead = decay_ref[...] if carried is None else carried * decay_ref[...]
+    stay = jnp.ones_like(ahead) if carried is None else carried
+    return upper, theirs, enter, jnp.where(upper, ahead, stay)
+
+
+def stage_kernel(bit, first, total_ref, theirs_ref, mine_ref, decay_ref, *refs):
+    entered, outs = (None, refs) if first else (refs[:2], refs[2:])
+    enter_ref, carried_ref, low_ref = outs[:3]
+    upper, theirs, enter, carried = arrive(bit, theirs_ref, decay_ref, entered)
+    enter_ref[...] = enter
+    carried_ref[...] = carried
     total = total_ref[...]
     total = jnp.where(upper, mine_ref[...] * theirs + total, decay_ref[...] * total + theirs)
-    next_ref[...] = total
     low_ref[...] = total.astype(BF16)
-
-
-def last_kernel(bit, theirs_ref, enter_in_ref, carried_ref, early_ref, tot_ref, core_ref, own_ref, give_ref):
-    me = lax.axis_index("seq")
-    mine = me % 2
+    if len(outs) == 4:
+        outs[3][...] = total
+
+
+def last_kernel(bit, theirs_ref, early_ref, tot_ref, core_ref, *refs):
+    own_ref, give_ref = refs[-2:]
+    mine = lax.axis_index("seq") % 2
     late = mine == 1
-    upper = (me >> bit) % 2 == 1
-    enter = enter_in_ref[...]
-    enter = enter + jnp.where(upper, carried_ref[...] * theirs_ref[...].astype(F32), 0.0)
+    enter = arrive(bit, theirs_ref, None, refs[:-2] or None)[2]
     first = jnp.where(late, half_of(core_ref, mine), half_of(tot_ref, mine))
     after = first * enter + early_ref[...]
     own_ref[...] = jnp.where(late, after, enter).astype(BF16)
@@ -282,12 +314,13 @@
     pairs = heads // 2
     half = feat // 2
     every = range(seq_count)
-    any_space = pltpu.HBM
 
     def swap(block, bit):
         return lax.ppermute(block, "seq", [(i, i ^ (1 << bit)) for i in every])
 
-    (kv,) = call(pack_kernel, [((2, blk, 2 * kv_width), BF16)], (keys, values), spaces=[any_space] * 2)
+    (kv,) = call(
+        pack_kernel, [((2, blk, 2 * kv_width), BF16)], (keys, values), spaces=[pltpu.HBM] * 2
+    )
     near = lax.ppermute(kv, "seq", [(i, (i + 1) % seq_count) for i in every])
     far_even = lax.ppermute(kv, "seq", [(i, (i + 2) % seq_count) for i in every if i % 2 == 0])
     far_odd = lax.ppermute(near, "seq", [(i, i + 1) for i in every if i % 2 == 0])
@@ -303,7 +336,7 @@
         ],
         (step, log_decay, in_b, out_c, skip),
         flops=1 << 30,
-        spaces=[VMEM] * 4 + [pltpu.SMEM],
+        spaces=[pltpu.HBM] * 5,
     )
     bits = seq_count.bit_length() - 1
     core = swap(tot, 0)
@@ -311,7 +344,10 @@
 
     args = (query, kv, near, far_even, far_odd)
     first, sums = call(
-        functools.partial(attention_kernel, False), [((blk, feat), BF16), ((8, blk), F32)], args, flops=1 << 28
+        functools.partial(attention_kernel, False),
+        [((blk, feat), BF16), ((8, blk), F32)],
+        args,
+        flops=1 << 28,
     )
     to_a = [(i, i // 2 + (i % 2) * (seq_count // 2)) for i in every]
     to_b = [(i, i // 2 + (1 - i % 2) * (seq_count // 2)) for i in every]
@@ -348,23 +384,28 @@
     got = swap(send, 0)
     state = ((STATE, half), F32)
     row = ((1, half), F32)
-    early, total, low = call(chip_kernel, [state, state, ((STATE, half), BF16)], (keep, got, tot, core))
-    enter, carried = jnp.zeros(*state), jnp.ones(*row)
+    early, total, low = call(
+        chip_kernel, [state, state, ((STATE, half), BF16)], (keep, got, tot, core)
+    )
+    entered = ()
     for bit in range(1, bits):
         theirs = swap(low, bit)
         if bit < bits - 1:
-            enter, carried, total, low = call(
-                functools.partial(stage_kernel, bit),
-                [state, row, state, ((STATE, half), BF16)],
-                (total, theirs, running[bit - 1], decays[bit - 1], enter, carried),
+            outs = call(
+                functools.partial(stage_kernel, bit, bit == 1),
+                [state, row, ((STATE, half), BF16)] + [state] * (bit < bits - 2),
+                (total, theirs, running[bit - 1], decays[bit - 1], *entered),
             )
+            entered, low, total = outs[:2], outs[2], outs[-1]
     own, give = call(
         functools.partial(last_kernel, bits - 1),
         [((STATE, half), BF16)] * 2,
-        (theirs, enter, carried, early, tot, core),
+        (theirs, early, tot, core, *entered),
     )
     other = swap(give, 0)
-    (out,) = call(final_kernel, [((toks, feat), BF16)], (local, scale, out_c, own, other), flops=1 << 28)
+    (out,) = call(
+        final_kernel, [((toks, feat), BF16)], (local, scale, out_c, own, other), flops=1 << 28
+    )
     return out
 
 
@@ -380,4 +421,6 @@
         P("head", "seq"),
         P("head"),
     )
-    return jax.shard_map(layer, mesh=mesh, in_specs=placed, out_specs=P("seq", "head"), check_vma=False)
+    return jax.shard_map(
+        layer, mesh=mesh, in_specs=placed, out_specs=P("seq", "head"), check_vma=False
+    )

time: 52.6 us -> 51.2 us (0.973)
  local copies, waits for them, and re-layouts: 2.89 us -> 1.05 us
  Pallas kernels: 8.57 us -> 9.25 us
    unnamed x18 -> x6, local copies, waits for them, and re-layouts: 2.87 us -> 1.05 us
    pallas_call x13, Pallas kernels: 8.57 us -> 9.25 us  [call(): pl.pallas_call(kernel, out_shape=[jax.ShapeDtypeStruct(s, d) for s, d in...]
  transfers between devices with their start and end apart: 15 -> 15, of which waited for: 8 -> 8; matrix products, arithmetic and copies ran while one was open for 0% -> 0% of each run, Pallas kernels for 5% -> 6%
where the time goes in v2:
time: 51.2 us; the launch traced here: 50.9 us
  starting transfers between devices  23.4 us (46%)
  waiting for transfers between devices  17.1 us (33%)
  Pallas kernels  9.25 us (18%)
  local copies, waits for them, and re-layouts  1.05 us (2%)
    pallas_call x13, Pallas kernels, call(): pl.pallas_call(kernel, out_shape=[jax.ShapeDtypeStruct(s, d) for s, d in...  9.25 us
    ppermute x6, waiting for transfers between devices, swap(): return lax.ppermute(block, 'seq', [(i, i ^ 1 << bit) for i in every])  9 us
    ppermute x1, starting transfers between devices, layer(): sums_b = lax.ppermute(added[1], 'seq', to_b)  5.41 us
    ppermute x1, starting transfers between devices, layer(): lax.ppermute(kv, 'seq', [(i, (i + 2) % seq_count) for i in every if i % 2...  4.37 us
    ppermute x2, starting transfers between devices, layer(): lax.ppermute(sums, 'head', [(i, i ^ 1 << bit) for i in range(head_count)])  4.23 us
    ppermute x2, waiting for transfers between devices, layer(): lax.ppermute(sums, 'head', [(i, i ^ 1 << bit) for i in range(head_count)])  4.03 us
    ppermute x6, starting transfers between devices, swap(): return lax.ppermute(block, 'seq', [(i, i ^ 1 << bit) for i in every])  3.97 us
    ppermute x1, waiting for transfers between devices, layer(): near = lax.ppermute(kv, 'seq', [(i, (i + 1) % seq_count) for i in every])  2.6 us
  transfers between devices with their start and end apart: 15, of which 8 were waited for; matrix products, arithmetic and copies ran while one was open for 0% of the time, Pallas kernels for 6%

profile of v2, /device:TPU:0, one launch (start us, length us, event | category | flops | bytes accessed | tf_op | source)
XLA Modules:
  0.0 50.9 jit_solution(4949808337080909964)
XLA Ops:
  0.0 1.0 %shard_map.91.kv_ref = bf16[2,128,512]{2,1,0:T(8,128)(2,1)S(1)} custom-call(bf16[2,128,256]{2,1,0:T(8,128)(2,1)} %k_ref.1, bf16[2,128,256]{2,1,0:T(8,128)(2,1)} %v_ref.1), custom_call_target="tpu_custom_call" | custom-call | flops 1 | bytes 1048576 | tf_op jit(solution)/shard_map/pallas_call | solution.py:35
  1.5 4.4 %collective-permute-start.1 = (bf16[2,128,512]{2,1,0:T(8,128)(2,1)S(1)}, bf16[2,128,512]{2,1,0:T(8,128)(2,1)S(1)}, u32[]{:S(2)}, u32[]{:S(2)}) collective-permute-start(bf16[2,128,512]{2,1,0:T(8,128)(2,1)S(1)} %shard_map.91.kv_ref), channel_id=1, source_target_pairs={{0,8},{8,16},{16,24},{24,0},{1,9},{9,17},{17,25},{25,1},{2,10},{10... | collective-permute-start | bytes 786440 | tf_op jit(solution)/shard_map/ppermute | solution.py:325
  5.8 2.6 %collective-permute-done.near_ref = bf16[2,128,512]{2,1,0:T(8,128)(2,1)S(1)} collective-permute-done((bf16[2,128,512]{2,1,0:T(8,128)(2,1)S(1)}, bf16[2,128,512]{2,1,0:T(8,128)(2,1)S(1)}, u32[]{:S(2)}, u32[]{:S(2)}) %collective-permute-start) | collective-permute-done | bytes 262176 | tf_op jit(solution)/shard_map/ppermute | solution.py:324
  8.4 1.3 %collective-permute-start.2 = (bf16[2,128,512]{2,1,0:T(8,128)(2,1)S(1)}, bf16[2,128,512]{2,1,0:T(8,128)(2,1)S(1)}, u32[]{:S(2)}, u32[]{:S(2)}) collective-permute-start(bf16[2,128,512]{2,1,0:T(8,128)(2,1)S(1)} %collective-permute-done.near_ref), channel_id=1, source_target_pairs={{0,4},{8,12},{16,20},{24,28},{1,5},{9,13},{17,21},{25,29},{2,6},{1... | collective-permute-start | bytes 786440 | tf_op jit(solution)/shard_map/ppermute | solution.py:326
  9.7 1.5 %collective-permute-done.1.far_even_ref = bf16[2,128,512]{2,1,0:T(8,128)(2,1)S(1)} collective-permute-done((bf16[2,128,512]{2,1,0:T(8,128)(2,1)S(1)}, bf16[2,128,512]{2,1,0:T(8,128)(2,1)S(1)}, u32[]{:S(2)}, u32[]{:S(2)}) %collective-permute-start.1) | collective-permute-done | bytes 262176 | tf_op jit(solution)/shard_map/ppermute | solution.py:325
  11.2 1.0 %copy-done = bf16[2,128,1024]{2,1,0:T(8,128)(2,1)S(1)} copy-done((bf16[2,128,1024]{2,1,0:T(8,128)(2,1)S(1)}, bf16[2,128,1024]{2,1,0:T(8,128)(2,1)}, u32[]{:S(2)}) %copy-start) | copy-done | bytes 524312
  12.2 1.0 %shard_map.92 = (bf16[128,1024]{1,0:T(8,128)(2,1)S(1)}, f32[8,128]{1,0:T(8,128)S(1)}) custom-call(bf16[2,128,1024]{2,1,0:T(8,128)(2,1)S(1)} %copy-done, bf16[2,128,512]{2,1,0:T(8,128)(2,1)S(1)} %shard_map.91.kv_ref, bf16[2,128,512]{2,1,0:T(8,128)(2,1)S(1)} %collective-permute-done.near_ref, bf16[2,128,512]{2,1,0:T(8,128)(2,1)S(1)} %collective-permute-done.1.far_even_ref, ...), custom_call_target="tpu_custom_call" | custom-call | flops 268435456 | bytes 1048576 | tf_op jit(solution)/shard_map/pallas_call | solution.py:35
  13.3 1.0 %shard_map.93 = (bf16[128,1024]{1,0:T(8,128)(2,1)S(1)}, f32[16,128]{1,0:T(8,128)S(1)}) custom-call(bf16[2,128,1024]{2,1,0:T(8,128)(2,1)S(1)} %copy-done, bf16[2,128,512]{2,1,0:T(8,128)(2,1)S(1)} %shard_map.91.kv_ref, bf16[2,128,512]{2,1,0:T(8,128)(2,1)S(1)} %collective-permute-done.near_ref, bf16[2,128,512]{2,1,0:T(8,128)(2,1)S(1)} %collective-permute-done.1.far_even_ref, ...), custom_call_target="tpu_custom_call" | custom-call | flops 268435456 | bytes 1048576 | tf_op jit(solution)/shard_map/pallas_call | solution.py:35
  14.3 2.3 %collective-permute-start.4 = (bf16[128,1024]{1,0:T(8,128)(2,1)S(1)}, bf16[128,1024]{1,0:T(8,128)(2,1)S(1)}, u32[]{:S(2)}, u32[]{:S(2)}) collective-permute-start(bf16[128,1024]{1,0:T(8,128)(2,1)S(1)} %get-tuple-element.29), channel_id=1, source_target_pairs={{0,16},{4,0},{8,20},{12,4},{16,24},{20,8},{24,28},{28,12},{1,17},{... | collective-permute-start | bytes 786440 | tf_op jit(solution)/shard_map/ppermute | solution.py:361
  16.6 0.7 %collective-permute-start.3 = (bf16[128,1024]{1,0:T(8,128)(2,1)S(1)}, bf16[128,1024]{1,0:T(8,128)(2,1)S(1)}, u32[]{:S(2)}, u32[]{:S(2)}) collective-permute-start(bf16[128,1024]{1,0:T(8,128)(2,1)S(1)} %get-tuple-element.27), channel_id=1, source_target_pairs={{0,0},{4,16},{8,4},{12,20},{16,8},{20,24},{24,12},{28,28},{1,1},{5... | collective-permute-start | bytes 786440 | tf_op jit(solution)/shard_map/ppermute | solution.py:354
  17.3 1.6 %collective-permute-start.5 = (f32[16,128]{1,0:T(8,128)S(1)}, f32[16,128]{1,0:T(8,128)S(1)}, u32[]{:S(2)}, u32[]{:S(2)}) collective-permute-start(f32[16,128]{1,0:T(8,128)S(1)} %get-tuple-element.30.a_ref), channel_id=1, source_target_pairs={{0,1},{1,0},{2,3},{3,2},{4,5},{5,4},{6,7},{7,6},{8,9},{9,8},{10,11... | collective-permute-start | bytes 24584 | tf_op jit(solution)/shard_map/ppermute | solution.py:364
  18.9 2.1 %collective-permute-done.5.b_ref = f32[16,128]{1,0:T(8,128)S(1)} collective-permute-done((f32[16,128]{1,0:T(8,128)S(1)}, f32[16,128]{1,0:T(8,128)S(1)}, u32[]{:S(2)}, u32[]{:S(2)}) %collective-permute-start.5) | collective-permute-done | bytes 8224 | tf_op jit(solution)/shard_map/ppermute | solution.py:364
  21.0 2.6 %collective-permute-start.6 = (f32[16,128]{1,0:T(8,128)S(1)}, f32[16,128]{1,0:T(8,128)S(1)}, u32[]{:S(2)}, u32[]{:S(2)}) collective-permute-start(f32[16,128]{1,0:T(8,128)S(1)} %shard_map.94.a_ref), channel_id=1, source_target_pairs={{0,2},{1,3},{2,0},{3,1},{4,6},{5,7},{6,4},{7,5},{8,10},{9,11},{10,... | collective-permute-start | bytes 24584 | tf_op jit(solution)/shard_map/ppermute | solution.py:364
  23.6 2.0 %collective-permute-done.6.b_ref = f32[16,128]{1,0:T(8,128)S(1)} collective-permute-done((f32[16,128]{1,0:T(8,128)S(1)}, f32[16,128]{1,0:T(8,128)S(1)}, u32[]{:S(2)}, u32[]{:S(2)}) %collective-permute-start.6) | collective-permute-done | bytes 8224 | tf_op jit(solution)/shard_map/ppermute | solution.py:364
  26.2 5.4 %collective-permute-start.8 = (f32[8,128]{1,0:T(8,128)S(1)}, f32[8,128]{1,0:T(8,128)S(1)}, u32[]{:S(2)}, u32[]{:S(2)}) collective-permute-start(f32[8,128]{1,0:T(8,128)S(1)} %get-tuple-element.32), channel_id=1, source_target_pairs={{0,16},{4,0},{8,20},{12,4},{16,24},{20,8},{24,28},{28,12},{1,17},{... | collective-permute-start | bytes 12296 | tf_op jit(solution)/shard_map/ppermute | solution.py:369
  31.6 2.4 %shard_map.96 = (bf16[8,256,512]{2,1,0:T(8,128)(2,1)S(1)}, bf16[8,128,512]{2,1,0:T(8,128)(2,1)S(1)}, f32[256,1024]{1,0:T(8,128)S(1)}, f32[1,1024]{1,0:T(1,128)S(1)}, f32[1,1024]{1,0:T(1,128)S(1)}) custom-call(f32[16,256]{1,0:T(8,128)} %refs_0_.1, f32[16,256]{1,0:T(8,128)} %refs_1_.1, bf16[256,128]{1,0:T(8,128)(2,1)} %refs_2_.1, bf16[256,128]{1,0:T(8,128)(2,1)} %c_ref.1, ...), custom_call_target="tpu_custom_call" | custom-call | flops 1073741824 | bytes 1048576 | tf_op jit(solution)/shard_map/pallas_call | solution.py:35
  34.1 1.7 %shard_map.97 = (bf16[256,1024]{1,0:T(8,128)(2,1)S(1)}, f32[128,512]{1,0:T(8,128)S(1)}, bf16[128,512]{1,0:T(8,128)(2,1)S(1)}) custom-call(bf16[128,1024]{1,0:T(8,128)(2,1)S(1)} %collective-permute-done.3.xa_ref, bf16[128,1024]{1,0:T(8,128)(2,1)S(1)} %collective-permute-done.4.xb_ref, f32[8,128]{1,0:T(8,128)S(1)} %collective-permute-done.7.ra_ref, ...), custom_call_target="tpu_custom_call" | custom-call | flops 268435456 | bytes 1048576 | tf_op jit(solution)/shard_map/pallas_call | solution.py:35
  36.4 0.8 %collective-permute-done.10.core_ref = f32[1,1024]{1,0:T(1,128)S(1)} collective-permute-done((f32[1,1024]{1,0:T(1,128)S(1)}, f32[1,1024]{1,0:T(1,128)S(1)}, u32[]{:S(2)}, u32[]{:S(2)}) %collective-permute-start.10) | collective-permute-done | bytes 4128 | tf_op jit(solution)/shard_map/ppermute | solution.py:319
  37.3 1.7 %collective-permute-start.11 = (bf16[128,512]{1,0:T(8,128)(2,1)S(1)}, bf16[128,512]{1,0:T(8,128)(2,1)S(1)}, u32[]{:S(2)}, u32[]{:S(2)}) collective-permute-start(bf16[128,512]{1,0:T(8,128)(2,1)S(1)} %get-tuple-element.42), channel_id=1, source_target_pairs={{0,8},{4,12},{8,0},{12,4},{16,24},{20,28},{24,16},{28,20},{1,9},{5... | collective-permute-start | bytes 393224 | tf_op jit(solution)/shard_map/ppermute | solution.py:319
  39.4 3.7 %collective-permute-done.12.decay_ref = f32[1,512]{1,0:T(1,128)S(1)} collective-permute-done((f32[1,512]{1,0:T(1,128)S(1)}, f32[1,512]{1,0:T(1,128)S(1)}, u32[]{:S(2)}, u32[]{:S(2)}) %collective-permute-start.12) | collective-permute-done | bytes 2080 | tf_op jit(solution)/shard_map/ppermute | solution.py:319
  43.3 1.2 %collective-permute-start.13 = (bf16[128,512]{1,0:T(8,128)(2,1)S(1)}, bf16[128,512]{1,0:T(8,128)(2,1)S(1)}, u32[]{:S(2)}, u32[]{:S(2)}) collective-permute-start(bf16[128,512]{1,0:T(8,128)(2,1)S(1)} %get-tuple-element.43), channel_id=1, source_target_pairs={{0,16},{4,20},{8,24},{12,28},{16,0},{20,4},{24,8},{28,12},{1,17},{... | collective-permute-start | bytes 393224 | tf_op jit(solution)/shard_map/ppermute | solution.py:319
  44.5 3.8 %collective-permute-done.13.theirs_ref = bf16[128,512]{1,0:T(8,128)(2,1)S(1)} collective-permute-done((bf16[128,512]{1,0:T(8,128)(2,1)S(1)}, bf16[128,512]{1,0:T(8,128)(2,1)S(1)}, u32[]{:S(2)}, u32[]{:S(2)}) %collective-permute-start.13) | collective-permute-done | bytes 131104 | tf_op jit(solution)/shard_map/ppermute | solution.py:319
  48.5 0.7 %shard_map.98.local_ref = f32[256,1024]{1,0:T(8,128)S(1)} custom-call(bf16[256,1024]{1,0:T(8,128)(2,1)S(1)} %get-tuple-element.34.x_ref, bf16[8,256,512]{2,1,0:T(8,128)(2,1)S(1)} %get-tuple-element.35.mix_ref, f32[1,1024]{1,0:T(1,128)S(1)} %get-tuple-element.36.skip_ref), custom_call_target="tpu_custom_call" | custom-call | flops 536870912 | bytes 1048576 | tf_op jit(solution)/shard_map/pallas_call | solution.py:35
  49.8 1.1 %shard_map.103 = bf16[256,1024]{1,0:T(8,128)(2,1)} custom-call(f32[256,1024]{1,0:T(8,128)S(1)} %shard_map.98.local_ref, f32[256,1024]{1,0:T(8,128)S(1)} %get-tuple-element.37.scale_ref, bf16[256,128]{1,0:T(8,128)(2,1)S(1)} %copy-done.1, bf16[128,512]{1,0:T(8,128)(2,1)S(1)} %get-tuple-element.47.own_ref, bf16[128,512]{1,0:T(8,128)(2,1)S(1)} %collective-permute-done.14.other_ref), custom_call_target="tpu_custom_call" | custom-call | flops 268435456 | bytes 1048576 | tf_op jit(solution)/shard_map/pallas_call | solution.py:35
  (25 shorter events, 3.1 us)
Async XLA Ops:
  1.0 7.5 %collective-permute-start = (bf16[2,128,512]{2,1,0:T(8,128)(2,1)S(1)}, bf16[2,128,512]{2,1,0:T(8,128)(2,1)S(1)}, u32[]{:S(2)}, u32[]{:S(2)}) collective-permute-start(bf16[2,128,512]{2,1,0:T(8,128)(2,1)S(1)} %shard_map.91.kv_ref), channel_id=1, source_target_pairs={{0,4},{4,8},{8,12},{12,16},{16,20},{20,24},{24,28},{28,0},{1,5},{5... | collective-permute-start | bytes 786440 | tf_op jit(solution)/shard_map/ppermute | solution.py:324
  1.5 9.7 %collective-permute-start.1 = (bf16[2,128,512]{2,1,0:T(8,128)(2,1)S(1)}, bf16[2,128,512]{2,1,0:T(8,128)(2,1)S(1)}, u32[]{:S(2)}, u32[]{:S(2)}) collective-permute-start(bf16[2,128,512]{2,1,0:T(8,128)(2,1)S(1)} %shard_map.91.kv_ref), channel_id=1, source_target_pairs={{0,8},{8,16},{16,24},{24,0},{1,9},{9,17},{17,25},{25,1},{2,10},{10... | collective-permute-start | bytes 786440 | tf_op jit(solution)/shard_map/ppermute | solution.py:325
  8.4 2.8 %collective-permute-start.2 = (bf16[2,128,512]{2,1,0:T(8,128)(2,1)S(1)}, bf16[2,128,512]{2,1,0:T(8,128)(2,1)S(1)}, u32[]{:S(2)}, u32[]{:S(2)}) collective-permute-start(bf16[2,128,512]{2,1,0:T(8,128)(2,1)S(1)} %collective-permute-done.near_ref), channel_id=1, source_target_pairs={{0,4},{8,12},{16,20},{24,28},{1,5},{9,13},{17,21},{25,29},{2,6},{1... | collective-permute-start | bytes 786440 | tf_op jit(solution)/shard_map/ppermute | solution.py:326
  11.2 1.0 %copy-start = (bf16[2,128,1024]{2,1,0:T(8,128)(2,1)S(1)}, bf16[2,128,1024]{2,1,0:T(8,128)(2,1)}, u32[]{:S(2)}) copy-start(bf16[2,128,1024]{2,1,0:T(8,128)(2,1)} %q_ref.3) | copy-start | bytes 1572868
  14.3 19.8 %copy-start.2 = (f32[1024]{0:T(1024)S(1)}, f32[1024]{0:T(1024)}, u32[]{:S(2)}) copy-start(f32[1024]{0:T(1024)} %param.12) | copy-start | bytes 12292
  14.3 19.8 %collective-permute-start.4 = (bf16[128,1024]{1,0:T(8,128)(2,1)S(1)}, bf16[128,1024]{1,0:T(8,128)(2,1)S(1)}, u32[]{:S(2)}, u32[]{:S(2)}) collective-permute-start(bf16[128,1024]{1,0:T(8,128)(2,1)S(1)} %get-tuple-element.29), channel_id=1, source_target_pairs={{0,16},{4,0},{8,20},{12,4},{16,24},{20,8},{24,28},{28,12},{1,17},{... | collective-permute-start | bytes 786440 | tf_op jit(solution)/shard_map/ppermute | solution.py:361
  16.6 17.5 %collective-permute-start.3 = (bf16[128,1024]{1,0:T(8,128)(2,1)S(1)}, bf16[128,1024]{1,0:T(8,128)(2,1)S(1)}, u32[]{:S(2)}, u32[]{:S(2)}) collective-permute-start(bf16[128,1024]{1,0:T(8,128)(2,1)S(1)} %get-tuple-element.27), channel_id=1, source_target_pairs={{0,0},{4,16},{8,4},{12,20},{16,8},{20,24},{24,12},{28,28},{1,1},{5... | collective-permute-start | bytes 786440 | tf_op jit(solution)/shard_map/ppermute | solution.py:354
  17.3 3.7 %collective-permute-start.5 = (f32[16,128]{1,0:T(8,128)S(1)}, f32[16,128]{1,0:T(8,128)S(1)}, u32[]{:S(2)}, u32[]{:S(2)}) collective-permute-start(f32[16,128]{1,0:T(8,128)S(1)} %get-tuple-element.30.a_ref), channel_id=1, source_target_pairs={{0,1},{1,0},{2,3},{3,2},{4,5},{5,4},{6,7},{7,6},{8,9},{9,8},{10,11... | collective-permute-start | bytes 24584 | tf_op jit(solution)/shard_map/ppermute | solution.py:364
  21.0 4.5 %collective-permute-start.6 = (f32[16,128]{1,0:T(8,128)S(1)}, f32[16,128]{1,0:T(8,128)S(1)}, u32[]{:S(2)}, u32[]{:S(2)}) collective-permute-start(f32[16,128]{1,0:T(8,128)S(1)} %shard_map.94.a_ref), channel_id=1, source_target_pairs={{0,2},{1,3},{2,0},{3,1},{4,6},{5,7},{6,4},{7,5},{8,10},{9,11},{10,... | collective-permute-start | bytes 24584 | tf_op jit(solution)/shard_map/ppermute | solution.py:364
  25.6 8.5 %collective-permute-start.7 = (f32[8,128]{1,0:T(8,128)S(1)}, f32[8,128]{1,0:T(8,128)S(1)}, u32[]{:S(2)}, u32[]{:S(2)}) collective-permute-start(f32[8,128]{1,0:T(8,128)S(1)} %get-tuple-element.31), channel_id=1, source_target_pairs={{0,0},{4,16},{8,4},{12,20},{16,8},{20,24},{24,12},{28,28},{1,1},{5... | collective-permute-start | bytes 12296 | tf_op jit(solution)/shard_map/ppermute | solution.py:368
  26.2 7.8 %collective-permute-start.8 = (f32[8,128]{1,0:T(8,128)S(1)}, f32[8,128]{1,0:T(8,128)S(1)}, u32[]{:S(2)}, u32[]{:S(2)}) collective-permute-start(f32[8,128]{1,0:T(8,128)S(1)} %get-tuple-element.32), channel_id=1, source_target_pairs={{0,16},{4,0},{8,20},{12,4},{16,24},{20,8},{24,28},{28,12},{1,17},{... | collective-permute-start | bytes 12296 | tf_op jit(solution)/shard_map/ppermute | solution.py:369
  35.8 1.4 %collective-permute-start.9 = (bf16[128,512]{1,0:T(8,128)(2,1)S(1)}, bf16[128,512]{1,0:T(8,128)(2,1)S(1)}, u32[]{:S(2)}, u32[]{:S(2)}) collective-permute-start(bf16[128,512]{1,0:T(8,128)(2,1)S(1)} %get-tuple-element.39), channel_id=1, source_target_pairs={{0,4},{4,0},{8,12},{12,8},{16,20},{20,16},{24,28},{28,24},{1,5},{5... | collective-permute-start | bytes 393224 | tf_op jit(solution)/shard_map/ppermute | solution.py:319
  36.0 1.2 %collective-permute-start.10 = (f32[1,1024]{1,0:T(1,128)S(1)}, f32[1,1024]{1,0:T(1,128)S(1)}, u32[]{:S(2)}, u32[]{:S(2)}) collective-permute-start(f32[1,1024]{1,0:T(1,128)S(1)} %get-tuple-element.40.tot_ref), channel_id=1, source_target_pairs={{0,4},{4,0},{8,12},{12,8},{16,20},{20,16},{24,28},{28,24},{1,5},{5... | collective-permute-start | bytes 12296 | tf_op jit(solution)/shard_map/ppermute | solution.py:319
  37.3 5.8 %collective-permute-start.11 = (bf16[128,512]{1,0:T(8,128)(2,1)S(1)}, bf16[128,512]{1,0:T(8,128)(2,1)S(1)}, u32[]{:S(2)}, u32[]{:S(2)}) collective-permute-start(bf16[128,512]{1,0:T(8,128)(2,1)S(1)} %get-tuple-element.42), channel_id=1, source_target_pairs={{0,8},{4,12},{8,0},{12,4},{16,24},{20,28},{24,16},{28,20},{1,9},{5... | collective-permute-start | bytes 393224 | tf_op jit(solution)/shard_map/ppermute | solution.py:319
  39.1 4.1 %collective-permute-start.12 = (f32[1,512]{1,0:T(1,128)S(1)}, f32[1,512]{1,0:T(1,128)S(1)}, u32[]{:S(2)}, u32[]{:S(2)}) collective-permute-start(f32[1,512]{1,0:T(1,128)S(1)} %shard_map.100.mine_ref), channel_id=1, source_target_pairs={{0,8},{4,12},{8,0},{12,4},{16,24},{20,28},{24,16},{28,20},{1,9},{5... | collective-permute-start | bytes 6152 | tf_op jit(solution)/shard_map/ppermute | solution.py:319
  43.3 5.0 %collective-permute-start.13 = (bf16[128,512]{1,0:T(8,128)(2,1)S(1)}, bf16[128,512]{1,0:T(8,128)(2,1)S(1)}, u32[]{:S(2)}, u32[]{:S(2)}) collective-permute-start(bf16[128,512]{1,0:T(8,128)(2,1)S(1)} %get-tuple-element.43), channel_id=1, source_target_pairs={{0,16},{4,20},{8,24},{12,28},{16,0},{20,4},{24,8},{28,12},{1,17},{... | collective-permute-start | bytes 393224 | tf_op jit(solution)/shard_map/ppermute | solution.py:319
  48.3 1.5 %copy-start.1 = (bf16[256,128]{1,0:T(8,128)(2,1)S(1)}, bf16[256,128]{1,0:T(8,128)(2,1)}, u32[]{:S(2)}) copy-start(bf16[256,128]{1,0:T(8,128)(2,1)} %c_ref.1) | copy-start | bytes 196612
  48.4 1.4 %collective-permute-start.14 = (bf16[128,512]{1,0:T(8,128)(2,1)S(1)}, bf16[128,512]{1,0:T(8,128)(2,1)S(1)}, u32[]{:S(2)}, u32[]{:S(2)}) collective-permute-start(bf16[128,512]{1,0:T(8,128)(2,1)S(1)} %get-tuple-element.48), channel_id=1, source_target_pairs={{0,4},{4,0},{8,12},{12,8},{16,20},{20,16},{24,28},{28,24},{1,5},{5... | collective-permute-start | bytes 393224 | tf_op jit(solution)/shard_map/ppermute | solution.py:319

commit v3 on v2

--- a/solution.py
+++ b/solution.py
@@ -42,20 +42,24 @@
     )(*[pltpu.with_memory_space_constraint(a, m) if m == pltpu.HBM else a for a, m in zip(args, spaces)])
 
 
-def pack_kernel(k_ref, v_ref, out_ref):
+def pack_kernel(q_ref, k_ref, v_ref, *refs):
     width = k_ref.shape[2]
+    mine = lax.axis_index("seq") % 2
+    copies = []
 
     def inner(sems):
-        copies = [
-            pltpu.make_async_copy(ref, out_ref.at[:, :, i * width : (i + 1) * width], sems.at[i])
-            for i, ref in enumerate((k_ref, v_ref))
-        ]
+        for i, (kv_ref, q_out_ref) in enumerate((refs[:2], refs[2:])):
+            slot = mine if i == 0 else 1 - mine
+            for j, (src, dst) in enumerate(
+                ((k_ref, kv_ref.at[:, :width]), (v_ref, kv_ref.at[:, width:]), (q_ref, q_out_ref))
+            ):
+                copies.append(pltpu.make_async_copy(src.at[slot], dst, sems.at[i, j]))
         for copy in copies:
             copy.start()
         for copy in copies:
             copy.wait()
 
-    pl.run_scoped(inner, pltpu.SemaphoreType.DMA((2,)))
+    pl.run_scoped(inner, pltpu.SemaphoreType.DMA((2, 3)))
 
 
 def prepare_kernel(*refs):
@@ -127,77 +131,73 @@
         )
 
 
-def attention_kernel(second, q_ref, kv_ref, near_ref, far_even_ref, far_odd_ref, *refs):
-    if second:
-        before_ref, out_ref, sums_ref = refs
-    else:
-        out_ref, sums_ref = refs
-    me, count = lax.axis_index("seq"), lax.axis_size("seq")
-    blk, feat = q_ref.shape[1:]
-    kv_local = kv_ref.shape[2] // (2 * HDIM)
+def attention_kernel(
+    q_keep_ref, q_got_ref, kv_keep_ref, kv_got_ref, old_keep_ref, old_got_ref, out_ref, sums_ref
+):
+    me = lax.axis_index("seq")
+    blk, feat = q_keep_ref.shape
+    kv_local = kv_keep_ref.shape[1] // (2 * HDIM)
     group = feat // HDIM // kv_local
-    odd = me % 2
-    slot = 1 - odd if second else odd
-    near_slot = jnp.where(me < 1, 0, slot)
-    far_slot = jnp.where(me < 2, 0, slot)
-    block = slot * count + me
+    late = me % 2 == 1
+    old_late = jnp.where(me < 2, me % 2 == 0, late)
+    has_old = me > 0
     rows = lax.broadcasted_iota(jnp.int32, (group * blk, blk), 0) % blk
     cols = lax.broadcasted_iota(jnp.int32, (group * blk, blk), 1)
     own_ok = cols <= rows
-    far_ok = (cols > rows) & (block >= 2)
-    near_ok = (cols >= 0) & (block >= 1)
+    far_ok = cols > rows
+    near_ok = cols >= 0
     factor = math.log2(math.e) / math.sqrt(HDIM)
-    squares = jnp.zeros((blk, 1), F32)
-
-    def take(column):
+
+    def pick(keep_ref, got_ref, swapped, column):
         at = slice(column * HDIM, (column + 1) * HDIM)
-        far = jnp.where(odd == 1, far_odd_ref[far_slot, :, at], far_even_ref[far_slot, :, at])
-        return jnp.concatenate([far, near_ref[near_slot, :, at], kv_ref[slot, :, at]], 0)
-
+        keep, got = keep_ref[:, at], got_ref[:, at]
+        return jnp.where(swapped, got, keep), jnp.where(swapped, keep, got)
+
+    squares = [jnp.zeros((blk, 1), F32)] * 2
     for g in range(kv_local):
-        heads = [
-            q_ref[slot, :, (g * group + i) * HDIM : (g * group + i + 1) * HDIM] for i in range(group)
-        ]
-        query = jnp.concatenate(heads, 0)
-        score = dot(query, take(g), (1, 1))
-        ok = jnp.concatenate([far_ok, near_ok, own_ok], 1)
-        score = jnp.where(ok, score, -jnp.inf)
-        peak = jnp.max(score, axis=1, keepdims=True)
-        terms = jnp.exp2((score - peak) * factor)
-        total = jnp.sum(terms, axis=1, keepdims=True)
-        result = dot(terms.astype(BF16), take(kv_local + g)) / total
-        result = result.astype(BF16)
-        wide = result.astype(F32)
-        part = jnp.sum(wide * wide, axis=1, keepdims=True)
-        for i in range(group):
-            out_ref[:, (g * group + i) * HDIM : (g * group + i + 1) * HDIM] = result[
-                i * blk : (i + 1) * blk
-            ]
-            squares = squares + part[i * blk : (i + 1) * blk]
-    turned = jnp.transpose(jnp.broadcast_to(squares, (blk, blk)))[:8]
-    if second:
-        sums_ref[:8] = before_ref[...]
-        sums_ref[8:] = turned
-    else:
-        sums_ref[...] = turned
-
-
-def home_kernel(xa_ref, xb_ref, ra_ref, rb_ref, gain_ref, bw_ref, x_ref, keep_ref, send_ref):
-    me, count = lax.axis_index("seq"), lax.axis_size("seq")
-    blk, feat = xa_ref.shape
-    upper = me >= count // 2
+        keys = pick(old_keep_ref, old_got_ref, old_late, g) + pick(kv_keep_ref, kv_got_ref, late, g)
+        c = kv_local + g
+        vals = pick(old_keep_ref, old_got_ref, old_late, c) + pick(kv_keep_ref, kv_got_ref, late, c)
+        heads = [pick(q_keep_ref, q_got_ref, late, g * group + i) for i in range(group)]
+        for part in range(2):
+            query = jnp.concatenate([h[part] for h in heads], 0)
+            score = dot(query, jnp.concatenate(keys[part : part + 3], 0), (1, 1))
+            ok = (
+                [far_ok & has_old, near_ok & has_old, own_ok]
+                if part == 0
+                else [far_ok & has_old, near_ok, own_ok]
+            )
+            score = jnp.where(jnp.concatenate(ok, 1), score, -jnp.inf)
+            peak = jnp.max(score, axis=1, keepdims=True)
+            terms = jnp.exp2((score - peak) * factor)
+            total = jnp.sum(terms, axis=1, keepdims=True)
+            values = jnp.concatenate(vals[part : part + 3], 0)
+            result = (dot(terms.astype(BF16), values) / total).astype(BF16)
+            wide = result.astype(F32)
+            square = jnp.sum(wide * wide, axis=1, keepdims=True)
+            for i in range(group):
+                at = slice((g * group + i) * HDIM, (g * group + i + 1) * HDIM)
+                out_ref[part * blk : (part + 1) * blk, at] = result[i * blk : (i + 1) * blk]
+                squares[part] = squares[part] + square[i * blk : (i + 1) * blk]
+    for part in range(2):
+        turned = jnp.transpose(jnp.broadcast_to(squares[part], (blk, blk)))
+        sums_ref[part * 8 : part * 8 + 8] = turned[:8]
+
+
+def home_kernel(rows_ref, sums_ref, gain_ref, bw_ref, x_ref, keep_ref, send_ref):
+    mine = lax.axis_index("seq") % 2
+    toks, feat = rows_ref.shape
+    blk = toks // 2
     pairs = feat // HDIM
-    mine = me % 2
     gain = gain_ref[...]
     for part in range(2):
-        swap = upper if part == 0 else jnp.logical_not(upper)
-        sums = jnp.where(swap, rb_ref[...], ra_ref[...])
-        mean = jnp.transpose(jnp.broadcast_to(sums[:1], (blk, blk))) / (HEADS * HDIM)
+        at = slice(part * blk, (part + 1) * blk)
+        sums = sums_ref[part * 8 : part * 8 + 1]
+        mean = jnp.transpose(jnp.broadcast_to(sums, (blk, blk))) / (HEADS * HDIM)
         inv = lax.rsqrt(mean + 1e-06)[:, :1]
-        rows = jnp.where(swap, xb_ref[...], xa_ref[...]).astype(F32)
-        x_ref[part * blk : (part + 1) * blk, :] = (rows * gain * inv).astype(BF16)
-    lanes = lax.broadcasted_iota(jnp.int32, (2 * blk, HDIM), 1)
-    zero = jnp.zeros((2 * blk, HDIM), BF16)
+        x_ref[at, :] = (rows_ref[at, :].astype(F32) * gain * inv).astype(BF16)
+    lanes = lax.broadcasted_iota(jnp.int32, (toks, HDIM), 1)
+    zero = jnp.zeros((toks, HDIM), BF16)
     for p in range(pairs):
         x = x_ref[:, p * HDIM : (p + 1) * HDIM]
         spread = jnp.concatenate([jnp.where(lanes < SDIM, x, zero), jnp.where(lanes < SDIM, zero, x)], 0)
@@ -234,11 +234,8 @@
         out_ref[:, at] = (local_ref[:, at] + part * scale_ref[:, at]).astype(BF16)
 
 
-def add_kernel(a_ref, b_ref, *out_refs):
-    rows = a_ref.shape[0] // len(out_refs)
-    for i, ref in enumerate(out_refs):
-        at = slice(i * rows, (i + 1) * rows)
-        ref[...] = a_ref[at] + b_ref[at]
+def add_kernel(a_ref, b_ref, out_ref):
+    out_ref[...] = a_ref[...] + b_ref[...]
 
 
 def half_of(ref, side):
@@ -318,12 +315,19 @@
     def swap(block, bit):
         return lax.ppermute(block, "seq", [(i, i ^ (1 << bit)) for i in every])
 
-    (kv,) = call(
-        pack_kernel, [((2, blk, 2 * kv_width), BF16)], (keys, values), spaces=[pltpu.HBM] * 2
-    )
-    near = lax.ppermute(kv, "seq", [(i, (i + 1) % seq_count) for i in every])
-    far_even = lax.ppermute(kv, "seq", [(i, (i + 2) % seq_count) for i in every if i % 2 == 0])
-    far_odd = lax.ppermute(near, "seq", [(i, i + 1) for i in every if i % 2 == 0])
+    width = 2 * kv_width
+    kv_keep, q_keep, kv_send, q_send = call(
+        pack_kernel,
+        [((blk, width), BF16), ((blk, feat), BF16)] * 2,
+        (query, keys, values),
+        spaces=[pltpu.HBM] * 3,
+    )
+    chips = seq_count // 2
+    onward = [(i, i + 2) for i in range(seq_count - 2)] + [(seq_count - 2, 1)]
+    kv_got = swap(kv_send, 0)
+    old_keep = lax.ppermute(kv_keep, "seq", onward)
+    old_got = lax.ppermute(kv_got, "seq", onward)
+    q_got = swap(q_send, 0)
 
     mix, b_weighted, scale, tot, skip_row = call(
         prepare_kernel,
@@ -342,31 +346,18 @@
     core = swap(tot, 0)
     (chip,) = call(decay_kernel, [((1, half), F32)], (tot, core))
 
-    args = (query, kv, near, far_even, far_odd)
-    first, sums = call(
-        functools.partial(attention_kernel, False),
-        [((blk, feat), BF16), ((8, blk), F32)],
-        args,
-        flops=1 << 28,
-    )
-    to_a = [(i, i // 2 + (i % 2) * (seq_count // 2)) for i in every]
-    to_b = [(i, i // 2 + (1 - i % 2) * (seq_count // 2)) for i in every]
-    home_a = lax.ppermute(first, "seq", to_a)
-    second, sums = call(
-        functools.partial(attention_kernel, True),
-        [((blk, feat), BF16), ((16, blk), F32)],
-        args + (sums,),
-        flops=1 << 28,
-    )
-    home_b = lax.ppermute(second, "seq", to_b)
-    z_bits = head_count.bit_length() - 1
-    for bit in range(z_bits):
+    attended, sums = call(
+        attention_kernel,
+        [((toks, feat), BF16), ((16, blk), F32)],
+        (q_keep, q_got, kv_keep, kv_got, old_keep, old_got),
+        flops=1 << 29,
+    )
+    to_home = [(i, i // 2 + (i % 2) * chips) for i in every]
+    sums = lax.ppermute(sums, "seq", to_home)
+    rows = lax.ppermute(attended, "seq", to_home)
+    for bit in range(head_count.bit_length() - 1):
         other = lax.ppermute(sums, "head", [(i, i ^ (1 << bit)) for i in range(head_count)])
-        parts = 2 if bit == z_bits - 1 else 1
-        added = call(add_kernel, [((16 // parts, blk), F32)] * parts, (sums, other))
-        sums = added[0]
-    sums_a = lax.ppermute(added[0], "seq", to_a)
-    sums_b = lax.ppermute(added[1], "seq", to_b)
+        (sums,) = call(add_kernel, [((16, blk), F32)], (sums, other))
     decays = []
     running = [chip]
     for bit in range(1, bits - 1):
@@ -377,7 +368,7 @@
     x, keep, send = call(
         home_kernel,
         [((toks, feat), BF16), ((STATE, half), F32), ((STATE, half), BF16)],
-        (home_a, home_b, sums_a, sums_b, norm_gain[None, :], b_weighted),
+        (rows, sums, norm_gain[None, :], b_weighted),
         flops=1 << 28,
     )
     (local,) = call(local_kernel, [((toks, feat), F32)], (x, mix, skip_row), flops=1 << 29)

time: 51.2 us -> 58.1 us (1.13)
  starting transfers between devices: 23.4 us -> 34.8 us
  waiting for transfers between devices: 17.1 us -> 13.8 us
  local copies, waits for them, and re-layouts: 1.05 us -> 0.01 us
    ppermute x6 -> x8, starting transfers between devices: 3.97 us -> 20.8 us  [swap(): return lax.ppermute(block, 'seq', [(i, i ^ 1 << bit) for i in every])]
    ppermute x7 -> x4, starting transfers between devices: 15.2 us -> 9.75 us  [the longest x1 4.87 us: layer(): old_keep = lax.ppermute(kv_keep, 'seq', onward)]
    ppermute x2, waiting for transfers between devices: 4.03 us -> 2.08 us  [layer(): lax.ppermute(sums, 'head', [(i, i ^ 1 << bit) for i in range(head_count)])]
    ppermute x7 -> x4, waiting for transfers between devices: 4.06 us -> 2.62 us  [the longest x1 2.61 us: layer(): old_got = lax.ppermute(kv_got, 'seq', onward)]
    unnamed x6 -> x4, local copies, waits for them, and re-layouts: 1.05 us -> 0.01 us
    pallas_call x13 -> x12, Pallas kernels: 9.25 us -> 9.11 us  [call(): pl.pallas_call(kernel, out_shape=[jax.ShapeDtypeStruct(s, d) for s, d in...]
    ppermute x6 -> x8, waiting for transfers between devices: 9 us -> 9.07 us  [swap(): return lax.ppermute(block, 'seq', [(i, i ^ 1 << bit) for i in every])]
  transfers between devices with their start and end apart: 15 -> 14, of which waited for: 8 -> 6; matrix products, arithmetic and copies ran while one was open for 0% -> 0% of each run, Pallas kernels for 6% -> 5%
where the time goes in v3:
time: 58.1 us; the launch traced here: 57.8 us
  starting transfers between devices  34.8 us (60%)
  waiting for transfers between devices  13.8 us (24%)
  Pallas kernels  9.11 us (16%)
    ppermute x8, starting transfers between devices, swap(): return lax.ppermute(block, 'seq', [(i, i ^ 1 << bit) for i in every])  20.8 us
    pallas_call x12, Pallas kernels, call(): pl.pallas_call(kernel, out_shape=[jax.ShapeDtypeStruct(s, d) for s, d in...  9.11 us
    ppermute x8, waiting for transfers between devices, swap(): return lax.ppermute(block, 'seq', [(i, i ^ 1 << bit) for i in every])  9.07 us
    ppermute x1, starting transfers between devices, layer(): old_keep = lax.ppermute(kv_keep, 'seq', onward)  4.87 us
    ppermute x2, starting transfers between devices, layer(): lax.ppermute(sums, 'head', [(i, i ^ 1 << bit) for i in range(head_count)])  4.23 us
    ppermute x1, starting transfers between devices, layer(): old_got = lax.ppermute(kv_got, 'seq', onward)  3.4 us
    ppermute x1, waiting for transfers between devices, layer(): old_got = lax.ppermute(kv_got, 'seq', onward)  2.61 us
    ppermute x2, waiting for transfers between devices, layer(): lax.ppermute(sums, 'head', [(i, i ^ 1 << bit) for i in range(head_count)])  2.08 us
  transfers between devices with their start and end apart: 14, of which 6 were waited for; matrix products, arithmetic and copies ran while one was open for 0% of the time, Pallas kernels for 5%

profile of v3, /device:TPU:0, one launch (start us, length us, event | category | flops | bytes accessed | tf_op | source)
XLA Modules:
  0.0 57.8 jit_solution(5997071578392839810)
XLA Ops:
  0.0 1.2 %shard_map.91 = (bf16[128,512]{1,0:T(8,128)(2,1)S(1)}, bf16[128,1024]{1,0:T(8,128)(2,1)S(1)}, bf16[128,512]{1,0:T(8,128)(2,1)S(1)}, bf16[128,1024]{1,0:T(8,128)(2,1)S(1)}) custom-call(bf16[2,128,1024]{2,1,0:T(8,128)(2,1)} %q_ref.1, bf16[2,128,256]{2,1,0:T(8,128)(2,1)} %k_ref.1, bf16[2,128,256]{2,1,0:T(8,128)(2,1)} %v_ref.1), custom_call_target="tpu_custom_call" | custom-call | flops 1 | bytes 1048576 | tf_op jit(solution)/shard_map/pallas_call | solution.py:35
  1.2 0.5 collective-permute-start.1
  1.7 4.9 %collective-permute-start.2 = (bf16[128,512]{1,0:T(8,128)(2,1)S(1)}, bf16[128,512]{1,0:T(8,128)(2,1)S(1)}, u32[]{:S(2)}, u32[]{:S(2)}) collective-permute-start(bf16[128,512]{1,0:T(8,128)(2,1)S(1)} %get-tuple-element.29.kv_keep_ref), channel_id=1, source_target_pairs={{0,8},{4,12},{8,16},{12,20},{16,24},{20,28},{24,4},{1,9},{5,13},{9... | collective-permute-start | bytes 393224 | tf_op jit(solution)/shard_map/ppermute | solution.py:328
  6.6 3.4 %collective-permute-start.3 = (bf16[128,512]{1,0:T(8,128)(2,1)S(1)}, bf16[128,512]{1,0:T(8,128)(2,1)S(1)}, u32[]{:S(2)}, u32[]{:S(2)}) collective-permute-start(bf16[128,512]{1,0:T(8,128)(2,1)S(1)} %collective-permute-done.1.kv_got_ref), channel_id=1, source_target_pairs={{0,8},{4,12},{8,16},{12,20},{16,24},{20,28},{24,4},{1,9},{5,13},{9... | collective-permute-start | bytes 393224 | tf_op jit(solution)/shard_map/ppermute | solution.py:329
  10.0 2.6 %collective-permute-done.3.old_got_ref = bf16[128,512]{1,0:T(8,128)(2,1)S(1)} collective-permute-done((bf16[128,512]{1,0:T(8,128)(2,1)S(1)}, bf16[128,512]{1,0:T(8,128)(2,1)S(1)}, u32[]{:S(2)}, u32[]{:S(2)}) %collective-permute-start.3) | collective-permute-done | bytes 131104 | tf_op jit(solution)/shard_map/ppermute | solution.py:329
  12.6 1.8 %shard_map.92 = (bf16[256,1024]{1,0:T(8,128)(2,1)S(1)}, f32[16,128]{1,0:T(8,128)S(1)}) custom-call(bf16[128,1024]{1,0:T(8,128)(2,1)S(1)} %get-tuple-element.27.q_keep_ref, bf16[128,1024]{1,0:T(8,128)(2,1)S(1)} %collective-permute-done.q_got_ref, bf16[128,512]{1,0:T(8,128)(2,1)S(1)} %get-tuple-element.29.kv_keep_ref, ...), custom_call_target="tpu_custom_call" | custom-call | flops 536870912 | bytes 1048576 | tf_op jit(solution)/shard_map/pallas_call | solution.py:35
  14.4 0.8 %collective-permute-start.4 = (bf16[256,1024]{1,0:T(8,128)(2,1)S(1)}, bf16[256,1024]{1,0:T(8,128)(2,1)S(1)}, u32[]{:S(2)}, u32[]{:S(2)}) collective-permute-start(bf16[256,1024]{1,0:T(8,128)(2,1)S(1)} %get-tuple-element.31), channel_id=1, source_target_pairs={{0,0},{4,16},{8,4},{12,20},{16,8},{20,24},{24,12},{28,28},{1,1},{5... | collective-permute-start | bytes 1572872 | tf_op jit(solution)/shard_map/ppermute | solution.py:357
  15.2 0.7 %collective-permute-start.5 = (f32[16,128]{1,0:T(8,128)S(1)}, f32[16,128]{1,0:T(8,128)S(1)}, u32[]{:S(2)}, u32[]{:S(2)}) collective-permute-start(f32[16,128]{1,0:T(8,128)S(1)} %get-tuple-element.32), channel_id=1, source_target_pairs={{0,0},{4,16},{8,4},{12,20},{16,8},{20,24},{24,12},{28,28},{1,1},{5... | collective-permute-start | bytes 24584 | tf_op jit(solution)/shard_map/ppermute | solution.py:356
  15.9 1.6 %collective-permute-start.6 = (f32[16,128]{1,0:T(8,128)S(1)}, f32[16,128]{1,0:T(8,128)S(1)}, u32[]{:S(2)}, u32[]{:S(2)}) collective-permute-start(f32[16,128]{1,0:T(8,128)S(1)} %collective-permute-done.5.a_ref), channel_id=1, source_target_pairs={{0,1},{1,0},{2,3},{3,2},{4,5},{5,4},{6,7},{7,6},{8,9},{9,8},{10,11... | collective-permute-start | bytes 24584 | tf_op jit(solution)/shard_map/ppermute | solution.py:359
  17.5 2.1 %collective-permute-done.6.b_ref = f32[16,128]{1,0:T(8,128)S(1)} collective-permute-done((f32[16,128]{1,0:T(8,128)S(1)}, f32[16,128]{1,0:T(8,128)S(1)}, u32[]{:S(2)}, u32[]{:S(2)}) %collective-permute-start.6) | collective-permute-done | bytes 8224 | tf_op jit(solution)/shard_map/ppermute | solution.py:359
  19.6 2.6 %collective-permute-start.7 = (f32[16,128]{1,0:T(8,128)S(1)}, f32[16,128]{1,0:T(8,128)S(1)}, u32[]{:S(2)}, u32[]{:S(2)}) collective-permute-start(f32[16,128]{1,0:T(8,128)S(1)} %shard_map.93.a_ref), channel_id=1, source_target_pairs={{0,2},{1,3},{2,0},{3,1},{4,6},{5,7},{6,4},{7,5},{8,10},{9,11},{10,... | collective-permute-start | bytes 24584 | tf_op jit(solution)/shard_map/ppermute | solution.py:359
  22.2 2.4 %shard_map.95 = (bf16[8,256,512]{2,1,0:T(8,128)(2,1)S(1)}, bf16[8,128,512]{2,1,0:T(8,128)(2,1)S(1)}, f32[256,1024]{1,0:T(8,128)S(1)}, f32[1,1024]{1,0:T(1,128)S(1)}, f32[1,1024]{1,0:T(1,128)S(1)}) custom-call(f32[16,256]{1,0:T(8,128)} %refs_0_.1, f32[16,256]{1,0:T(8,128)} %refs_1_.1, bf16[256,128]{1,0:T(8,128)(2,1)} %refs_2_.1, bf16[256,128]{1,0:T(8,128)(2,1)} %c_ref.1, ...), custom_call_target="tpu_custom_call" | custom-call | flops 1073741824 | bytes 1048576 | tf_op jit(solution)/shard_map/pallas_call | solution.py:35
  24.6 1.7 %shard_map.96 = (bf16[256,1024]{1,0:T(8,128)(2,1)S(1)}, f32[128,512]{1,0:T(8,128)S(1)}, bf16[128,512]{1,0:T(8,128)(2,1)S(1)}) custom-call(bf16[256,1024]{1,0:T(8,128)(2,1)S(1)} %collective-permute-done.4.rows_ref, f32[16,128]{1,0:T(8,128)S(1)} %shard_map.94.sums_ref, f32[1,1024]{1,0:T(1,128)S(1)} %bitcast.1, bf16[8,128,512]{2,1,0:T(8,128)(2,1)S(1)} %get-tuple-element.33.bw_ref), custom_call_target="tpu_custom_call" | custom-call | flops 268435456 | bytes 1048576 | tf_op jit(solution)/shard_map/pallas_call | solution.py:35
  26.3 14.3 %collective-permute-start.8 = (bf16[128,512]{1,0:T(8,128)(2,1)S(1)}, bf16[128,512]{1,0:T(8,128)(2,1)S(1)}, u32[]{:S(2)}, u32[]{:S(2)}) collective-permute-start(bf16[128,512]{1,0:T(8,128)(2,1)S(1)} %get-tuple-element.39), channel_id=1, source_target_pairs={{0,4},{4,0},{8,12},{12,8},{16,20},{20,16},{24,28},{28,24},{1,5},{5... | collective-permute-start | bytes 393224 | tf_op jit(solution)/shard_map/ppermute | solution.py:316
  40.7 1.1 %collective-permute-done.9.core_ref = f32[1,1024]{1,0:T(1,128)S(1)} collective-permute-done((f32[1,1024]{1,0:T(1,128)S(1)}, f32[1,1024]{1,0:T(1,128)S(1)}, u32[]{:S(2)}, u32[]{:S(2)}) %collective-permute-start.9) | collective-permute-done | bytes 4128 | tf_op jit(solution)/shard_map/ppermute | solution.py:316
  41.7 0.1 shard_map.98
  41.9 4.0 %collective-permute-start.10 = (bf16[128,512]{1,0:T(8,128)(2,1)S(1)}, bf16[128,512]{1,0:T(8,128)(2,1)S(1)}, u32[]{:S(2)}, u32[]{:S(2)}) collective-permute-start(bf16[128,512]{1,0:T(8,128)(2,1)S(1)} %get-tuple-element.42), channel_id=1, source_target_pairs={{0,8},{4,12},{8,0},{12,4},{16,24},{20,28},{24,16},{28,20},{1,9},{5... | collective-permute-start | bytes 393224 | tf_op jit(solution)/shard_map/ppermute | solution.py:316
  45.9 0.1 collective-permute-start.11
  46.0 3.9 %collective-permute-done.11.decay_ref = f32[1,512]{1,0:T(1,128)S(1)} collective-permute-done((f32[1,512]{1,0:T(1,128)S(1)}, f32[1,512]{1,0:T(1,128)S(1)}, u32[]{:S(2)}, u32[]{:S(2)}) %collective-permute-start.11) | collective-permute-done | bytes 2080 | tf_op jit(solution)/shard_map/ppermute | solution.py:316
  50.0 1.8 %collective-permute-start.12 = (bf16[128,512]{1,0:T(8,128)(2,1)S(1)}, bf16[128,512]{1,0:T(8,128)(2,1)S(1)}, u32[]{:S(2)}, u32[]{:S(2)}) collective-permute-start(bf16[128,512]{1,0:T(8,128)(2,1)S(1)} %get-tuple-element.43), channel_id=1, source_target_pairs={{0,16},{4,20},{8,24},{12,28},{16,0},{20,4},{24,8},{28,12},{1,17},{... | collective-permute-start | bytes 393224 | tf_op jit(solution)/shard_map/ppermute | solution.py:316
  51.8 3.4 %collective-permute-done.12.theirs_ref = bf16[128,512]{1,0:T(8,128)(2,1)S(1)} collective-permute-done((bf16[128,512]{1,0:T(8,128)(2,1)S(1)}, bf16[128,512]{1,0:T(8,128)(2,1)S(1)}, u32[]{:S(2)}, u32[]{:S(2)}) %collective-permute-start.12) | collective-permute-done | bytes 131104 | tf_op jit(solution)/shard_map/ppermute | solution.py:316
  55.4 0.7 %shard_map.97.local_ref = f32[256,1024]{1,0:T(8,128)S(1)} custom-call(bf16[256,1024]{1,0:T(8,128)(2,1)S(1)} %get-tuple-element.34.x_ref, bf16[8,256,512]{2,1,0:T(8,128)(2,1)S(1)} %get-tuple-element.35.mix_ref, f32[1,1024]{1,0:T(1,128)S(1)} %get-tuple-element.36.skip_ref), custom_call_target="tpu_custom_call" | custom-call | flops 536870912 | bytes 1048576 | tf_op jit(solution)/shard_map/pallas_call | solution.py:35
  56.1 0.6 %collective-permute-done.13.other_ref = bf16[128,512]{1,0:T(8,128)(2,1)S(1)} collective-permute-done((bf16[128,512]{1,0:T(8,128)(2,1)S(1)}, bf16[128,512]{1,0:T(8,128)(2,1)S(1)}, u32[]{:S(2)}, u32[]{:S(2)}) %collective-permute-start.13) | collective-permute-done | bytes 131104 | tf_op jit(solution)/shard_map/ppermute | solution.py:316
  56.7 1.1 %shard_map.102 = bf16[256,1024]{1,0:T(8,128)(2,1)} custom-call(f32[256,1024]{1,0:T(8,128)S(1)} %shard_map.97.local_ref, f32[256,1024]{1,0:T(8,128)S(1)} %get-tuple-element.37.scale_ref, bf16[256,128]{1,0:T(8,128)(2,1)S(1)} %copy-done, bf16[128,512]{1,0:T(8,128)(2,1)S(1)} %get-tuple-element.47.own_ref, bf16[128,512]{1,0:T(8,128)(2,1)S(1)} %collective-permute-done.13.other_ref), custom_call_target="tpu_custom_call" | custom-call | flops 268435456 | bytes 1048576 | tf_op jit(solution)/shard_map/pallas_call | solution.py:35
  (20 shorter events, 0.4 us)
Async XLA Ops:
  1.2 5.4 %collective-permute-start.1 = (bf16[128,512]{1,0:T(8,128)(2,1)S(1)}, bf16[128,512]{1,0:T(8,128)(2,1)S(1)}, u32[]{:S(2)}, u32[]{:S(2)}) collective-permute-start(bf16[128,512]{1,0:T(8,128)(2,1)S(1)} %get-tuple-element.30), channel_id=1, source_target_pairs={{0,4},{4,0},{8,12},{12,8},{16,20},{20,16},{24,28},{28,24},{1,5},{5... | collective-permute-start | bytes 393224 | tf_op jit(solution)/shard_map/ppermute | solution.py:316
  1.7 10.9 %collective-permute-start = (bf16[128,1024]{1,0:T(8,128)(2,1)S(1)}, bf16[128,1024]{1,0:T(8,128)(2,1)S(1)}, u32[]{:S(2)}, u32[]{:S(2)}) collective-permute-start(bf16[128,1024]{1,0:T(8,128)(2,1)S(1)} %get-tuple-element.28), channel_id=1, source_target_pairs={{0,4},{4,0},{8,12},{12,8},{16,20},{20,16},{24,28},{28,24},{1,5},{5... | collective-permute-start | bytes 786440 | tf_op jit(solution)/shard_map/ppermute | solution.py:316
  1.7 8.3 %collective-permute-start.2 = (bf16[128,512]{1,0:T(8,128)(2,1)S(1)}, bf16[128,512]{1,0:T(8,128)(2,1)S(1)}, u32[]{:S(2)}, u32[]{:S(2)}) collective-permute-start(bf16[128,512]{1,0:T(8,128)(2,1)S(1)} %get-tuple-element.29.kv_keep_ref), channel_id=1, source_target_pairs={{0,8},{4,12},{8,16},{12,20},{16,24},{20,28},{24,4},{1,9},{5,13},{9... | collective-permute-start | bytes 393224 | tf_op jit(solution)/shard_map/ppermute | solution.py:328
  6.6 6.0 %collective-permute-start.3 = (bf16[128,512]{1,0:T(8,128)(2,1)S(1)}, bf16[128,512]{1,0:T(8,128)(2,1)S(1)}, u32[]{:S(2)}, u32[]{:S(2)}) collective-permute-start(bf16[128,512]{1,0:T(8,128)(2,1)S(1)} %collective-permute-done.1.kv_got_ref), channel_id=1, source_target_pairs={{0,8},{4,12},{8,16},{12,20},{16,24},{20,28},{24,4},{1,9},{5,13},{9... | collective-permute-start | bytes 393224 | tf_op jit(solution)/shard_map/ppermute | solution.py:329
  14.4 10.3 %copy-start.1 = (f32[1024]{0:T(1024)S(1)}, f32[1024]{0:T(1024)}, u32[]{:S(2)}) copy-start(f32[1024]{0:T(1024)} %param.12) | copy-start | bytes 12292
  14.4 10.2 %collective-permute-start.4 = (bf16[256,1024]{1,0:T(8,128)(2,1)S(1)}, bf16[256,1024]{1,0:T(8,128)(2,1)S(1)}, u32[]{:S(2)}, u32[]{:S(2)}) collective-permute-start(bf16[256,1024]{1,0:T(8,128)(2,1)S(1)} %get-tuple-element.31), channel_id=1, source_target_pairs={{0,0},{4,16},{8,4},{12,20},{16,8},{20,24},{24,12},{28,28},{1,1},{5... | collective-permute-start | bytes 1572872 | tf_op jit(solution)/shard_map/ppermute | solution.py:357
  15.2 0.7 %collective-permute-start.5 = (f32[16,128]{1,0:T(8,128)S(1)}, f32[16,128]{1,0:T(8,128)S(1)}, u32[]{:S(2)}, u32[]{:S(2)}) collective-permute-start(f32[16,128]{1,0:T(8,128)S(1)} %get-tuple-element.32), channel_id=1, source_target_pairs={{0,0},{4,16},{8,4},{12,20},{16,8},{20,24},{24,12},{28,28},{1,1},{5... | collective-permute-start | bytes 24584 | tf_op jit(solution)/shard_map/ppermute | solution.py:356
  15.9 3.7 %collective-permute-start.6 = (f32[16,128]{1,0:T(8,128)S(1)}, f32[16,128]{1,0:T(8,128)S(1)}, u32[]{:S(2)}, u32[]{:S(2)}) collective-permute-start(f32[16,128]{1,0:T(8,128)S(1)} %collective-permute-done.5.a_ref), channel_id=1, source_target_pairs={{0,1},{1,0},{2,3},{3,2},{4,5},{5,4},{6,7},{7,6},{8,9},{9,8},{10,11... | collective-permute-start | bytes 24584 | tf_op jit(solution)/shard_map/ppermute | solution.py:359
  19.6 5.0 %collective-permute-start.7 = (f32[16,128]{1,0:T(8,128)S(1)}, f32[16,128]{1,0:T(8,128)S(1)}, u32[]{:S(2)}, u32[]{:S(2)}) collective-permute-start(f32[16,128]{1,0:T(8,128)S(1)} %shard_map.93.a_ref), channel_id=1, source_target_pairs={{0,2},{1,3},{2,0},{3,1},{4,6},{5,7},{6,4},{7,5},{8,10},{9,11},{10,... | collective-permute-start | bytes 24584 | tf_op jit(solution)/shard_map/ppermute | solution.py:359
  26.3 15.4 %collective-permute-start.8 = (bf16[128,512]{1,0:T(8,128)(2,1)S(1)}, bf16[128,512]{1,0:T(8,128)(2,1)S(1)}, u32[]{:S(2)}, u32[]{:S(2)}) collective-permute-start(bf16[128,512]{1,0:T(8,128)(2,1)S(1)} %get-tuple-element.39), channel_id=1, source_target_pairs={{0,4},{4,0},{8,12},{12,8},{16,20},{20,16},{24,28},{28,24},{1,5},{5... | collective-permute-start | bytes 393224 | tf_op jit(solution)/shard_map/ppermute | solution.py:316
  40.6 1.2 %collective-permute-start.9 = (f32[1,1024]{1,0:T(1,128)S(1)}, f32[1,1024]{1,0:T(1,128)S(1)}, u32[]{:S(2)}, u32[]{:S(2)}) collective-permute-start(f32[1,1024]{1,0:T(1,128)S(1)} %get-tuple-element.40.tot_ref), channel_id=1, source_target_pairs={{0,4},{4,0},{8,12},{12,8},{16,20},{20,16},{24,28},{28,24},{1,5},{5... | collective-permute-start | bytes 12296 | tf_op jit(solution)/shard_map/ppermute | solution.py:316
  41.9 8.1 %collective-permute-start.10 = (bf16[128,512]{1,0:T(8,128)(2,1)S(1)}, bf16[128,512]{1,0:T(8,128)(2,1)S(1)}, u32[]{:S(2)}, u32[]{:S(2)}) collective-permute-start(bf16[128,512]{1,0:T(8,128)(2,1)S(1)} %get-tuple-element.42), channel_id=1, source_target_pairs={{0,8},{4,12},{8,0},{12,4},{16,24},{20,28},{24,16},{28,20},{1,9},{5... | collective-permute-start | bytes 393224 | tf_op jit(solution)/shard_map/ppermute | solution.py:316
  45.9 4.0 %collective-permute-start.11 = (f32[1,512]{1,0:T(1,128)S(1)}, f32[1,512]{1,0:T(1,128)S(1)}, u32[]{:S(2)}, u32[]{:S(2)}) collective-permute-start(f32[1,512]{1,0:T(1,128)S(1)} %shard_map.99.mine_ref), channel_id=1, source_target_pairs={{0,8},{4,12},{8,0},{12,4},{16,24},{20,28},{24,16},{28,20},{1,9},{5... | collective-permute-start | bytes 6152 | tf_op jit(solution)/shard_map/ppermute | solution.py:316
  50.0 5.2 %collective-permute-start.12 = (bf16[128,512]{1,0:T(8,128)(2,1)S(1)}, bf16[128,512]{1,0:T(8,128)(2,1)S(1)}, u32[]{:S(2)}, u32[]{:S(2)}) collective-permute-start(bf16[128,512]{1,0:T(8,128)(2,1)S(1)} %get-tuple-element.43), channel_id=1, source_target_pairs={{0,16},{4,20},{8,24},{12,28},{16,0},{20,4},{24,8},{28,12},{1,17},{... | collective-permute-start | bytes 393224 | tf_op jit(solution)/shard_map/ppermute | solution.py:316
  55.2 1.5 %copy-start = (bf16[256,128]{1,0:T(8,128)(2,1)S(1)}, bf16[256,128]{1,0:T(8,128)(2,1)}, u32[]{:S(2)}) copy-start(bf16[256,128]{1,0:T(8,128)(2,1)} %c_ref.1) | copy-start | bytes 196612
  55.3 1.4 %collective-permute-start.13 = (bf16[128,512]{1,0:T(8,128)(2,1)S(1)}, bf16[128,512]{1,0:T(8,128)(2,1)S(1)}, u32[]{:S(2)}, u32[]{:S(2)}) collective-permute-start(bf16[128,512]{1,0:T(8,128)(2,1)S(1)} %get-tuple-element.48), channel_id=1, source_target_pairs={{0,4},{4,0},{8,12},{12,8},{16,20},{20,16},{24,28},{28,24},{1,5},{5... | collective-permute-start | bytes 393224 | tf_op jit(solution)/shard_map/ppermute | solution.py:316

commit v4 on v3

--- a/solution.py
+++ b/solution.py
@@ -49,7 +49,7 @@
 
     def inner(sems):
         for i, (kv_ref, q_out_ref) in enumerate((refs[:2], refs[2:])):
-            slot = mine if i == 0 else 1 - mine
+            slot = 1 - mine if i == 0 else mine
             for j, (src, dst) in enumerate(
                 ((k_ref, kv_ref.at[:, :width]), (v_ref, kv_ref.at[:, width:]), (q_ref, q_out_ref))
             ):
@@ -140,7 +140,7 @@
     group = feat // HDIM // kv_local
     late = me % 2 == 1
     old_late = jnp.where(me < 2, me % 2 == 0, late)
-    has_old = me > 0
+    has_old = me != 1
     rows = lax.broadcasted_iota(jnp.int32, (group * blk, blk), 0) % blk
     cols = lax.broadcasted_iota(jnp.int32, (group * blk, blk), 1)
     own_ok = cols <= rows
@@ -323,7 +323,7 @@
         spaces=[pltpu.HBM] * 3,
     )
     chips = seq_count // 2
-    onward = [(i, i + 2) for i in range(seq_count - 2)] + [(seq_count - 2, 1)]
+    onward = [(i, i + 2) for i in range(seq_count - 2)] + [(seq_count - 2, 1), (seq_count - 1, 0)]
     kv_got = swap(kv_send, 0)
     old_keep = lax.ppermute(kv_keep, "seq", onward)
     old_got = lax.ppermute(kv_got, "seq", onward)
@@ -352,7 +352,7 @@
         (q_keep, q_got, kv_keep, kv_got, old_keep, old_got),
         flops=1 << 29,
     )
-    to_home = [(i, i // 2 + (i % 2) * chips) for i in every]
+    to_home = [(i, i // 2 + (1 - i % 2) * chips) for i in every]
     sums = lax.ppermute(sums, "seq", to_home)
     rows = lax.ppermute(attended, "seq", to_home)
     for bit in range(head_count.bit_length() - 1):

time: 58.1 us -> 54.2 us (0.933)
  starting transfers between devices: 34.8 us -> 17.5 us
  waiting for transfers between devices: 13.8 us -> 27.4 us
    ppermute x8, starting transfers between devices: 20.8 us -> 5.76 us  [swap(): return lax.ppermute(block, 'seq', [(i, i ^ 1 << bit) for i in every])]
    ppermute x1, waiting for transfers between devices: 0.01 us -> 11.7 us  [layer(): sums = lax.ppermute(sums, 'seq', to_home)]
    ppermute x1, waiting for transfers between devices: 0.01 us -> 2.43 us  [layer(): old_keep = lax.ppermute(kv_keep, 'seq', onward)]
    ppermute x1, starting transfers between devices: 3.4 us -> 1.49 us  [layer(): old_got = lax.ppermute(kv_got, 'seq', onward)]
    ppermute x1, starting transfers between devices: 4.87 us -> 2.97 us  [layer(): old_keep = lax.ppermute(kv_keep, 'seq', onward)]
    ppermute x1, starting transfers between devices: 0.82 us -> 2.45 us  [layer(): rows = lax.ppermute(attended, 'seq', to_home)]
    ppermute x8, waiting for transfers between devices: 9.07 us -> 8.35 us  [swap(): return lax.ppermute(block, 'seq', [(i, i ^ 1 << bit) for i in every])]
  transfers between devices with their start and end apart: 14 -> 14, of which waited for: 6 -> 8; matrix products, arithmetic and copies ran while one was open for 0% -> 0% of each run, Pallas kernels for 5% -> 6%
where the time goes in v4:
time: 54.2 us; the launch traced here: 54.1 us
  waiting for transfers between devices  27.4 us (51%)
  starting transfers between devices  17.5 us (32%)
  Pallas kernels  9.11 us (17%)
    ppermute x1, waiting for transfers between devices, layer(): sums = lax.ppermute(sums, 'seq', to_home)  11.7 us
    pallas_call x12, Pallas kernels, call(): pl.pallas_call(kernel, out_shape=[jax.ShapeDtypeStruct(s, d) for s, d in...  9.11 us
    ppermute x8, waiting for transfers between devices, swap(): return lax.ppermute(block, 'seq', [(i, i ^ 1 << bit) for i in every])  8.35 us
    ppermute x8, starting transfers between devices, swap(): return lax.ppermute(block, 'seq', [(i, i ^ 1 << bit) for i in every])  5.76 us
    ppermute x2, starting transfers between devices, layer(): lax.ppermute(sums, 'head', [(i, i ^ 1 << bit) for i in range(head_count)])  4.23 us
    ppermute x1, starting transfers between devices, layer(): old_keep = lax.ppermute(kv_keep, 'seq', onward)  2.97 us
    ppermute x1, waiting for transfers between devices, layer(): old_got = lax.ppermute(kv_got, 'seq', onward)  2.81 us
    ppermute x1, starting transfers between devices, layer(): rows = lax.ppermute(attended, 'seq', to_home)  2.45 us
  transfers between devices with their start and end apart: 14, of which 8 were waited for; matrix products, arithmetic and copies ran while one was open for 0% of the time, Pallas kernels for 6%

profile of v4, /device:TPU:0, one launch (start us, length us, event | category | flops | bytes accessed | tf_op | source)
XLA Modules:
  0.0 54.1 jit_solution(9299739584126300845)
XLA Ops:
  0.0 1.2 %shard_map.91 = (bf16[128,512]{1,0:T(8,128)(2,1)S(1)}, bf16[128,1024]{1,0:T(8,128)(2,1)S(1)}, bf16[128,512]{1,0:T(8,128)(2,1)S(1)}, bf16[128,1024]{1,0:T(8,128)(2,1)S(1)}) custom-call(bf16[2,128,1024]{2,1,0:T(8,128)(2,1)} %q_ref.1, bf16[2,128,256]{2,1,0:T(8,128)(2,1)} %k_ref.1, bf16[2,128,256]{2,1,0:T(8,128)(2,1)} %v_ref.1), custom_call_target="tpu_custom_call" | custom-call | flops 1 | bytes 1048576 | tf_op jit(solution)/shard_map/pallas_call | solution.py:35
  1.7 3.0 %collective-permute-start.2 = (bf16[128,512]{1,0:T(8,128)(2,1)S(1)}, bf16[128,512]{1,0:T(8,128)(2,1)S(1)}, u32[]{:S(2)}, u32[]{:S(2)}) collective-permute-start(bf16[128,512]{1,0:T(8,128)(2,1)S(1)} %get-tuple-element.29.kv_keep_ref), channel_id=1, source_target_pairs={{0,8},{4,12},{8,16},{12,20},{16,24},{20,28},{24,4},{28,0},{1,9},{5... | collective-permute-start | bytes 393224 | tf_op jit(solution)/shard_map/ppermute | solution.py:328
  4.6 1.5 %collective-permute-start.3 = (bf16[128,512]{1,0:T(8,128)(2,1)S(1)}, bf16[128,512]{1,0:T(8,128)(2,1)S(1)}, u32[]{:S(2)}, u32[]{:S(2)}) collective-permute-start(bf16[128,512]{1,0:T(8,128)(2,1)S(1)} %collective-permute-done.1.kv_got_ref), channel_id=1, source_target_pairs={{0,8},{4,12},{8,16},{12,20},{16,24},{20,28},{24,4},{28,0},{1,9},{5... | collective-permute-start | bytes 393224 | tf_op jit(solution)/shard_map/ppermute | solution.py:329
  6.1 2.4 %collective-permute-done.2.old_keep_ref = bf16[128,512]{1,0:T(8,128)(2,1)S(1)} collective-permute-done((bf16[128,512]{1,0:T(8,128)(2,1)S(1)}, bf16[128,512]{1,0:T(8,128)(2,1)S(1)}, u32[]{:S(2)}, u32[]{:S(2)}) %collective-permute-start.2) | collective-permute-done | bytes 131104 | tf_op jit(solution)/shard_map/ppermute | solution.py:328
  8.6 2.8 %collective-permute-done.3.old_got_ref = bf16[128,512]{1,0:T(8,128)(2,1)S(1)} collective-permute-done((bf16[128,512]{1,0:T(8,128)(2,1)S(1)}, bf16[128,512]{1,0:T(8,128)(2,1)S(1)}, u32[]{:S(2)}, u32[]{:S(2)}) %collective-permute-start.3) | collective-permute-done | bytes 131104 | tf_op jit(solution)/shard_map/ppermute | solution.py:329
  11.4 1.8 %shard_map.92 = (bf16[256,1024]{1,0:T(8,128)(2,1)S(1)}, f32[16,128]{1,0:T(8,128)S(1)}) custom-call(bf16[128,1024]{1,0:T(8,128)(2,1)S(1)} %get-tuple-element.27.q_keep_ref, bf16[128,1024]{1,0:T(8,128)(2,1)S(1)} %collective-permute-done.q_got_ref, bf16[128,512]{1,0:T(8,128)(2,1)S(1)} %get-tuple-element.29.kv_keep_ref, ...), custom_call_target="tpu_custom_call" | custom-call | flops 536870912 | bytes 1048576 | tf_op jit(solution)/shard_map/pallas_call | solution.py:35
  13.2 2.5 %collective-permute-start.4 = (bf16[256,1024]{1,0:T(8,128)(2,1)S(1)}, bf16[256,1024]{1,0:T(8,128)(2,1)S(1)}, u32[]{:S(2)}, u32[]{:S(2)}) collective-permute-start(bf16[256,1024]{1,0:T(8,128)(2,1)S(1)} %get-tuple-element.31), channel_id=1, source_target_pairs={{0,16},{4,0},{8,20},{12,4},{16,24},{20,8},{24,28},{28,12},{1,17},{... | collective-permute-start | bytes 1572872 | tf_op jit(solution)/shard_map/ppermute | solution.py:357
  15.6 0.6 %collective-permute-start.5 = (f32[16,128]{1,0:T(8,128)S(1)}, f32[16,128]{1,0:T(8,128)S(1)}, u32[]{:S(2)}, u32[]{:S(2)}) collective-permute-start(f32[16,128]{1,0:T(8,128)S(1)} %get-tuple-element.32), channel_id=1, source_target_pairs={{0,16},{4,0},{8,20},{12,4},{16,24},{20,8},{24,28},{28,12},{1,17},{... | collective-permute-start | bytes 24584 | tf_op jit(solution)/shard_map/ppermute | solution.py:356
  16.2 11.7 %collective-permute-done.5.a_ref = f32[16,128]{1,0:T(8,128)S(1)} collective-permute-done((f32[16,128]{1,0:T(8,128)S(1)}, f32[16,128]{1,0:T(8,128)S(1)}, u32[]{:S(2)}, u32[]{:S(2)}) %collective-permute-start.5) | collective-permute-done | bytes 8224 | tf_op jit(solution)/shard_map/ppermute | solution.py:356
  27.9 1.6 %collective-permute-start.6 = (f32[16,128]{1,0:T(8,128)S(1)}, f32[16,128]{1,0:T(8,128)S(1)}, u32[]{:S(2)}, u32[]{:S(2)}) collective-permute-start(f32[16,128]{1,0:T(8,128)S(1)} %collective-permute-done.5.a_ref), channel_id=1, source_target_pairs={{0,1},{1,0},{2,3},{3,2},{4,5},{5,4},{6,7},{7,6},{8,9},{9,8},{10,11... | collective-permute-start | bytes 24584 | tf_op jit(solution)/shard_map/ppermute | solution.py:359
  29.6 2.0 %collective-permute-done.6.b_ref = f32[16,128]{1,0:T(8,128)S(1)} collective-permute-done((f32[16,128]{1,0:T(8,128)S(1)}, f32[16,128]{1,0:T(8,128)S(1)}, u32[]{:S(2)}, u32[]{:S(2)}) %collective-permute-start.6) | collective-permute-done | bytes 8224 | tf_op jit(solution)/shard_map/ppermute | solution.py:359
  31.6 2.6 %collective-permute-start.7 = (f32[16,128]{1,0:T(8,128)S(1)}, f32[16,128]{1,0:T(8,128)S(1)}, u32[]{:S(2)}, u32[]{:S(2)}) collective-permute-start(f32[16,128]{1,0:T(8,128)S(1)} %shard_map.93.a_ref), channel_id=1, source_target_pairs={{0,2},{1,3},{2,0},{3,1},{4,6},{5,7},{6,4},{7,5},{8,10},{9,11},{10,... | collective-permute-start | bytes 24584 | tf_op jit(solution)/shard_map/ppermute | solution.py:359
  34.2 2.4 %shard_map.95 = (bf16[8,256,512]{2,1,0:T(8,128)(2,1)S(1)}, bf16[8,128,512]{2,1,0:T(8,128)(2,1)S(1)}, f32[256,1024]{1,0:T(8,128)S(1)}, f32[1,1024]{1,0:T(1,128)S(1)}, f32[1,1024]{1,0:T(1,128)S(1)}) custom-call(f32[16,256]{1,0:T(8,128)} %refs_0_.1, f32[16,256]{1,0:T(8,128)} %refs_1_.1, bf16[256,128]{1,0:T(8,128)(2,1)} %refs_2_.1, bf16[256,128]{1,0:T(8,128)(2,1)} %c_ref.1, ...), custom_call_target="tpu_custom_call" | custom-call | flops 1073741824 | bytes 1048576 | tf_op jit(solution)/shard_map/pallas_call | solution.py:35
  36.7 1.7 %shard_map.96 = (bf16[256,1024]{1,0:T(8,128)(2,1)S(1)}, f32[128,512]{1,0:T(8,128)S(1)}, bf16[128,512]{1,0:T(8,128)(2,1)S(1)}) custom-call(bf16[256,1024]{1,0:T(8,128)(2,1)S(1)} %collective-permute-done.4.rows_ref, f32[16,128]{1,0:T(8,128)S(1)} %shard_map.94.sums_ref, f32[1,1024]{1,0:T(1,128)S(1)} %bitcast.1, bf16[8,128,512]{2,1,0:T(8,128)(2,1)S(1)} %get-tuple-element.33.bw_ref), custom_call_target="tpu_custom_call" | custom-call | flops 268435456 | bytes 1048576 | tf_op jit(solution)/shard_map/pallas_call | solution.py:35
  38.4 0.5 collective-permute-start.9
  38.9 0.8 %collective-permute-done.9.core_ref = f32[1,1024]{1,0:T(1,128)S(1)} collective-permute-done((f32[1,1024]{1,0:T(1,128)S(1)}, f32[1,1024]{1,0:T(1,128)S(1)}, u32[]{:S(2)}, u32[]{:S(2)}) %collective-permute-start.9) | collective-permute-done | bytes 4128 | tf_op jit(solution)/shard_map/ppermute | solution.py:316
  39.9 1.5 %collective-permute-start.10 = (bf16[128,512]{1,0:T(8,128)(2,1)S(1)}, bf16[128,512]{1,0:T(8,128)(2,1)S(1)}, u32[]{:S(2)}, u32[]{:S(2)}) collective-permute-start(bf16[128,512]{1,0:T(8,128)(2,1)S(1)} %get-tuple-element.42), channel_id=1, source_target_pairs={{0,8},{4,12},{8,0},{12,4},{16,24},{20,28},{24,16},{28,20},{1,9},{5... | collective-permute-start | bytes 393224 | tf_op jit(solution)/shard_map/ppermute | solution.py:316
  41.3 0.6 %collective-permute-start.11 = (f32[1,512]{1,0:T(1,128)S(1)}, f32[1,512]{1,0:T(1,128)S(1)}, u32[]{:S(2)}, u32[]{:S(2)}) collective-permute-start(f32[1,512]{1,0:T(1,128)S(1)} %shard_map.99.mine_ref), channel_id=1, source_target_pairs={{0,8},{4,12},{8,0},{12,4},{16,24},{20,28},{24,16},{28,20},{1,9},{5... | collective-permute-start | bytes 6152 | tf_op jit(solution)/shard_map/ppermute | solution.py:316
  42.0 3.7 %collective-permute-done.11.decay_ref = f32[1,512]{1,0:T(1,128)S(1)} collective-permute-done((f32[1,512]{1,0:T(1,128)S(1)}, f32[1,512]{1,0:T(1,128)S(1)}, u32[]{:S(2)}, u32[]{:S(2)}) %collective-permute-start.11) | collective-permute-done | bytes 2080 | tf_op jit(solution)/shard_map/ppermute | solution.py:316
  45.8 2.5 %collective-permute-start.12 = (bf16[128,512]{1,0:T(8,128)(2,1)S(1)}, bf16[128,512]{1,0:T(8,128)(2,1)S(1)}, u32[]{:S(2)}, u32[]{:S(2)}) collective-permute-start(bf16[128,512]{1,0:T(8,128)(2,1)S(1)} %get-tuple-element.43), channel_id=1, source_target_pairs={{0,16},{4,20},{8,24},{12,28},{16,0},{20,4},{24,8},{28,12},{1,17},{... | collective-permute-start | bytes 393224 | tf_op jit(solution)/shard_map/ppermute | solution.py:316
  48.3 3.1 %collective-permute-done.12.theirs_ref = bf16[128,512]{1,0:T(8,128)(2,1)S(1)} collective-permute-done((bf16[128,512]{1,0:T(8,128)(2,1)S(1)}, bf16[128,512]{1,0:T(8,128)(2,1)S(1)}, u32[]{:S(2)}, u32[]{:S(2)}) %collective-permute-start.12) | collective-permute-done | bytes 131104 | tf_op jit(solution)/shard_map/ppermute | solution.py:316
  51.6 0.7 %shard_map.97.local_ref = f32[256,1024]{1,0:T(8,128)S(1)} custom-call(bf16[256,1024]{1,0:T(8,128)(2,1)S(1)} %get-tuple-element.34.x_ref, bf16[8,256,512]{2,1,0:T(8,128)(2,1)S(1)} %get-tuple-element.35.mix_ref, f32[1,1024]{1,0:T(1,128)S(1)} %get-tuple-element.36.skip_ref), custom_call_target="tpu_custom_call" | custom-call | flops 536870912 | bytes 1048576 | tf_op jit(solution)/shard_map/pallas_call | solution.py:35
  52.3 0.6 %collective-permute-done.13.other_ref = bf16[128,512]{1,0:T(8,128)(2,1)S(1)} collective-permute-done((bf16[128,512]{1,0:T(8,128)(2,1)S(1)}, bf16[128,512]{1,0:T(8,128)(2,1)S(1)}, u32[]{:S(2)}, u32[]{:S(2)}) %collective-permute-start.13) | collective-permute-done | bytes 131104 | tf_op jit(solution)/shard_map/ppermute | solution.py:316
  53.0 1.1 %shard_map.102 = bf16[256,1024]{1,0:T(8,128)(2,1)} custom-call(f32[256,1024]{1,0:T(8,128)S(1)} %shard_map.97.local_ref, f32[256,1024]{1,0:T(8,128)S(1)} %get-tuple-element.37.scale_ref, bf16[256,128]{1,0:T(8,128)(2,1)S(1)} %copy-done, bf16[128,512]{1,0:T(8,128)(2,1)S(1)} %get-tuple-element.47.own_ref, bf16[128,512]{1,0:T(8,128)(2,1)S(1)} %collective-permute-done.13.other_ref), custom_call_target="tpu_custom_call" | custom-call | flops 268435456 | bytes 1048576 | tf_op jit(solution)/shard_map/pallas_call | solution.py:35
  (20 shorter events, 1.0 us)
Async XLA Ops:
  1.2 3.5 %collective-permute-start.1 = (bf16[128,512]{1,0:T(8,128)(2,1)S(1)}, bf16[128,512]{1,0:T(8,128)(2,1)S(1)}, u32[]{:S(2)}, u32[]{:S(2)}) collective-permute-start(bf16[128,512]{1,0:T(8,128)(2,1)S(1)} %get-tuple-element.30), channel_id=1, source_target_pairs={{0,4},{4,0},{8,12},{12,8},{16,20},{20,16},{24,28},{28,24},{1,5},{5... | collective-permute-start | bytes 393224 | tf_op jit(solution)/shard_map/ppermute | solution.py:316
  1.7 9.7 %collective-permute-start = (bf16[128,1024]{1,0:T(8,128)(2,1)S(1)}, bf16[128,1024]{1,0:T(8,128)(2,1)S(1)}, u32[]{:S(2)}, u32[]{:S(2)}) collective-permute-start(bf16[128,1024]{1,0:T(8,128)(2,1)S(1)} %get-tuple-element.28), channel_id=1, source_target_pairs={{0,4},{4,0},{8,12},{12,8},{16,20},{20,16},{24,28},{28,24},{1,5},{5... | collective-permute-start | bytes 786440 | tf_op jit(solution)/shard_map/ppermute | solution.py:316
  1.7 6.9 %collective-permute-start.2 = (bf16[128,512]{1,0:T(8,128)(2,1)S(1)}, bf16[128,512]{1,0:T(8,128)(2,1)S(1)}, u32[]{:S(2)}, u32[]{:S(2)}) collective-permute-start(bf16[128,512]{1,0:T(8,128)(2,1)S(1)} %get-tuple-element.29.kv_keep_ref), channel_id=1, source_target_pairs={{0,8},{4,12},{8,16},{12,20},{16,24},{20,28},{24,4},{28,0},{1,9},{5... | collective-permute-start | bytes 393224 | tf_op jit(solution)/shard_map/ppermute | solution.py:328
  4.6 6.7 %collective-permute-start.3 = (bf16[128,512]{1,0:T(8,128)(2,1)S(1)}, bf16[128,512]{1,0:T(8,128)(2,1)S(1)}, u32[]{:S(2)}, u32[]{:S(2)}) collective-permute-start(bf16[128,512]{1,0:T(8,128)(2,1)S(1)} %collective-permute-done.1.kv_got_ref), channel_id=1, source_target_pairs={{0,8},{4,12},{8,16},{12,20},{16,24},{20,28},{24,4},{28,0},{1,9},{5... | collective-permute-start | bytes 393224 | tf_op jit(solution)/shard_map/ppermute | solution.py:329
  13.2 23.5 %copy-start.1 = (f32[1024]{0:T(1024)S(1)}, f32[1024]{0:T(1024)}, u32[]{:S(2)}) copy-start(f32[1024]{0:T(1024)} %param.12) | copy-start | bytes 12292
  13.2 23.5 %collective-permute-start.4 = (bf16[256,1024]{1,0:T(8,128)(2,1)S(1)}, bf16[256,1024]{1,0:T(8,128)(2,1)S(1)}, u32[]{:S(2)}, u32[]{:S(2)}) collective-permute-start(bf16[256,1024]{1,0:T(8,128)(2,1)S(1)} %get-tuple-element.31), channel_id=1, source_target_pairs={{0,16},{4,0},{8,20},{12,4},{16,24},{20,8},{24,28},{28,12},{1,17},{... | collective-permute-start | bytes 1572872 | tf_op jit(solution)/shard_map/ppermute | solution.py:357
  15.6 12.3 %collective-permute-start.5 = (f32[16,128]{1,0:T(8,128)S(1)}, f32[16,128]{1,0:T(8,128)S(1)}, u32[]{:S(2)}, u32[]{:S(2)}) collective-permute-start(f32[16,128]{1,0:T(8,128)S(1)} %get-tuple-element.32), channel_id=1, source_target_pairs={{0,16},{4,0},{8,20},{12,4},{16,24},{20,8},{24,28},{28,12},{1,17},{... | collective-permute-start | bytes 24584 | tf_op jit(solution)/shard_map/ppermute | solution.py:356
  27.9 3.7 %collective-permute-start.6 = (f32[16,128]{1,0:T(8,128)S(1)}, f32[16,128]{1,0:T(8,128)S(1)}, u32[]{:S(2)}, u32[]{:S(2)}) collective-permute-start(f32[16,128]{1,0:T(8,128)S(1)} %collective-permute-done.5.a_ref), channel_id=1, source_target_pairs={{0,1},{1,0},{2,3},{3,2},{4,5},{5,4},{6,7},{7,6},{8,9},{9,8},{10,11... | collective-permute-start | bytes 24584 | tf_op jit(solution)/shard_map/ppermute | solution.py:359
  31.6 5.0 %collective-permute-start.7 = (f32[16,128]{1,0:T(8,128)S(1)}, f32[16,128]{1,0:T(8,128)S(1)}, u32[]{:S(2)}, u32[]{:S(2)}) collective-permute-start(f32[16,128]{1,0:T(8,128)S(1)} %shard_map.93.a_ref), channel_id=1, source_target_pairs={{0,2},{1,3},{2,0},{3,1},{4,6},{5,7},{6,4},{7,5},{8,10},{9,11},{10,... | collective-permute-start | bytes 24584 | tf_op jit(solution)/shard_map/ppermute | solution.py:359
  38.3 1.4 %collective-permute-start.8 = (bf16[128,512]{1,0:T(8,128)(2,1)S(1)}, bf16[128,512]{1,0:T(8,128)(2,1)S(1)}, u32[]{:S(2)}, u32[]{:S(2)}) collective-permute-start(bf16[128,512]{1,0:T(8,128)(2,1)S(1)} %get-tuple-element.39), channel_id=1, source_target_pairs={{0,4},{4,0},{8,12},{12,8},{16,20},{20,16},{24,28},{28,24},{1,5},{5... | collective-permute-start | bytes 393224 | tf_op jit(solution)/shard_map/ppermute | solution.py:316
  38.4 1.3 %collective-permute-start.9 = (f32[1,1024]{1,0:T(1,128)S(1)}, f32[1,1024]{1,0:T(1,128)S(1)}, u32[]{:S(2)}, u32[]{:S(2)}) collective-permute-start(f32[1,1024]{1,0:T(1,128)S(1)} %get-tuple-element.40.tot_ref), channel_id=1, source_target_pairs={{0,4},{4,0},{8,12},{12,8},{16,20},{20,16},{24,28},{28,24},{1,5},{5... | collective-permute-start | bytes 12296 | tf_op jit(solution)/shard_map/ppermute | solution.py:316
  39.9 5.8 %collective-permute-start.10 = (bf16[128,512]{1,0:T(8,128)(2,1)S(1)}, bf16[128,512]{1,0:T(8,128)(2,1)S(1)}, u32[]{:S(2)}, u32[]{:S(2)}) collective-permute-start(bf16[128,512]{1,0:T(8,128)(2,1)S(1)} %get-tuple-element.42), channel_id=1, source_target_pairs={{0,8},{4,12},{8,0},{12,4},{16,24},{20,28},{24,16},{28,20},{1,9},{5... | collective-permute-start | bytes 393224 | tf_op jit(solution)/shard_map/ppermute | solution.py:316
  41.3 4.4 %collective-permute-start.11 = (f32[1,512]{1,0:T(1,128)S(1)}, f32[1,512]{1,0:T(1,128)S(1)}, u32[]{:S(2)}, u32[]{:S(2)}) collective-permute-start(f32[1,512]{1,0:T(1,128)S(1)} %shard_map.99.mine_ref), channel_id=1, source_target_pairs={{0,8},{4,12},{8,0},{12,4},{16,24},{20,28},{24,16},{28,20},{1,9},{5... | collective-permute-start | bytes 6152 | tf_op jit(solution)/shard_map/ppermute | solution.py:316
  45.8 5.6 %collective-permute-start.12 = (bf16[128,512]{1,0:T(8,128)(2,1)S(1)}, bf16[128,512]{1,0:T(8,128)(2,1)S(1)}, u32[]{:S(2)}, u32[]{:S(2)}) collective-permute-start(bf16[128,512]{1,0:T(8,128)(2,1)S(1)} %get-tuple-element.43), channel_id=1, source_target_pairs={{0,16},{4,20},{8,24},{12,28},{16,0},{20,4},{24,8},{28,12},{1,17},{... | collective-permute-start | bytes 393224 | tf_op jit(solution)/shard_map/ppermute | solution.py:316
  51.4 1.5 %copy-start = (bf16[256,128]{1,0:T(8,128)(2,1)S(1)}, bf16[256,128]{1,0:T(8,128)(2,1)}, u32[]{:S(2)}) copy-start(bf16[256,128]{1,0:T(8,128)(2,1)} %c_ref.1) | copy-start | bytes 196612
  51.5 1.4 %collective-permute-start.13 = (bf16[128,512]{1,0:T(8,128)(2,1)S(1)}, bf16[128,512]{1,0:T(8,128)(2,1)S(1)}, u32[]{:S(2)}, u32[]{:S(2)}) collective-permute-start(bf16[128,512]{1,0:T(8,128)(2,1)S(1)} %get-tuple-element.48), channel_id=1, source_target_pairs={{0,4},{4,0},{8,12},{12,8},{16,20},{20,16},{24,28},{28,24},{1,5},{5... | collective-permute-start | bytes 393224 | tf_op jit(solution)/shard_map/ppermute | solution.py:316

commit v5 on v4

--- a/solution.py
+++ b/solution.py
@@ -264,40 +264,61 @@
     low_ref[...] = total.astype(BF16)
 
 
-def arrive(bit, theirs_ref, decay_ref, entered):
+def stage_kernel(bit, first, total_ref, theirs_ref, mine_ref, decay_ref, *refs):
     upper = (lax.axis_index("seq") >> bit) % 2 == 1
-    theirs = theirs_ref[...].astype(F32)
-    enter, carried = (None, None) if entered is None else (entered[0][...], entered[1][...])
-    step = theirs if carried is None else carried * theirs
-    step = jnp.where(upper, step, 0.0)
-    enter = step if enter is None else enter + step
-    if decay_ref is None:
-        return upper, theirs, enter, None
-    ahead = decay_ref[...] if carried is None else carried * decay_ref[...]
-    stay = jnp.ones_like(ahead) if carried is None else carried
-    return upper, theirs, enter, jnp.where(upper, ahead, stay)
-
-
-def stage_kernel(bit, first, total_ref, theirs_ref, mine_ref, decay_ref, *refs):
-    entered, outs = (None, refs) if first else (refs[:2], refs[2:])
-    enter_ref, carried_ref, low_ref = outs[:3]
-    upper, theirs, enter, carried = arrive(bit, theirs_ref, decay_ref, entered)
-    enter_ref[...] = enter
-    carried_ref[...] = carried
-    total = total_ref[...]
-    total = jnp.where(upper, mine_ref[...] * theirs + total, decay_ref[...] * total + theirs)
+    enter_ref, carried_ref, low_ref, next_ref = refs[-4:]
+    theirs, decay, total = theirs_ref[...].astype(F32), decay_ref[...], total_ref[...]
+    if first:
+        enter_ref[...] = jnp.where(upper, theirs, 0.0)
+        carried_ref[...] = jnp.where(upper, decay, 1.0)
+    else:
+        carried = refs[1][...]
+        enter_ref[...] = refs[0][...] + jnp.where(upper, carried * theirs, 0.0)
+        carried_ref[...] = jnp.where(upper, carried * decay, carried)
+    total = jnp.where(upper, mine_ref[...] * theirs + total, decay * total + theirs)
     low_ref[...] = total.astype(BF16)
-    if len(outs) == 4:
-        outs[3][...] = total
-
-
-def last_kernel(bit, theirs_ref, early_ref, tot_ref, core_ref, *refs):
+    next_ref[...] = total
+
+
+def middle_kernel(shift, total_ref, first_ref, mine_ref, near_ref, low_ref):
+    me = lax.axis_index("seq")
+    quarter, late = me >> shift, me % 2 == 1
+    upper = quarter % 2 == 1
+    mine, near = mine_ref[...], near_ref[...]
+    one, zero = jnp.ones_like(mine), jnp.zeros_like(mine)
+    theirs = jnp.where(
+        late,
+        jnp.where(upper, one, jnp.where(quarter == 2, mine * near, zero)),
+        jnp.where(upper, mine, one),
+    )
+    own = jnp.where(late, jnp.where(upper, zero, one), jnp.where(upper, one, near))
+    low_ref[...] = (theirs * first_ref[...].astype(F32) + own * total_ref[...]).astype(BF16)
+
+
+def last_kernel(
+    shift, first_ref, second_ref, near_ref, early_ref, tot_ref, core_ref, *refs
+):
     own_ref, give_ref = refs[-2:]
-    mine = lax.axis_index("seq") % 2
-    late = mine == 1
-    enter = arrive(bit, theirs_ref, None, refs[:-2] or None)[2]
-    first = jnp.where(late, half_of(core_ref, mine), half_of(tot_ref, mine))
-    after = first * enter + early_ref[...]
+    me = lax.axis_index("seq")
+    side = me % 2
+    quarter, late = me >> shift, side == 1
+    near = near_ref[...]
+    one, zero = jnp.ones_like(near), jnp.zeros_like(near)
+    a = jnp.where(
+        late,
+        jnp.where(quarter >= 2, near, zero),
+        jnp.where(quarter % 2 == 1, one, zero),
+    )
+    b = jnp.where(
+        late,
+        jnp.where(quarter >= 1, one, zero),
+        jnp.where(quarter == 3, near, jnp.where(quarter == 2, one, zero)),
+    )
+    enter = a * first_ref[...].astype(F32) + b * second_ref[...].astype(F32)
+    if len(refs) == 4:
+        enter = refs[0][...] + refs[1][...] * enter
+    ahead = jnp.where(late, half_of(core_ref, side), half_of(tot_ref, side))
+    after = ahead * enter + early_ref[...]
     own_ref[...] = jnp.where(late, after, enter).astype(BF16)
     give_ref[...] = jnp.where(late, enter, after).astype(BF16)
 
@@ -359,11 +380,17 @@
         other = lax.ppermute(sums, "head", [(i, i ^ (1 << bit)) for i in range(head_count)])
         (sums,) = call(add_kernel, [((16, blk), F32)], (sums, other))
     decays = []
-    running = [chip]
-    for bit in range(1, bits - 1):
-        decays.append(swap(running[-1], bit))
-        if bit < bits - 2:
-            running += call(times_kernel, [((1, half), F32)], (running[-1], decays[-1]))
+    running = chip
+    for bit in range(1, bits - 2):
+        theirs = swap(running, bit)
+        decays.append((running, theirs))
+        (running,) = call(times_kernel, [((1, half), F32)], (running, theirs))
+    inner, outer = bits - 2, bits - 1
+    near = lax.ppermute(
+        running,
+        "seq",
+        [(i, (i + (1 << inner)) % seq_count if i % 2 else i ^ (1 << inner)) for i in every],
+    )
 
     x, keep, send = call(
         home_kernel,
@@ -379,19 +406,25 @@
         chip_kernel, [state, state, ((STATE, half), BF16)], (keep, got, tot, core)
     )
     entered = ()
-    for bit in range(1, bits):
+    for bit in range(1, bits - 2):
         theirs = swap(low, bit)
-        if bit < bits - 1:
-            outs = call(
-                functools.partial(stage_kernel, bit, bit == 1),
-                [state, row, ((STATE, half), BF16)] + [state] * (bit < bits - 2),
-                (total, theirs, running[bit - 1], decays[bit - 1], *entered),
-            )
-            entered, low, total = outs[:2], outs[2], outs[-1]
+        *entered, low, total = call(
+            functools.partial(stage_kernel, bit, bit == 1),
+            [state, row, ((STATE, half), BF16), state],
+            (total, theirs, *decays[bit - 1], *entered),
+        )
+    by_core = [[(i, i ^ (1 << (outer if i % 2 == turn else inner))) for i in every] for turn in (1, 0)]
+    first = lax.ppermute(low, "seq", by_core[0])
+    (low,) = call(
+        functools.partial(middle_kernel, inner),
+        [((STATE, half), BF16)],
+        (total, first, running, near),
+    )
+    second = lax.ppermute(low, "seq", by_core[1])
     own, give = call(
-        functools.partial(last_kernel, bits - 1),
+        functools.partial(last_kernel, inner),
         [((STATE, half), BF16)] * 2,
-        (theirs, early, tot, core, *entered),
+        (first, second, near, early, tot, core, *entered),
     )
     other = swap(give, 0)
     (out,) = call(

time: 54.2 us -> 53.3 us (0.983)
  waiting for transfers between devices: 27.4 us -> 26.4 us
    ppermute x8 -> x5, waiting for transfers between devices: 8.35 us -> 1.48 us  [swap(): return lax.ppermute(block, 'seq', [(i, i ^ 1 << bit) for i in every])]
    ppermute x0 -> x3, waiting for transfers between devices: none -> 5.93 us  [the longest x1 2.98 us: layer(): lax.ppermute(running, 'seq', [(i, (i + (1 << inner)) % seq_count if i % 2...]
    ppermute x0 -> x3, starting transfers between devices: none -> 4.61 us  [the longest x1 2.52 us: layer(): second = lax.ppermute(low, 'seq', by_core[1])]
    ppermute x8 -> x5, starting transfers between devices: 5.76 us -> 1.15 us  [swap(): return lax.ppermute(block, 'seq', [(i, i ^ 1 << bit) for i in every])]
where the time goes in v5:
time: 53.3 us; the launch traced here: 53.1 us
  waiting for transfers between devices  26.4 us (50%)
  starting transfers between devices  17.5 us (33%)
  Pallas kernels  9.11 us (17%)
    ppermute x1, waiting for transfers between devices, layer(): sums = lax.ppermute(sums, 'seq', to_home)  11.7 us
    pallas_call x12, Pallas kernels, call(): pl.pallas_call(kernel, out_shape=[jax.ShapeDtypeStruct(s, d) for s, d in...  9.11 us
    ppermute x2, starting transfers between devices, layer(): lax.ppermute(sums, 'head', [(i, i ^ 1 << bit) for i in range(head_count)])  4.23 us
    ppermute x1, waiting for transfers between devices, layer(): lax.ppermute(running, 'seq', [(i, (i + (1 << inner)) % seq_count if i % 2...  2.98 us
    ppermute x1, starting transfers between devices, layer(): old_keep = lax.ppermute(kv_keep, 'seq', onward)  2.97 us
    ppermute x1, waiting for transfers between devices, layer(): second = lax.ppermute(low, 'seq', by_core[1])  2.95 us
    ppermute x1, waiting for transfers between devices, layer(): old_got = lax.ppermute(kv_got, 'seq', onward)  2.81 us
    ppermute x1, starting transfers between devices, layer(): second = lax.ppermute(low, 'seq', by_core[1])  2.52 us
  transfers between devices with their start and end apart: 14, of which 8 were waited for; matrix products, arithmetic and copies ran while one was open for 0% of the time, Pallas kernels for 6%

profile of v5, /device:TPU:0, one launch (start us, length us, event | category | flops | bytes accessed | tf_op | source)
XLA Modules:
  0.0 53.1 jit_solution(8214035522953231341)
XLA Ops:
  0.0 1.2 %shard_map.91 = (bf16[128,512]{1,0:T(8,128)(2,1)S(1)}, bf16[128,1024]{1,0:T(8,128)(2,1)S(1)}, bf16[128,512]{1,0:T(8,128)(2,1)S(1)}, bf16[128,1024]{1,0:T(8,128)(2,1)S(1)}) custom-call(bf16[2,128,1024]{2,1,0:T(8,128)(2,1)} %q_ref.1, bf16[2,128,256]{2,1,0:T(8,128)(2,1)} %k_ref.1, bf16[2,128,256]{2,1,0:T(8,128)(2,1)} %v_ref.1), custom_call_target="tpu_custom_call" | custom-call | flops 1 | bytes 1048576 | tf_op jit(solution)/shard_map/pallas_call | solution.py:35
  1.7 3.0 %collective-permute-start.2 = (bf16[128,512]{1,0:T(8,128)(2,1)S(1)}, bf16[128,512]{1,0:T(8,128)(2,1)S(1)}, u32[]{:S(2)}, u32[]{:S(2)}) collective-permute-start(bf16[128,512]{1,0:T(8,128)(2,1)S(1)} %get-tuple-element.26.kv_keep_ref), channel_id=1, source_target_pairs={{0,8},{4,12},{8,16},{12,20},{16,24},{20,28},{24,4},{28,0},{1,9},{5... | collective-permute-start | bytes 393224 | tf_op jit(solution)/shard_map/ppermute | solution.py:349
  4.6 1.5 %collective-permute-start.3 = (bf16[128,512]{1,0:T(8,128)(2,1)S(1)}, bf16[128,512]{1,0:T(8,128)(2,1)S(1)}, u32[]{:S(2)}, u32[]{:S(2)}) collective-permute-start(bf16[128,512]{1,0:T(8,128)(2,1)S(1)} %collective-permute-done.1.kv_got_ref), channel_id=1, source_target_pairs={{0,8},{4,12},{8,16},{12,20},{16,24},{20,28},{24,4},{28,0},{1,9},{5... | collective-permute-start | bytes 393224 | tf_op jit(solution)/shard_map/ppermute | solution.py:350
  6.1 2.4 %collective-permute-done.2.old_keep_ref = bf16[128,512]{1,0:T(8,128)(2,1)S(1)} collective-permute-done((bf16[128,512]{1,0:T(8,128)(2,1)S(1)}, bf16[128,512]{1,0:T(8,128)(2,1)S(1)}, u32[]{:S(2)}, u32[]{:S(2)}) %collective-permute-start.2) | collective-permute-done | bytes 131104 | tf_op jit(solution)/shard_map/ppermute | solution.py:349
  8.6 2.8 %collective-permute-done.3.old_got_ref = bf16[128,512]{1,0:T(8,128)(2,1)S(1)} collective-permute-done((bf16[128,512]{1,0:T(8,128)(2,1)S(1)}, bf16[128,512]{1,0:T(8,128)(2,1)S(1)}, u32[]{:S(2)}, u32[]{:S(2)}) %collective-permute-start.3) | collective-permute-done | bytes 131104 | tf_op jit(solution)/shard_map/ppermute | solution.py:350
  11.4 1.8 %shard_map.92 = (bf16[256,1024]{1,0:T(8,128)(2,1)S(1)}, f32[16,128]{1,0:T(8,128)S(1)}) custom-call(bf16[128,1024]{1,0:T(8,128)(2,1)S(1)} %get-tuple-element.24.q_keep_ref, bf16[128,1024]{1,0:T(8,128)(2,1)S(1)} %collective-permute-done.q_got_ref, bf16[128,512]{1,0:T(8,128)(2,1)S(1)} %get-tuple-element.26.kv_keep_ref, ...), custom_call_target="tpu_custom_call" | custom-call | flops 536870912 | bytes 1048576 | tf_op jit(solution)/shard_map/pallas_call | solution.py:35
  13.2 2.5 %collective-permute-start.4 = (bf16[256,1024]{1,0:T(8,128)(2,1)S(1)}, bf16[256,1024]{1,0:T(8,128)(2,1)S(1)}, u32[]{:S(2)}, u32[]{:S(2)}) collective-permute-start(bf16[256,1024]{1,0:T(8,128)(2,1)S(1)} %get-tuple-element.28), channel_id=1, source_target_pairs={{0,16},{4,0},{8,20},{12,4},{16,24},{20,8},{24,28},{28,12},{1,17},{... | collective-permute-start | bytes 1572872 | tf_op jit(solution)/shard_map/ppermute | solution.py:378
  15.6 0.6 %collective-permute-start.5 = (f32[16,128]{1,0:T(8,128)S(1)}, f32[16,128]{1,0:T(8,128)S(1)}, u32[]{:S(2)}, u32[]{:S(2)}) collective-permute-start(f32[16,128]{1,0:T(8,128)S(1)} %get-tuple-element.29), channel_id=1, source_target_pairs={{0,16},{4,0},{8,20},{12,4},{16,24},{20,8},{24,28},{28,12},{1,17},{... | collective-permute-start | bytes 24584 | tf_op jit(solution)/shard_map/ppermute | solution.py:377
  16.2 11.7 %collective-permute-done.5.a_ref = f32[16,128]{1,0:T(8,128)S(1)} collective-permute-done((f32[16,128]{1,0:T(8,128)S(1)}, f32[16,128]{1,0:T(8,128)S(1)}, u32[]{:S(2)}, u32[]{:S(2)}) %collective-permute-start.5) | collective-permute-done | bytes 8224 | tf_op jit(solution)/shard_map/ppermute | solution.py:377
  27.9 1.6 %collective-permute-start.6 = (f32[16,128]{1,0:T(8,128)S(1)}, f32[16,128]{1,0:T(8,128)S(1)}, u32[]{:S(2)}, u32[]{:S(2)}) collective-permute-start(f32[16,128]{1,0:T(8,128)S(1)} %collective-permute-done.5.a_ref), channel_id=1, source_target_pairs={{0,1},{1,0},{2,3},{3,2},{4,5},{5,4},{6,7},{7,6},{8,9},{9,8},{10,11... | collective-permute-start | bytes 24584 | tf_op jit(solution)/shard_map/ppermute | solution.py:380
  29.6 2.0 %collective-permute-done.6.b_ref = f32[16,128]{1,0:T(8,128)S(1)} collective-permute-done((f32[16,128]{1,0:T(8,128)S(1)}, f32[16,128]{1,0:T(8,128)S(1)}, u32[]{:S(2)}, u32[]{:S(2)}) %collective-permute-start.6) | collective-permute-done | bytes 8224 | tf_op jit(solution)/shard_map/ppermute | solution.py:380
  31.6 2.6 %collective-permute-start.7 = (f32[16,128]{1,0:T(8,128)S(1)}, f32[16,128]{1,0:T(8,128)S(1)}, u32[]{:S(2)}, u32[]{:S(2)}) collective-permute-start(f32[16,128]{1,0:T(8,128)S(1)} %shard_map.93.a_ref), channel_id=1, source_target_pairs={{0,2},{1,3},{2,0},{3,1},{4,6},{5,7},{6,4},{7,5},{8,10},{9,11},{10,... | collective-permute-start | bytes 24584 | tf_op jit(solution)/shard_map/ppermute | solution.py:380
  34.2 2.4 %shard_map.95 = (bf16[8,256,512]{2,1,0:T(8,128)(2,1)S(1)}, bf16[8,128,512]{2,1,0:T(8,128)(2,1)S(1)}, f32[256,1024]{1,0:T(8,128)S(1)}, f32[1,1024]{1,0:T(1,128)S(1)}, f32[1,1024]{1,0:T(1,128)S(1)}) custom-call(f32[16,256]{1,0:T(8,128)} %refs_0_.1, f32[16,256]{1,0:T(8,128)} %refs_1_.1, bf16[256,128]{1,0:T(8,128)(2,1)} %refs_2_.1, bf16[256,128]{1,0:T(8,128)(2,1)} %c_ref.1, ...), custom_call_target="tpu_custom_call" | custom-call | flops 1073741824 | bytes 1048576 | tf_op jit(solution)/shard_map/pallas_call | solution.py:35
  36.7 1.7 %shard_map.96 = (bf16[256,1024]{1,0:T(8,128)(2,1)S(1)}, f32[128,512]{1,0:T(8,128)S(1)}, bf16[128,512]{1,0:T(8,128)(2,1)S(1)}) custom-call(bf16[256,1024]{1,0:T(8,128)(2,1)S(1)} %collective-permute-done.4.rows_ref, f32[16,128]{1,0:T(8,128)S(1)} %shard_map.94.sums_ref, f32[1,1024]{1,0:T(1,128)S(1)} %bitcast.1, bf16[8,128,512]{2,1,0:T(8,128)(2,1)S(1)} %get-tuple-element.30.bw_ref), custom_call_target="tpu_custom_call" | custom-call | flops 268435456 | bytes 1048576 | tf_op jit(solution)/shard_map/pallas_call | solution.py:35
  38.4 0.5 collective-permute-start.9
  38.9 0.8 %collective-permute-done.9.core_ref = f32[1,1024]{1,0:T(1,128)S(1)} collective-permute-done((f32[1,1024]{1,0:T(1,128)S(1)}, f32[1,1024]{1,0:T(1,128)S(1)}, u32[]{:S(2)}, u32[]{:S(2)}) %collective-permute-start.9) | collective-permute-done | bytes 4128 | tf_op jit(solution)/shard_map/ppermute | solution.py:337
  39.9 1.5 %collective-permute-start.10 = (bf16[128,512]{1,0:T(8,128)(2,1)S(1)}, bf16[128,512]{1,0:T(8,128)(2,1)S(1)}, u32[]{:S(2)}, u32[]{:S(2)}) collective-permute-start(bf16[128,512]{1,0:T(8,128)(2,1)S(1)} %get-tuple-element.38), channel_id=1, source_target_pairs={{0,8},{4,20},{8,0},{12,28},{16,24},{20,4},{24,16},{28,12},{1,9},{5... | collective-permute-start | bytes 393224 | tf_op jit(solution)/shard_map/ppermute | solution.py:417
  41.3 0.6 %collective-permute-start.11 = (f32[1,512]{1,0:T(1,128)S(1)}, f32[1,512]{1,0:T(1,128)S(1)}, u32[]{:S(2)}, u32[]{:S(2)}) collective-permute-start(f32[1,512]{1,0:T(1,128)S(1)} %shard_map.99.mine_ref), channel_id=1, source_target_pairs={{0,8},{4,12},{8,0},{12,20},{16,24},{20,28},{24,16},{28,4},{1,9},{5... | collective-permute-start | bytes 6152 | tf_op jit(solution)/shard_map/ppermute | solution.py:389
  42.0 3.0 %collective-permute-done.11.near_ref = f32[1,512]{1,0:T(1,128)S(1)} collective-permute-done((f32[1,512]{1,0:T(1,128)S(1)}, f32[1,512]{1,0:T(1,128)S(1)}, u32[]{:S(2)}, u32[]{:S(2)}) %collective-permute-start.11) | collective-permute-done | bytes 2080 | tf_op jit(solution)/shard_map/ppermute | solution.py:389
  45.0 2.5 %collective-permute-start.12 = (bf16[128,512]{1,0:T(8,128)(2,1)S(1)}, bf16[128,512]{1,0:T(8,128)(2,1)S(1)}, u32[]{:S(2)}, u32[]{:S(2)}) collective-permute-start(bf16[128,512]{1,0:T(8,128)(2,1)S(1)} %shard_map.100), channel_id=1, source_target_pairs={{0,16},{4,12},{8,24},{12,4},{16,0},{20,28},{24,8},{28,20},{1,17},{... | collective-permute-start | bytes 393224 | tf_op jit(solution)/shard_map/ppermute | solution.py:423
  47.5 2.9 %collective-permute-done.12.second_ref = bf16[128,512]{1,0:T(8,128)(2,1)S(1)} collective-permute-done((bf16[128,512]{1,0:T(8,128)(2,1)S(1)}, bf16[128,512]{1,0:T(8,128)(2,1)S(1)}, u32[]{:S(2)}, u32[]{:S(2)}) %collective-permute-start.12) | collective-permute-done | bytes 131104 | tf_op jit(solution)/shard_map/ppermute | solution.py:423
  50.7 0.7 %shard_map.97.local_ref = f32[256,1024]{1,0:T(8,128)S(1)} custom-call(bf16[256,1024]{1,0:T(8,128)(2,1)S(1)} %get-tuple-element.31.x_ref, bf16[8,256,512]{2,1,0:T(8,128)(2,1)S(1)} %get-tuple-element.32.mix_ref, f32[1,1024]{1,0:T(1,128)S(1)} %get-tuple-element.33.skip_ref), custom_call_target="tpu_custom_call" | custom-call | flops 536870912 | bytes 1048576 | tf_op jit(solution)/shard_map/pallas_call | solution.py:35
  51.4 0.6 %collective-permute-done.13.other_ref = bf16[128,512]{1,0:T(8,128)(2,1)S(1)} collective-permute-done((bf16[128,512]{1,0:T(8,128)(2,1)S(1)}, bf16[128,512]{1,0:T(8,128)(2,1)S(1)}, u32[]{:S(2)}, u32[]{:S(2)}) %collective-permute-start.13) | collective-permute-done | bytes 131104 | tf_op jit(solution)/shard_map/ppermute | solution.py:337
  52.0 1.1 %shard_map.102 = bf16[256,1024]{1,0:T(8,128)(2,1)} custom-call(f32[256,1024]{1,0:T(8,128)S(1)} %shard_map.97.local_ref, f32[256,1024]{1,0:T(8,128)S(1)} %get-tuple-element.34.scale_ref, bf16[256,128]{1,0:T(8,128)(2,1)S(1)} %copy-done, bf16[128,512]{1,0:T(8,128)(2,1)S(1)} %get-tuple-element.41.own_ref, bf16[128,512]{1,0:T(8,128)(2,1)S(1)} %collective-permute-done.13.other_ref), custom_call_target="tpu_custom_call" | custom-call | flops 268435456 | bytes 1048576 | tf_op jit(solution)/shard_map/pallas_call | solution.py:35
  (20 shorter events, 1.0 us)
Async XLA Ops:
  1.2 3.5 %collective-permute-start.1 = (bf16[128,512]{1,0:T(8,128)(2,1)S(1)}, bf16[128,512]{1,0:T(8,128)(2,1)S(1)}, u32[]{:S(2)}, u32[]{:S(2)}) collective-permute-start(bf16[128,512]{1,0:T(8,128)(2,1)S(1)} %get-tuple-element.27), channel_id=1, source_target_pairs={{0,4},{4,0},{8,12},{12,8},{16,20},{20,16},{24,28},{28,24},{1,5},{5... | collective-permute-start | bytes 393224 | tf_op jit(solution)/shard_map/ppermute | solution.py:337
  1.7 9.7 %collective-permute-start = (bf16[128,1024]{1,0:T(8,128)(2,1)S(1)}, bf16[128,1024]{1,0:T(8,128)(2,1)S(1)}, u32[]{:S(2)}, u32[]{:S(2)}) collective-permute-start(bf16[128,1024]{1,0:T(8,128)(2,1)S(1)} %get-tuple-element.25), channel_id=1, source_target_pairs={{0,4},{4,0},{8,12},{12,8},{16,20},{20,16},{24,28},{28,24},{1,5},{5... | collective-permute-start | bytes 786440 | tf_op jit(solution)/shard_map/ppermute | solution.py:337
  1.7 6.9 %collective-permute-start.2 = (bf16[128,512]{1,0:T(8,128)(2,1)S(1)}, bf16[128,512]{1,0:T(8,128)(2,1)S(1)}, u32[]{:S(2)}, u32[]{:S(2)}) collective-permute-start(bf16[128,512]{1,0:T(8,128)(2,1)S(1)} %get-tuple-element.26.kv_keep_ref), channel_id=1, source_target_pairs={{0,8},{4,12},{8,16},{12,20},{16,24},{20,28},{24,4},{28,0},{1,9},{5... | collective-permute-start | bytes 393224 | tf_op jit(solution)/shard_map/ppermute | solution.py:349
  4.6 6.7 %collective-permute-start.3 = (bf16[128,512]{1,0:T(8,128)(2,1)S(1)}, bf16[128,512]{1,0:T(8,128)(2,1)S(1)}, u32[]{:S(2)}, u32[]{:S(2)}) collective-permute-start(bf16[128,512]{1,0:T(8,128)(2,1)S(1)} %collective-permute-done.1.kv_got_ref), channel_id=1, source_target_pairs={{0,8},{4,12},{8,16},{12,20},{16,24},{20,28},{24,4},{28,0},{1,9},{5... | collective-permute-start | bytes 393224 | tf_op jit(solution)/shard_map/ppermute | solution.py:350
  13.2 23.5 %copy-start.1 = (f32[1024]{0:T(1024)S(1)}, f32[1024]{0:T(1024)}, u32[]{:S(2)}) copy-start(f32[1024]{0:T(1024)} %param.12) | copy-start | bytes 12292
  13.2 23.5 %collective-permute-start.4 = (bf16[256,1024]{1,0:T(8,128)(2,1)S(1)}, bf16[256,1024]{1,0:T(8,128)(2,1)S(1)}, u32[]{:S(2)}, u32[]{:S(2)}) collective-permute-start(bf16[256,1024]{1,0:T(8,128)(2,1)S(1)} %get-tuple-element.28), channel_id=1, source_target_pairs={{0,16},{4,0},{8,20},{12,4},{16,24},{20,8},{24,28},{28,12},{1,17},{... | collective-permute-start | bytes 1572872 | tf_op jit(solution)/shard_map/ppermute | solution.py:378
  15.6 12.3 %collective-permute-start.5 = (f32[16,128]{1,0:T(8,128)S(1)}, f32[16,128]{1,0:T(8,128)S(1)}, u32[]{:S(2)}, u32[]{:S(2)}) collective-permute-start(f32[16,128]{1,0:T(8,128)S(1)} %get-tuple-element.29), channel_id=1, source_target_pairs={{0,16},{4,0},{8,20},{12,4},{16,24},{20,8},{24,28},{28,12},{1,17},{... | collective-permute-start | bytes 24584 | tf_op jit(solution)/shard_map/ppermute | solution.py:377
  27.9 3.7 %collective-permute-start.6 = (f32[16,128]{1,0:T(8,128)S(1)}, f32[16,128]{1,0:T(8,128)S(1)}, u32[]{:S(2)}, u32[]{:S(2)}) collective-permute-start(f32[16,128]{1,0:T(8,128)S(1)} %collective-permute-done.5.a_ref), channel_id=1, source_target_pairs={{0,1},{1,0},{2,3},{3,2},{4,5},{5,4},{6,7},{7,6},{8,9},{9,8},{10,11... | collective-permute-start | bytes 24584 | tf_op jit(solution)/shard_map/ppermute | solution.py:380
  31.6 5.0 %collective-permute-start.7 = (f32[16,128]{1,0:T(8,128)S(1)}, f32[16,128]{1,0:T(8,128)S(1)}, u32[]{:S(2)}, u32[]{:S(2)}) collective-permute-start(f32[16,128]{1,0:T(8,128)S(1)} %shard_map.93.a_ref), channel_id=1, source_target_pairs={{0,2},{1,3},{2,0},{3,1},{4,6},{5,7},{6,4},{7,5},{8,10},{9,11},{10,... | collective-permute-start | bytes 24584 | tf_op jit(solution)/shard_map/ppermute | solution.py:380
  38.3 1.4 %collective-permute-start.8 = (bf16[128,512]{1,0:T(8,128)(2,1)S(1)}, bf16[128,512]{1,0:T(8,128)(2,1)S(1)}, u32[]{:S(2)}, u32[]{:S(2)}) collective-permute-start(bf16[128,512]{1,0:T(8,128)(2,1)S(1)} %get-tuple-element.36), channel_id=1, source_target_pairs={{0,4},{4,0},{8,12},{12,8},{16,20},{20,16},{24,28},{28,24},{1,5},{5... | collective-permute-start | bytes 393224 | tf_op jit(solution)/shard_map/ppermute | solution.py:337
  38.4 1.3 %collective-permute-start.9 = (f32[1,1024]{1,0:T(1,128)S(1)}, f32[1,1024]{1,0:T(1,128)S(1)}, u32[]{:S(2)}, u32[]{:S(2)}) collective-permute-start(f32[1,1024]{1,0:T(1,128)S(1)} %get-tuple-element.37.tot_ref), channel_id=1, source_target_pairs={{0,4},{4,0},{8,12},{12,8},{16,20},{20,16},{24,28},{28,24},{1,5},{5... | collective-permute-start | bytes 12296 | tf_op jit(solution)/shard_map/ppermute | solution.py:337
  39.9 5.1 %collective-permute-start.10 = (bf16[128,512]{1,0:T(8,128)(2,1)S(1)}, bf16[128,512]{1,0:T(8,128)(2,1)S(1)}, u32[]{:S(2)}, u32[]{:S(2)}) collective-permute-start(bf16[128,512]{1,0:T(8,128)(2,1)S(1)} %get-tuple-element.38), channel_id=1, source_target_pairs={{0,8},{4,20},{8,0},{12,28},{16,24},{20,4},{24,16},{28,12},{1,9},{5... | collective-permute-start | bytes 393224 | tf_op jit(solution)/shard_map/ppermute | solution.py:417
  41.3 3.6 %collective-permute-start.11 = (f32[1,512]{1,0:T(1,128)S(1)}, f32[1,512]{1,0:T(1,128)S(1)}, u32[]{:S(2)}, u32[]{:S(2)}) collective-permute-start(f32[1,512]{1,0:T(1,128)S(1)} %shard_map.99.mine_ref), channel_id=1, source_target_pairs={{0,8},{4,12},{8,0},{12,20},{16,24},{20,28},{24,16},{28,4},{1,9},{5... | collective-permute-start | bytes 6152 | tf_op jit(solution)/shard_map/ppermute | solution.py:389
  45.0 5.5 %collective-permute-start.12 = (bf16[128,512]{1,0:T(8,128)(2,1)S(1)}, bf16[128,512]{1,0:T(8,128)(2,1)S(1)}, u32[]{:S(2)}, u32[]{:S(2)}) collective-permute-start(bf16[128,512]{1,0:T(8,128)(2,1)S(1)} %shard_map.100), channel_id=1, source_target_pairs={{0,16},{4,12},{8,24},{12,4},{16,0},{20,28},{24,8},{28,20},{1,17},{... | collective-permute-start | bytes 393224 | tf_op jit(solution)/shard_map/ppermute | solution.py:423
  50.5 1.5 %copy-start = (bf16[256,128]{1,0:T(8,128)(2,1)S(1)}, bf16[256,128]{1,0:T(8,128)(2,1)}, u32[]{:S(2)}) copy-start(bf16[256,128]{1,0:T(8,128)(2,1)} %c_ref.1) | copy-start | bytes 196612
  50.6 1.4 %collective-permute-start.13 = (bf16[128,512]{1,0:T(8,128)(2,1)S(1)}, bf16[128,512]{1,0:T(8,128)(2,1)S(1)}, u32[]{:S(2)}, u32[]{:S(2)}) collective-permute-start(bf16[128,512]{1,0:T(8,128)(2,1)S(1)} %get-tuple-element.42), channel_id=1, source_target_pairs={{0,4},{4,0},{8,12},{12,8},{16,20},{20,16},{24,28},{28,24},{1,5},{5... | collective-permute-start | bytes 393224 | tf_op jit(solution)/shard_map/ppermute | solution.py:337

commit v6 on v4

v6 whole, which is shorter than its diff:
```python
import functools
import math

import jax
import jax.numpy as jnp
from jax import lax
from jax.experimental import pallas as pl
from jax.experimental.pallas import tpu as pltpu
from jax.sharding import PartitionSpec as P


HEADS = 32
HDIM = 128
SDIM = 64
STATE = 128
TAIL = 16

F32 = jnp.float32
BF16 = jnp.bfloat16
VMEM = pltpu.VMEM
GRANT = 12 << 20


def dot(a, b, contract=(1, 0), precision=None):
    return lax.dot_general(
        a,
        b,
        (((contract[0],), (contract[1],)), ((), ())),
        precision=precision,
        preferred_element_type=F32,
    )


def call(kernel, outs, args, flops=1, spaces=None):
    spaces = spaces or [VMEM] * len(args)
    return pl.pallas_call(
        kernel,
        out_shape=[jax.ShapeDtypeStruct(s, d) for s, d in outs],
        in_specs=[pl.BlockSpec(memory_space=m) for m in spaces],
        out_specs=[pl.BlockSpec(memory_space=VMEM)] * len(outs),
        compiler_params=pltpu.CompilerParams(vmem_limit_bytes=GRANT),
        cost_estimate=pl.CostEstimate(flops=flops, bytes_accessed=1 << 20, transcendentals=0),
    )(*[pltpu.with_memory_space_constraint(a, m) if m == pltpu.HBM else a for a, m in zip(args, spaces)])


def gather(copies, sems):
    started = [pltpu.make_async_copy(a, b, sems.at[i]) for i, (a, b) in enumerate(copies)]
    for copy in started:
        copy.start()
    for copy in started:
        copy.wait()


def part_kernel(kv_ref, k_ref, v_ref):
    width = k_ref.shape[1]
    k_ref[...] = kv_ref[:, :width]
    v_ref[...] = kv_ref[:, width:]


def pack_kv_kernel(k_ref, v_ref, keep_ref, send_ref):
    width = k_ref.shape[2]
    mine = lax.axis_index("seq") % 2
    copies = []
    for slot, out_ref in ((1 - mine, keep_ref), (mine, send_ref)):
        copies.append((k_ref.at[slot], out_ref.at[:, :width]))
        copies.append((v_ref.at[slot], out_ref.at[:, width:]))
    pl.run_scoped(functools.partial(gather, copies), pltpu.SemaphoreType.DMA((4,)))


def pack_q_kernel(q_ref, keep_ref, send_ref):
    mine = lax.axis_index("seq") % 2
    copies = [(q_ref.at[1 - mine], keep_ref), (q_ref.at[mine], send_ref)]
    pl.run_scoped(functools.partial(gather, copies), pltpu.SemaphoreType.DMA((2,)))


def prepare_kernel(*refs):
    def inner(sems, *inside):
        copies = [
            pltpu.make_async_copy(src, dst, sems.at[i])
            for i, (src, dst) in enumerate(zip(refs[:5], inside))
        ]
        for copy in copies:
            copy.start()
        for copy in copies:
            copy.wait()
        prepare(*inside, *refs[5:])

    pl.run_scoped(
        inner,
        pltpu.SemaphoreType.DMA((5,)),
        *[VMEM(r.shape, r.dtype) for r in refs[:4]],
        pltpu.SMEM(refs[4].shape, refs[4].dtype),
    )


def prepare(step_ref, log_ref, b_ref, c_ref, skip_ref, mix_ref, bw_ref, scale_ref, tot_ref, pass_ref):
    heads, toks = step_ref.shape
    half = toks // 2
    highest = lax.Precision.HIGHEST
    log = log_ref[...]
    step = step_ref[...]
    rows = lax.broadcasted_iota(jnp.int32, (toks, toks), 0)
    cols = lax.broadcasted_iota(jnp.int32, (toks, toks), 1)
    lower = (rows >= cols).astype(F32)
    cum = dot(log, lower, (1, 1), highest)
    cum_cols = dot(lower, log, (1, 1), highest)
    total = cum[:, toks - 1 :]
    weight = jnp.exp(total - cum) * step
    cross = dot(c_ref[...], b_ref[...], (1, 1))
    b_t = jnp.transpose(b_ref[...].astype(F32))
    causal = (
        lax.broadcasted_iota(jnp.int32, (half, half), 0)
        >= lax.broadcasted_iota(jnp.int32, (half, half), 1)
    )
    lanes = lax.broadcasted_iota(jnp.int32, (toks, HDIM), 1)
    for pair in range(heads // 2):
        for side in range(2):
            k = 2 * pair + side
            at = side * toks
            for r in range(2):
                for c in range(2):
                    dst = (pair, slice(r * half, (r + 1) * half), slice(at + c * half, at + (c + 1) * half))
                    if c > r:
                        mix_ref[dst] = jnp.zeros((half, half), BF16)
                        continue
                    rs, cs = slice(r * half, (r + 1) * half), slice(c * half, (c + 1) * half)
                    gap = cum_cols[rs, k : k + 1] - cum[k : k + 1, cs]
                    if r == c:
                        gap = jnp.where(causal, gap, -jnp.inf)
                    mix_ref[dst] = (jnp.exp(gap) * cross[rs, cs] * step[k : k + 1, cs]).astype(BF16)
            bw_ref[pair, :, at : at + toks] = (b_t * weight[k : k + 1, :]).astype(BF16)
        both = jnp.where(
            lanes < SDIM,
            cum_cols[:, 2 * pair : 2 * pair + 1],
            cum_cols[:, 2 * pair + 1 : 2 * pair + 2],
        )
        both = jnp.exp(both)
        scale_ref[:, pair * HDIM : (pair + 1) * HDIM] = both
        tot_ref[:, pair * HDIM : (pair + 1) * HDIM] = both[toks - 1 :, :]
        pass_ref[:, pair * HDIM : (pair + 1) * HDIM] = jnp.where(
            lanes[:1] < SDIM, skip_ref[2 * pair], skip_ref[2 * pair + 1]
        )


def pick(keep_ref, got_ref, swapped, column, got_column=None):
    keep, got = [
        ref[:, c * HDIM : (c + 1) * HDIM]
        for ref, c in ((keep_ref, column), (got_ref, column if got_column is None else got_column))
    ]
    return jnp.where(swapped, got, keep), jnp.where(swapped, keep, got)


def places():
    me = lax.axis_index("seq")
    late = me % 2 == 1
    return late, jnp.where(me < 2, me % 2 == 0, late), me != 1


def score_kernel(
    q_keep_ref, q_got_ref, kv_keep_ref, kv_got_ref, old_keep_ref, old_got_ref, weight_ref, scale_ref
):
    blk, feat = q_keep_ref.shape
    kv_local = kv_keep_ref.shape[1] // (2 * HDIM)
    group = feat // HDIM // kv_local
    late, old_late, has_old = places()
    rows = lax.broadcasted_iota(jnp.int32, (group * blk, blk), 0) % blk
    cols = lax.broadcasted_iota(jnp.int32, (group * blk, blk), 1)
    own_ok = cols <= rows
    far_ok = (cols > rows) & has_old
    near_ok = (cols >= 0) & has_old
    factor = math.log2(math.e) / math.sqrt(HDIM)
    for g in range(kv_local):
        keys = pick(old_keep_ref, old_got_ref, old_late, g) + pick(kv_keep_ref, kv_got_ref, late, g)
        heads = [pick(q_keep_ref, q_got_ref, late, g * group + i) for i in range(group)]
        for part in range(2):
            query = jnp.concatenate([h[part] for h in heads], 0)
            score = dot(query, jnp.concatenate(keys[part : part + 3], 0), (1, 1))
            near = score[:, blk : 2 * blk]
            if part == 0:
                near = jnp.where(near_ok, near, -jnp.inf)
            far = jnp.where(far_ok, score[:, :blk], -jnp.inf)
            score = jnp.concatenate([far, near, jnp.where(own_ok, score[:, 2 * blk :], -jnp.inf)], 1)
            peak = jnp.max(score, axis=1, keepdims=True)
            terms = jnp.exp2((score - peak) * factor)
            total = pl.reciprocal(jnp.sum(terms, axis=1, keepdims=True))
            weight_ref[2 * g + part] = terms.astype(BF16)
            scale_ref[2 * g + part] = jnp.broadcast_to(total, (group * blk, HDIM))


def value_kernel(
    weight_ref, scale_ref, kv_keep_ref, kv_got_ref, old_keep_ref, old_got_ref, out_ref, sums_ref
):
    blk = kv_keep_ref.shape[0]
    kv_local = kv_keep_ref.shape[1] // (2 * HDIM)
    group = out_ref.shape[1] // HDIM // kv_local
    late, old_late, _ = places()
    squares = [jnp.zeros((blk, 1), F32)] * 2
    for g in range(kv_local):
        c = kv_local + g
        vals = pick(old_keep_ref, old_got_ref, old_late, c, g) + pick(kv_keep_ref, kv_got_ref, late, c)
        for part in range(2):
            values = jnp.concatenate(vals[part : part + 3], 0)
            result = dot(weight_ref[2 * g + part], values) * scale_ref[2 * g + part]
            result = result.astype(BF16)
            wide = result.astype(F32)
            square = jnp.sum(wide * wide, axis=1, keepdims=True)
            for i in range(group):
                at = slice((g * group + i) * HDIM, (g * group + i + 1) * HDIM)
                out_ref[part * blk : (part + 1) * blk, at] = result[i * blk : (i + 1) * blk]
                squares[part] = squares[part] + square[i * blk : (i + 1) * blk]
    for part in range(2):
        turned = jnp.transpose(jnp.broadcast_to(squares[part], (blk, blk)))
        sums_ref[part * 8 : part * 8 + 8] = turned[:8]


def spread(x):
    lanes = lax.broadcasted_iota(jnp.int32, x.shape, 1)
    zero = jnp.zeros_like(x)
    return jnp.concatenate([jnp.where(lanes < SDIM, x, zero), jnp.where(lanes < SDIM, zero, x)], 0)


def pack_state(ref, state, decay, at=slice(None)):
    ref[:STATE, at] = state.astype(BF16)
    high = decay.astype(BF16).astype(F32)
    row = lax.broadcasted_iota(jnp.int32, (TAIL, decay.shape[1]), 0)
    ref[STATE:, at] = jnp.where(row == 0, high, decay - high).astype(BF16)


def unpack_state(ref):
    tail = ref[STATE:].astype(F32)
    return ref[:STATE].astype(F32), tail[:1] + tail[1:2]


def home_kernel(keeps, rows_ref, sums_ref, gain_ref, bw_ref, tot_ref, x_ref, state_ref):
    mine = lax.axis_index("seq") % 2
    side = mine if keeps else 1 - mine
    toks, half = x_ref.shape
    blk = toks // 2
    pairs = half // HDIM
    lanes = pl.ds(pl.multiple_of(side * half, half), half)
    gain = gain_ref[:, lanes]
    for part in range(2):
        at = slice(part * blk, (part + 1) * blk)
        sums = sums_ref[part * 8 : part * 8 + 1]
        mean = jnp.transpose(jnp.broadcast_to(sums, (blk, blk))) / (HEADS * HDIM)
        inv = lax.rsqrt(mean + 1e-06)[:, :1]
        x_ref[at, :] = (rows_ref[at, lanes].astype(F32) * gain * inv).astype(BF16)
    for p in range(pairs):
        at = slice(p * HDIM, (p + 1) * HDIM)
        state = dot(bw_ref[side * pairs + p], spread(x_ref[:, at]))
        if keeps:
            state_ref[:, at] = state
        else:
            decay = tot_ref[:, pl.ds(pl.multiple_of(side * half + p * HDIM, HDIM), HDIM)]
            pack_state(state_ref, state, decay, at)


def local_kernel(x_keep_ref, x_send_ref, mix_ref, skip_ref, keep_ref, send_ref):
    mine = lax.axis_index("seq") % 2
    half = x_keep_ref.shape[1]
    pairs = half // HDIM
    for x_ref, out_ref, side in ((x_keep_ref, keep_ref, mine), (x_send_ref, send_ref, 1 - mine)):
        skip = skip_ref[:, pl.ds(pl.multiple_of(side * half, half), half)]
        for p in range(pairs):
            at = slice(p * HDIM, (p + 1) * HDIM)
            x = x_ref[:, at]
            out_ref[:, at] = dot(mix_ref[side * pairs + p], spread(x)) + skip[:, at] * x.astype(F32)


def final_kernel(keep_ref, send_ref, scale_ref, c_ref, own_ref, other_ref, out_ref):
    mine = lax.axis_index("seq") % 2
    half = keep_ref.shape[1]
    for local_ref, enter_ref, side in ((keep_ref, own_ref, mine), (send_ref, other_ref, 1 - mine)):
        lanes = pl.ds(pl.multiple_of(side * half, half), half)
        part = dot(c_ref[...], enter_ref[...])
        out_ref[:, lanes] = (local_ref[...] + part * scale_ref[:, lanes]).astype(BF16)


def add_kernel(a_ref, b_ref, out_ref):
    out_ref[...] = a_ref[...] + b_ref[...]


def half_of(ref, side):
    half = ref.shape[1] // 2
    return ref[:, pl.ds(pl.multiple_of(side * half, half), half)]


def chip_kernel(keep_ref, got_ref, tot_ref, early_ref, ahead_ref, low_ref, *refs):
    mine = lax.axis_index("seq") % 2
    late = mine == 1
    keep, here = keep_ref[...], half_of(tot_ref, mine)
    got, there = unpack_state(got_ref)
    early = jnp.where(late, got, keep)
    total = jnp.where(late, here, there) * early + jnp.where(late, keep, got)
    early_ref[...] = early
    ahead_ref[...] = jnp.where(late, there, here)
    pack_state(low_ref, total, here * there)
    if refs:
        refs[0][...] = total
        refs[1][...] = here * there


def stage_kernel(bit, first, total_ref, mine_ref, theirs_ref, *refs):
    upper = (lax.axis_index("seq") >> bit) % 2 == 1
    enter_ref, carried_ref, low_ref, next_ref, running_ref = refs[-5:]
    theirs, decay = unpack_state(theirs_ref)
    total, mine = total_ref[...], mine_ref[...]
    if first:
        enter_ref[...] = jnp.where(upper, theirs, 0.0)
        carried_ref[...] = jnp.where(upper, decay, 1.0)
    else:
        carried = refs[1][...]
        enter_ref[...] = refs[0][...] + jnp.where(upper, carried * theirs, 0.0)
        carried_ref[...] = jnp.where(upper, carried * decay, carried)
    total = jnp.where(upper, mine * theirs + total, decay * total + theirs)
    pack_state(low_ref, total, mine * decay)
    next_ref[...] = total
    running_ref[...] = mine * decay


def last_kernel(shift, inner_ref, outer_ref, both_ref, early_ref, ahead_ref, *refs):
    own_ref, give_ref = refs[-2:]
    me = lax.axis_index("seq")
    quarter, late = me >> shift, me % 2 == 1
    beside, by_inner = unpack_state(inner_ref)
    across, by_outer = unpack_state(outer_ref)
    diagonal, by_both = unpack_state(both_ref)
    one, zero = jnp.ones_like(by_inner), jnp.zeros_like(by_inner)

    def by_quarter(second, third, fourth):
        last = jnp.where(quarter == 3, fourth, zero)
        return jnp.where(quarter == 1, second, jnp.where(quarter == 2, third, last))

    enter = by_quarter(one, zero, one) * beside
    enter = enter + by_quarter(zero, by_both, by_inner) * across
    enter = enter + by_quarter(zero, one, by_inner * by_outer) * diagonal
    if len(refs) == 4:
        enter = refs[0][...] + refs[1][...] * enter
    after = ahead_ref[...] * enter + early_ref[...]
    own_ref[...] = jnp.where(late, after, enter).astype(BF16)
    give_ref[...] = jnp.where(late, enter, after).astype(BF16)


def layer(query, keys, values, norm_gain, in_b, out_c, step, log_decay, skip):
    seq_count = lax.axis_size("seq")
    head_count = lax.axis_size("head")
    blk, feat = query.shape[1:]
    heads, toks = step.shape
    kv_width = keys.shape[2]
    pairs = heads // 2
    half = feat // 2
    every = range(seq_count)

    def swap(block, bit):
        return lax.ppermute(block, "seq", [(i, i ^ (1 << bit)) for i in every])

    width = 2 * kv_width
    kv_keep, kv_send = call(
        pack_kv_kernel, [((blk, width), BF16)] * 2, (keys, values), spaces=[pltpu.HBM] * 2
    )
    q_keep, q_send = call(pack_q_kernel, [((blk, feat), BF16)] * 2, (query,), spaces=[pltpu.HBM])
    chips = seq_count // 2
    onward = [(i, i + 2) for i in range(seq_count - 2)] + [(seq_count - 2, 1), (seq_count - 1, 0)]
    kv_got = swap(kv_send, 0)
    old_keep = lax.ppermute(kv_keep, "seq", onward)
    got_k, got_v = call(part_kernel, [((blk, kv_width), BF16)] * 2, (kv_got,))
    old_k = lax.ppermute(got_k, "seq", onward)
    old_v = lax.ppermute(got_v, "seq", onward)
    q_got = swap(q_send, 0)

    mix, b_weighted, scale, tot, skip_row = call(
        prepare_kernel,
        [
            ((pairs, toks, 2 * toks), BF16),
            ((pairs, STATE, 2 * toks), BF16),
            ((toks, feat), F32),
            ((1, feat), F32),
            ((1, feat), F32),
        ],
        (step, log_decay, in_b, out_c, skip),
        flops=1 << 30,
        spaces=[pltpu.HBM] * 5,
    )
    bits = seq_count.bit_length() - 1
    rows_at_once = feat // kv_width * blk
    weights, scales = call(
        score_kernel,
        [((2 * kv_width // HDIM, rows_at_once, 3 * blk), BF16), ((2 * kv_width // HDIM, rows_at_once, HDIM), F32)],
        (q_keep, q_got, kv_keep, kv_got, old_keep, old_k),
        flops=1 << 28,
    )
    attended, sums = call(
        value_kernel,
        [((toks, feat), BF16), ((16, blk), F32)],
        (weights, scales, kv_keep, kv_got, old_keep, old_v),
        flops=1 << 28,
    )
    to_home = [(i, i // 2 + (1 - i % 2) * chips) for i in every]
    rows = lax.ppermute(attended, "seq", to_home)
    for bit in range(head_count.bit_length() - 1):
        other = lax.ppermute(sums, "head", [(i, i ^ (1 << bit)) for i in range(head_count)])
        (sums,) = call(add_kernel, [((16, blk), F32)], (sums, other))
    sums = lax.ppermute(sums, "seq", to_home)
    quarter = 1 << (bits - 2)

    def exchange(block, flip):
        return lax.ppermute(block, "seq", [(i, i ^ (flip * quarter)) for i in every])

    gain = norm_gain[None, :]
    state, row, packed = ((STATE, half), F32), ((1, half), F32), ((STATE + TAIL, half), BF16)
    x_send, send = call(
        functools.partial(home_kernel, False),
        [((toks, half), BF16), packed],
        (rows, sums, gain, b_weighted, tot),
        flops=1 << 27,
    )
    x_keep, keep = call(
        functools.partial(home_kernel, True),
        [((toks, half), BF16), state],
        (rows, sums, gain, b_weighted, tot),
        flops=1 << 27,
    )
    local_keep, local_send = call(
        local_kernel, [((toks, half), F32)] * 2, (x_keep, x_send, mix, skip_row), flops=1 << 29
    )
    got = swap(send, 0)
    stages = range(1, bits - 2)
    early, ahead, low, *held = call(
        chip_kernel, [state, row, packed] + [state, row] * bool(stages), (keep, got, tot)
    )
    entered = ()
    for bit in stages:
        theirs = swap(low, bit)
        *entered, low, total, running = call(
            functools.partial(stage_kernel, bit, bit == 1),
            [state, row, packed, state, row],
            (*held, theirs, *entered),
        )
        held = (total, running)
    both = exchange(low, 3)
    inner = exchange(low, 1)
    outer = exchange(low, 2)
    own, give = call(
        functools.partial(last_kernel, bits - 2),
        [((STATE, half), BF16)] * 2,
        (inner, outer, both, early, ahead, *entered),
    )
    other = swap(give, 0)
    (out,) = call(
        final_kernel,
        [((toks, feat), BF16)],
        (local_keep, local_send, scale, out_c, own, other),
        flops=1 << 28,
    )
    return out


def solution(mesh):
    placed = (
        P(None, "seq", "head"),
        P(None, "seq", "head"),
        P(None, "seq", "head"),
        P("head"),
        P("seq", None),
        P("seq", None),
        P("head", "seq"),
        P("head", "seq"),
        P("head"),
    )
    return jax.shard_map(
        layer, mesh=mesh, in_specs=placed, out_specs=P("seq", "head"), check_vma=False
    )
```

time: 54.2 us -> 43.9 us (0.81)
  waiting for transfers between devices: 27.4 us -> 16.1 us
  starting transfers between devices: 17.5 us -> 18.2 us
    ppermute x1, waiting for transfers between devices: 11.7 us -> 0.88 us  [layer(): sums = lax.ppermute(sums, 'seq', to_home)]
    ppermute x8 -> x4, waiting for transfers between devices: 8.35 us -> 1.48 us  [swap(): return lax.ppermute(block, 'seq', [(i, i ^ 1 << bit) for i in every])]
    ppermute x1 -> x5, waiting for transfers between devices: 2.81 us -> 8.85 us  [the longest x3 7.07 us: exchange(): return lax.ppermute(block, 'seq', [(i, i ^ flip * quarter) for i in every])]
    ppermute x1 -> x5, starting transfers between devices: 1.49 us -> 7.05 us  [the longest x3 4.01 us: exchange(): return lax.ppermute(block, 'seq', [(i, i ^ flip * quarter) for i in every])]
    ppermute x8 -> x4, starting transfers between devices: 5.76 us -> 0.65 us  [swap(): return lax.ppermute(block, 'seq', [(i, i ^ 1 << bit) for i in every])]
    ppermute x2, waiting for transfers between devices: 2.04 us -> 4.03 us  [layer(): lax.ppermute(sums, 'head', [(i, i ^ 1 << bit) for i in range(head_count)])]
    ppermute x1, waiting for transfers between devices: 2.43 us -> 0.87 us  [layer(): old_keep = lax.ppermute(kv_keep, 'seq', onward)]
    pallas_call x12 -> x14, Pallas kernels: 9.11 us -> 9.22 us  [call(): pl.pallas_call(kernel, out_shape=[jax.ShapeDtypeStruct(s, d) for s, d in...]
  transfers between devices with their start and end apart: 14 -> 14, of which waited for: 8 -> 11; matrix products, arithmetic and copies ran while one was open for 0% -> 0% of each run, Pallas kernels for 6% -> 13%
where the time goes in v6:
time: 43.9 us; the launch traced here: 43.7 us
  starting transfers between devices  18.2 us (41%)
  waiting for transfers between devices  16.1 us (37%)
  Pallas kernels  9.22 us (21%)
    pallas_call x14, Pallas kernels, call(): pl.pallas_call(kernel, out_shape=[jax.ShapeDtypeStruct(s, d) for s, d in...  9.22 us
    ppermute x3, waiting for transfers between devices, exchange(): return lax.ppermute(block, 'seq', [(i, i ^ flip * quarter) for i in every])  7.07 us
    ppermute x2, starting transfers between devices, layer(): lax.ppermute(sums, 'head', [(i, i ^ 1 << bit) for i in range(head_count)])  4.17 us
    ppermute x2, waiting for transfers between devices, layer(): lax.ppermute(sums, 'head', [(i, i ^ 1 << bit) for i in range(head_count)])  4.03 us
    ppermute x3, starting transfers between devices, exchange(): return lax.ppermute(block, 'seq', [(i, i ^ flip * quarter) for i in every])  4.01 us
    ppermute x1, starting transfers between devices, layer(): old_keep = lax.ppermute(kv_keep, 'seq', onward)  2.97 us
    ppermute x1, starting transfers between devices, layer(): rows = lax.ppermute(attended, 'seq', to_home)  2.8 us
    ppermute x1, starting transfers between devices, layer(): old_k = lax.ppermute(got_k, 'seq', onward)  1.55 us
  transfers between devices with their start and end apart: 14, of which 11 were waited for; matrix products, arithmetic and copies ran while one was open for 0% of the time, Pallas kernels for 13%

profile of v6, /device:TPU:0, one launch (start us, length us, event | category | flops | bytes accessed | tf_op | source)
XLA Modules:
  0.0 43.7 jit_solution(16212668485906370279)
XLA Ops:
  0.0 1.0 %shard_map.91 = (bf16[128,1024]{1,0:T(8,128)(2,1)S(1)}, bf16[128,1024]{1,0:T(8,128)(2,1)S(1)}) custom-call(bf16[2,128,1024]{2,1,0:T(8,128)(2,1)} %q_ref.1), custom_call_target="tpu_custom_call" | custom-call | flops 1 | bytes 1048576 | tf_op jit(solution)/shard_map/pallas_call | solution.py:36
  1.5 0.9 %shard_map.92 = (bf16[128,512]{1,0:T(8,128)(2,1)S(1)}, bf16[128,512]{1,0:T(8,128)(2,1)S(1)}) custom-call(bf16[2,128,256]{2,1,0:T(8,128)(2,1)} %k_ref.1, bf16[2,128,256]{2,1,0:T(8,128)(2,1)} %v_ref.1), custom_call_target="tpu_custom_call" | custom-call | flops 1 | bytes 1048576 | tf_op jit(solution)/shard_map/pallas_call | solution.py:36
  2.5 3.0 %collective-permute-start.2 = (bf16[128,512]{1,0:T(8,128)(2,1)S(1)}, bf16[128,512]{1,0:T(8,128)(2,1)S(1)}, u32[]{:S(2)}, u32[]{:S(2)}) collective-permute-start(bf16[128,512]{1,0:T(8,128)(2,1)S(1)} %get-tuple-element.33.kv_keep_ref), channel_id=1, source_target_pairs={{0,8},{4,12},{8,16},{12,20},{16,24},{20,28},{24,4},{28,0},{1,9},{5... | collective-permute-start | bytes 393224 | tf_op jit(solution)/shard_map/ppermute | solution.py:365
  5.5 1.6 %collective-permute-start.3 = (bf16[128,256]{1,0:T(8,128)(2,1)S(1)}, bf16[128,256]{1,0:T(8,128)(2,1)S(1)}, u32[]{:S(2)}, u32[]{:S(2)}) collective-permute-start(bf16[128,256]{1,0:T(8,128)(2,1)S(1)} %get-tuple-element.35), channel_id=1, source_target_pairs={{0,8},{4,12},{8,16},{12,20},{16,24},{20,28},{24,4},{28,0},{1,9},{5... | collective-permute-start | bytes 196616 | tf_op jit(solution)/shard_map/ppermute | solution.py:367
  7.0 1.5 %collective-permute-start.4 = (bf16[128,256]{1,0:T(8,128)(2,1)S(1)}, bf16[128,256]{1,0:T(8,128)(2,1)S(1)}, u32[]{:S(2)}, u32[]{:S(2)}) collective-permute-start(bf16[128,256]{1,0:T(8,128)(2,1)S(1)} %get-tuple-element.38), channel_id=1, source_target_pairs={{0,8},{4,12},{8,16},{12,20},{16,24},{20,28},{24,4},{28,0},{1,9},{5... | collective-permute-start | bytes 196616 | tf_op jit(solution)/shard_map/ppermute | solution.py:368
  8.5 0.9 %collective-permute-done.2.old_keep_ref = bf16[128,512]{1,0:T(8,128)(2,1)S(1)} collective-permute-done((bf16[128,512]{1,0:T(8,128)(2,1)S(1)}, bf16[128,512]{1,0:T(8,128)(2,1)S(1)}, u32[]{:S(2)}, u32[]{:S(2)}) %collective-permute-start.2) | collective-permute-done | bytes 131104 | tf_op jit(solution)/shard_map/ppermute | solution.py:365
  9.4 1.4 %collective-permute-done.3.old_got_ref = bf16[128,256]{1,0:T(8,128)(2,1)S(1)} collective-permute-done((bf16[128,256]{1,0:T(8,128)(2,1)S(1)}, bf16[128,256]{1,0:T(8,128)(2,1)S(1)}, u32[]{:S(2)}, u32[]{:S(2)}) %collective-permute-start.3) | collective-permute-done | bytes 65568 | tf_op jit(solution)/shard_map/ppermute | solution.py:367
  10.8 1.1 %shard_map.94 = (bf16[4,512,384]{2,1,0:T(8,128)(2,1)S(1)}, f32[4,512,128]{2,1,0:T(8,128)S(1)}) custom-call(bf16[128,1024]{1,0:T(8,128)(2,1)S(1)} %get-tuple-element.31.q_keep_ref, bf16[128,1024]{1,0:T(8,128)(2,1)S(1)} %collective-permute-done.q_got_ref, bf16[128,512]{1,0:T(8,128)(2,1)S(1)} %get-tuple-element.33.kv_keep_ref, ...), custom_call_target="tpu_custom_call" | custom-call | flops 268435456 | bytes 1048576 | tf_op jit(solution)/shard_map/pallas_call | solution.py:36
  12.3 0.7 %shard_map.95 = (bf16[256,1024]{1,0:T(8,128)(2,1)S(1)}, f32[16,128]{1,0:T(8,128)S(1)}) custom-call(bf16[4,512,384]{2,1,0:T(8,128)(2,1)S(1)} %get-tuple-element.36.weight_ref, f32[4,512,128]{2,1,0:T(8,128)S(1)} %get-tuple-element.37.scale_ref, bf16[128,512]{1,0:T(8,128)(2,1)S(1)} %get-tuple-element.33.kv_keep_ref, ...), custom_call_target="tpu_custom_call" | custom-call | flops 268435456 | bytes 1048576 | tf_op jit(solution)/shard_map/pallas_call | solution.py:36
  13.0 2.8 %collective-permute-start.5 = (bf16[256,1024]{1,0:T(8,128)(2,1)S(1)}, bf16[256,1024]{1,0:T(8,128)(2,1)S(1)}, u32[]{:S(2)}, u32[]{:S(2)}) collective-permute-start(bf16[256,1024]{1,0:T(8,128)(2,1)S(1)} %get-tuple-element.39), channel_id=1, source_target_pairs={{0,16},{4,0},{8,20},{12,4},{16,24},{20,8},{24,28},{28,12},{1,17},{... | collective-permute-start | bytes 1572872 | tf_op jit(solution)/shard_map/ppermute | solution.py:399
  15.8 1.6 %collective-permute-start.6 = (f32[16,128]{1,0:T(8,128)S(1)}, f32[16,128]{1,0:T(8,128)S(1)}, u32[]{:S(2)}, u32[]{:S(2)}) collective-permute-start(f32[16,128]{1,0:T(8,128)S(1)} %get-tuple-element.40.a_ref), channel_id=1, source_target_pairs={{0,1},{1,0},{2,3},{3,2},{4,5},{5,4},{6,7},{7,6},{8,9},{9,8},{10,11... | collective-permute-start | bytes 24584 | tf_op jit(solution)/shard_map/ppermute | solution.py:401
  17.4 2.1 %collective-permute-done.6.b_ref = f32[16,128]{1,0:T(8,128)S(1)} collective-permute-done((f32[16,128]{1,0:T(8,128)S(1)}, f32[16,128]{1,0:T(8,128)S(1)}, u32[]{:S(2)}, u32[]{:S(2)}) %collective-permute-start.6) | collective-permute-done | bytes 8224 | tf_op jit(solution)/shard_map/ppermute | solution.py:401
  19.5 2.6 %collective-permute-start.7 = (f32[16,128]{1,0:T(8,128)S(1)}, f32[16,128]{1,0:T(8,128)S(1)}, u32[]{:S(2)}, u32[]{:S(2)}) collective-permute-start(f32[16,128]{1,0:T(8,128)S(1)} %shard_map.96.a_ref), channel_id=1, source_target_pairs={{0,2},{1,3},{2,0},{3,1},{4,6},{5,7},{6,4},{7,5},{8,10},{9,11},{10,... | collective-permute-start | bytes 24584 | tf_op jit(solution)/shard_map/ppermute | solution.py:401
  22.1 2.0 %collective-permute-done.7.b_ref = f32[16,128]{1,0:T(8,128)S(1)} collective-permute-done((f32[16,128]{1,0:T(8,128)S(1)}, f32[16,128]{1,0:T(8,128)S(1)}, u32[]{:S(2)}, u32[]{:S(2)}) %collective-permute-start.7) | collective-permute-done | bytes 8224 | tf_op jit(solution)/shard_map/ppermute | solution.py:401
  24.6 2.4 %shard_map.98 = (bf16[8,256,512]{2,1,0:T(8,128)(2,1)S(1)}, bf16[8,128,512]{2,1,0:T(8,128)(2,1)S(1)}, f32[256,1024]{1,0:T(8,128)S(1)}, f32[1,1024]{1,0:T(1,128)S(1)}, f32[1,1024]{1,0:T(1,128)S(1)}) custom-call(f32[16,256]{1,0:T(8,128)} %refs_0_.1, f32[16,256]{1,0:T(8,128)} %refs_1_.1, bf16[256,128]{1,0:T(8,128)(2,1)} %refs_2_.1, bf16[256,128]{1,0:T(8,128)(2,1)} %c_ref.1, ...), custom_call_target="tpu_custom_call" | custom-call | flops 1073741824 | bytes 1048576 | tf_op jit(solution)/shard_map/pallas_call | solution.py:36
  27.0 0.9 %collective-permute-done.8.sums_ref = f32[16,128]{1,0:T(8,128)S(1)} collective-permute-done((f32[16,128]{1,0:T(8,128)S(1)}, f32[16,128]{1,0:T(8,128)S(1)}, u32[]{:S(2)}, u32[]{:S(2)}) %collective-permute-start.8) | collective-permute-done | bytes 8224 | tf_op jit(solution)/shard_map/ppermute | solution.py:403
  29.0 0.9 %collective-permute-done.9.got_ref = bf16[144,512]{1,0:T(8,128)(2,1)S(1)} collective-permute-done((bf16[144,512]{1,0:T(8,128)(2,1)S(1)}, bf16[144,512]{1,0:T(8,128)(2,1)S(1)}, u32[]{:S(2)}, u32[]{:S(2)}) %collective-permute-start.9) | collective-permute-done | bytes 147488 | tf_op jit(solution)/shard_map/ppermute | solution.py:355
  29.9 2.4 %collective-permute-start.12 = (bf16[144,512]{1,0:T(8,128)(2,1)S(1)}, bf16[144,512]{1,0:T(8,128)(2,1)S(1)}, u32[]{:S(2)}, u32[]{:S(2)}) collective-permute-start(bf16[144,512]{1,0:T(8,128)(2,1)S(1)} %get-tuple-element.52), channel_id=1, source_target_pairs={{0,24},{4,28},{8,16},{12,20},{16,8},{20,12},{24,0},{28,4},{1,25},{... | collective-permute-start | bytes 442376 | tf_op jit(solution)/shard_map/ppermute | solution.py:407
  32.3 0.8 %collective-permute-start.11 = (bf16[144,512]{1,0:T(8,128)(2,1)S(1)}, bf16[144,512]{1,0:T(8,128)(2,1)S(1)}, u32[]{:S(2)}, u32[]{:S(2)}) collective-permute-start(bf16[144,512]{1,0:T(8,128)(2,1)S(1)} %get-tuple-element.52), channel_id=1, source_target_pairs={{0,16},{4,20},{8,24},{12,28},{16,0},{20,4},{24,8},{28,12},{1,17},{... | collective-permute-start | bytes 442376 | tf_op jit(solution)/shard_map/ppermute | solution.py:407
  33.1 0.8 %collective-permute-start.10 = (bf16[144,512]{1,0:T(8,128)(2,1)S(1)}, bf16[144,512]{1,0:T(8,128)(2,1)S(1)}, u32[]{:S(2)}, u32[]{:S(2)}) collective-permute-start(bf16[144,512]{1,0:T(8,128)(2,1)S(1)} %get-tuple-element.52), channel_id=1, source_target_pairs={{0,8},{4,12},{8,0},{12,4},{16,24},{20,28},{24,16},{28,20},{1,9},{5... | collective-permute-start | bytes 442376 | tf_op jit(solution)/shard_map/ppermute | solution.py:407
  33.9 3.7 %collective-permute-done.12.both_ref = bf16[144,512]{1,0:T(8,128)(2,1)S(1)} collective-permute-done((bf16[144,512]{1,0:T(8,128)(2,1)S(1)}, bf16[144,512]{1,0:T(8,128)(2,1)S(1)}, u32[]{:S(2)}, u32[]{:S(2)}) %collective-permute-start.12) | collective-permute-done | bytes 147488 | tf_op jit(solution)/shard_map/ppermute | solution.py:407
  37.6 2.3 %collective-permute-done.11.outer_ref = bf16[144,512]{1,0:T(8,128)(2,1)S(1)} collective-permute-done((bf16[144,512]{1,0:T(8,128)(2,1)S(1)}, bf16[144,512]{1,0:T(8,128)(2,1)S(1)}, u32[]{:S(2)}, u32[]{:S(2)}) %collective-permute-start.11) | collective-permute-done | bytes 147488 | tf_op jit(solution)/shard_map/ppermute | solution.py:407
  39.9 1.1 %collective-permute-done.10.inner_ref = bf16[144,512]{1,0:T(8,128)(2,1)S(1)} collective-permute-done((bf16[144,512]{1,0:T(8,128)(2,1)S(1)}, bf16[144,512]{1,0:T(8,128)(2,1)S(1)}, u32[]{:S(2)}, u32[]{:S(2)}) %collective-permute-start.10) | collective-permute-done | bytes 147488 | tf_op jit(solution)/shard_map/ppermute | solution.py:407
  42.6 1.1 %shard_map.104 = bf16[256,1024]{1,0:T(8,128)(2,1)} custom-call(f32[256,512]{1,0:T(8,128)S(1)} %get-tuple-element.47.keep_ref, f32[256,512]{1,0:T(8,128)S(1)} %get-tuple-element.48.send_ref, f32[256,1024]{1,0:T(8,128)S(1)} %get-tuple-element.49.scale_ref, bf16[256,128]{1,0:T(8,128)(2,1)S(1)} %copy-done, bf16[128,512]{1,0:T(8,128)(2,1)S(1)} %get-tuple-element.55.own_ref, ...), custom_call_target="tpu_custom_call" | custom-call | flops 268435456 | bytes 1048576 | tf_op jit(solution)/shard_map/pallas_call | solution.py:36
  (22 shorter events, 4.1 us)
Async XLA Ops:
  1.0 9.8 %collective-permute-start = (bf16[128,1024]{1,0:T(8,128)(2,1)S(1)}, bf16[128,1024]{1,0:T(8,128)(2,1)S(1)}, u32[]{:S(2)}, u32[]{:S(2)}) collective-permute-start(bf16[128,1024]{1,0:T(8,128)(2,1)S(1)} %get-tuple-element.32), channel_id=1, source_target_pairs={{0,4},{4,0},{8,12},{12,8},{16,20},{20,16},{24,28},{28,24},{1,5},{5... | collective-permute-start | bytes 786440 | tf_op jit(solution)/shard_map/ppermute | solution.py:355
  2.5 3.0 %collective-permute-start.1 = (bf16[128,512]{1,0:T(8,128)(2,1)S(1)}, bf16[128,512]{1,0:T(8,128)(2,1)S(1)}, u32[]{:S(2)}, u32[]{:S(2)}) collective-permute-start(bf16[128,512]{1,0:T(8,128)(2,1)S(1)} %get-tuple-element.34), channel_id=1, source_target_pairs={{0,4},{4,0},{8,12},{12,8},{16,20},{20,16},{24,28},{28,24},{1,5},{5... | collective-permute-start | bytes 393224 | tf_op jit(solution)/shard_map/ppermute | solution.py:355
  2.5 6.9 %collective-permute-start.2 = (bf16[128,512]{1,0:T(8,128)(2,1)S(1)}, bf16[128,512]{1,0:T(8,128)(2,1)S(1)}, u32[]{:S(2)}, u32[]{:S(2)}) collective-permute-start(bf16[128,512]{1,0:T(8,128)(2,1)S(1)} %get-tuple-element.33.kv_keep_ref), channel_id=1, source_target_pairs={{0,8},{4,12},{8,16},{12,20},{16,24},{20,28},{24,4},{28,0},{1,9},{5... | collective-permute-start | bytes 393224 | tf_op jit(solution)/shard_map/ppermute | solution.py:365
  5.5 5.3 %collective-permute-start.3 = (bf16[128,256]{1,0:T(8,128)(2,1)S(1)}, bf16[128,256]{1,0:T(8,128)(2,1)S(1)}, u32[]{:S(2)}, u32[]{:S(2)}) collective-permute-start(bf16[128,256]{1,0:T(8,128)(2,1)S(1)} %get-tuple-element.35), channel_id=1, source_target_pairs={{0,8},{4,12},{8,16},{12,20},{16,24},{20,28},{24,4},{28,0},{1,9},{5... | collective-permute-start | bytes 196616 | tf_op jit(solution)/shard_map/ppermute | solution.py:367
  7.0 5.3 %collective-permute-start.4 = (bf16[128,256]{1,0:T(8,128)(2,1)S(1)}, bf16[128,256]{1,0:T(8,128)(2,1)S(1)}, u32[]{:S(2)}, u32[]{:S(2)}) collective-permute-start(bf16[128,256]{1,0:T(8,128)(2,1)S(1)} %get-tuple-element.38), channel_id=1, source_target_pairs={{0,8},{4,12},{8,16},{12,20},{16,24},{20,28},{24,4},{28,0},{1,9},{5... | collective-permute-start | bytes 196616 | tf_op jit(solution)/shard_map/ppermute | solution.py:368
  13.0 14.9 %copy-start.1 = (f32[1024]{0:T(1024)S(1)}, f32[1024]{0:T(1024)}, u32[]{:S(2)}) copy-start(f32[1024]{0:T(1024)} %param.12) | copy-start | bytes 12292
  13.0 14.9 %collective-permute-start.5 = (bf16[256,1024]{1,0:T(8,128)(2,1)S(1)}, bf16[256,1024]{1,0:T(8,128)(2,1)S(1)}, u32[]{:S(2)}, u32[]{:S(2)}) collective-permute-start(bf16[256,1024]{1,0:T(8,128)(2,1)S(1)} %get-tuple-element.39), channel_id=1, source_target_pairs={{0,16},{4,0},{8,20},{12,4},{16,24},{20,8},{24,28},{28,12},{1,17},{... | collective-permute-start | bytes 1572872 | tf_op jit(solution)/shard_map/ppermute | solution.py:399
  15.8 3.7 %collective-permute-start.6 = (f32[16,128]{1,0:T(8,128)S(1)}, f32[16,128]{1,0:T(8,128)S(1)}, u32[]{:S(2)}, u32[]{:S(2)}) collective-permute-start(f32[16,128]{1,0:T(8,128)S(1)} %get-tuple-element.40.a_ref), channel_id=1, source_target_pairs={{0,1},{1,0},{2,3},{3,2},{4,5},{5,4},{6,7},{7,6},{8,9},{9,8},{10,11... | collective-permute-start | bytes 24584 | tf_op jit(solution)/shard_map/ppermute | solution.py:401
  19.5 4.5 %collective-permute-start.7 = (f32[16,128]{1,0:T(8,128)S(1)}, f32[16,128]{1,0:T(8,128)S(1)}, u32[]{:S(2)}, u32[]{:S(2)}) collective-permute-start(f32[16,128]{1,0:T(8,128)S(1)} %shard_map.96.a_ref), channel_id=1, source_target_pairs={{0,2},{1,3},{2,0},{3,1},{4,6},{5,7},{6,4},{7,5},{8,10},{9,11},{10,... | collective-permute-start | bytes 24584 | tf_op jit(solution)/shard_map/ppermute | solution.py:401
  24.0 3.9 %collective-permute-start.8 = (f32[16,128]{1,0:T(8,128)S(1)}, f32[16,128]{1,0:T(8,128)S(1)}, u32[]{:S(2)}, u32[]{:S(2)}) collective-permute-start(f32[16,128]{1,0:T(8,128)S(1)} %shard_map.97), channel_id=1, source_target_pairs={{0,16},{4,0},{8,20},{12,4},{16,24},{20,8},{24,28},{28,12},{1,17},{... | collective-permute-start | bytes 24584 | tf_op jit(solution)/shard_map/ppermute | solution.py:403
  28.4 1.4 %collective-permute-start.9 = (bf16[144,512]{1,0:T(8,128)(2,1)S(1)}, bf16[144,512]{1,0:T(8,128)(2,1)S(1)}, u32[]{:S(2)}, u32[]{:S(2)}) collective-permute-start(bf16[144,512]{1,0:T(8,128)(2,1)S(1)} %get-tuple-element.51), channel_id=1, source_target_pairs={{0,4},{4,0},{8,12},{12,8},{16,20},{20,16},{24,28},{28,24},{1,5},{5... | collective-permute-start | bytes 442376 | tf_op jit(solution)/shard_map/ppermute | solution.py:355
  28.9 13.6 %copy-start = (bf16[256,128]{1,0:T(8,128)(2,1)S(1)}, bf16[256,128]{1,0:T(8,128)(2,1)}, u32[]{:S(2)}) copy-start(bf16[256,128]{1,0:T(8,128)(2,1)} %c_ref.1) | copy-start | bytes 196612
  29.9 7.7 %collective-permute-start.12 = (bf16[144,512]{1,0:T(8,128)(2,1)S(1)}, bf16[144,512]{1,0:T(8,128)(2,1)S(1)}, u32[]{:S(2)}, u32[]{:S(2)}) collective-permute-start(bf16[144,512]{1,0:T(8,128)(2,1)S(1)} %get-tuple-element.52), channel_id=1, source_target_pairs={{0,24},{4,28},{8,16},{12,20},{16,8},{20,12},{24,0},{28,4},{1,25},{... | collective-permute-start | bytes 442376 | tf_op jit(solution)/shard_map/ppermute | solution.py:407
  32.3 7.7 %collective-permute-start.11 = (bf16[144,512]{1,0:T(8,128)(2,1)S(1)}, bf16[144,512]{1,0:T(8,128)(2,1)S(1)}, u32[]{:S(2)}, u32[]{:S(2)}) collective-permute-start(bf16[144,512]{1,0:T(8,128)(2,1)S(1)} %get-tuple-element.52), channel_id=1, source_target_pairs={{0,16},{4,20},{8,24},{12,28},{16,0},{20,4},{24,8},{28,12},{1,17},{... | collective-permute-start | bytes 442376 | tf_op jit(solution)/shard_map/ppermute | solution.py:407
  33.1 7.9 %collective-permute-start.10 = (bf16[144,512]{1,0:T(8,128)(2,1)S(1)}, bf16[144,512]{1,0:T(8,128)(2,1)S(1)}, u32[]{:S(2)}, u32[]{:S(2)}) collective-permute-start(bf16[144,512]{1,0:T(8,128)(2,1)S(1)} %get-tuple-element.52), channel_id=1, source_target_pairs={{0,8},{4,12},{8,0},{12,4},{16,24},{20,28},{24,16},{28,20},{1,9},{5... | collective-permute-start | bytes 442376 | tf_op jit(solution)/shard_map/ppermute | solution.py:407
  41.2 1.4 %collective-permute-start.13 = (bf16[128,512]{1,0:T(8,128)(2,1)S(1)}, bf16[128,512]{1,0:T(8,128)(2,1)S(1)}, u32[]{:S(2)}, u32[]{:S(2)}) collective-permute-start(bf16[128,512]{1,0:T(8,128)(2,1)S(1)} %get-tuple-element.56), channel_id=1, source_target_pairs={{0,4},{4,0},{8,12},{12,8},{16,20},{20,16},{24,28},{28,24},{1,5},{5... | collective-permute-start | bytes 393224 | tf_op jit(solution)/shard_map/ppermute | solution.py:355

commit v7 on v6

--- a/solution.py
+++ b/solution.py
@@ -267,13 +267,18 @@
             out_ref[:, at] = dot(mix_ref[side * pairs + p], spread(x)) + skip[:, at] * x.astype(F32)
 
 
-def final_kernel(keep_ref, send_ref, scale_ref, c_ref, own_ref, other_ref, out_ref):
-    mine = lax.axis_index("seq") % 2
-    half = keep_ref.shape[1]
-    for local_ref, enter_ref, side in ((keep_ref, own_ref, mine), (send_ref, other_ref, 1 - mine)):
-        lanes = pl.ds(pl.multiple_of(side * half, half), half)
-        part = dot(c_ref[...], enter_ref[...])
-        out_ref[:, lanes] = (local_ref[...] + part * scale_ref[:, lanes]).astype(BF16)
+def finish_kernel(keeps, local_ref, scale_ref, c_ref, enter_ref, *refs):
+    mine = lax.axis_index("seq") % 2
+    half = local_ref.shape[1]
+    side = mine if keeps else 1 - mine
+    lanes = pl.ds(pl.multiple_of(side * half, half), half)
+    out = local_ref[...] + dot(c_ref[...], enter_ref[...]) * scale_ref[:, lanes]
+    if keeps:
+        refs[0][...] = out.astype(BF16)
+    else:
+        own_ref, out_ref = refs
+        out_ref[:, lanes] = out.astype(BF16)
+        out_ref[:, pl.ds(pl.multiple_of(mine * half, half), half)] = own_ref[...]
 
 
 def add_kernel(a_ref, b_ref, out_ref):
@@ -324,16 +329,12 @@
     quarter, late = me >> shift, me % 2 == 1
     beside, by_inner = unpack_state(inner_ref)
     across, by_outer = unpack_state(outer_ref)
-    diagonal, by_both = unpack_state(both_ref)
+    diagonal, _ = unpack_state(both_ref)
+    third, fourth = quarter == 2, quarter == 3
     one, zero = jnp.ones_like(by_inner), jnp.zeros_like(by_inner)
-
-    def by_quarter(second, third, fourth):
-        last = jnp.where(quarter == 3, fourth, zero)
-        return jnp.where(quarter == 1, second, jnp.where(quarter == 2, third, last))
-
-    enter = by_quarter(one, zero, one) * beside
-    enter = enter + by_quarter(zero, by_both, by_inner) * across
-    enter = enter + by_quarter(zero, one, by_inner * by_outer) * diagonal
+    enter = jnp.where(quarter > 0, one, zero) * beside
+    enter = enter + jnp.where(third | fourth, by_inner, zero) * across
+    enter = enter + jnp.where(fourth, by_inner * by_outer, zero) * diagonal
     if len(refs) == 4:
         enter = refs[0][...] + refs[1][...] * enter
     after = ahead_ref[...] * enter + early_ref[...]
@@ -403,8 +404,12 @@
     sums = lax.ppermute(sums, "seq", to_home)
     quarter = 1 << (bits - 2)
 
-    def exchange(block, flip):
-        return lax.ppermute(block, "seq", [(i, i ^ (flip * quarter)) for i in every])
+    def hop(block, quarters):
+        route = []
+        for i in every:
+            to = quarters[i // quarter]
+            route.append((i, i ^ 1 if to is None else to * quarter + i % quarter))
+        return lax.ppermute(block, "seq", route)
 
     gain = norm_gain[None, :]
     state, row, packed = ((STATE, half), F32), ((1, half), F32), ((STATE + TAIL, half), BF16)
@@ -437,20 +442,26 @@
             (*held, theirs, *entered),
         )
         held = (total, running)
-    both = exchange(low, 3)
-    inner = exchange(low, 1)
-    outer = exchange(low, 2)
+    both = hop(low, (3, 0, None, 1))
+    inner = hop(low, (1, 2, 3, 0))
+    outer = hop(low, (2, 3, 0, 1))
     own, give = call(
         functools.partial(last_kernel, bits - 2),
         [((STATE, half), BF16)] * 2,
         (inner, outer, both, early, ahead, *entered),
     )
     other = swap(give, 0)
+    (kept,) = call(
+        functools.partial(finish_kernel, True),
+        [((toks, half), BF16)],
+        (local_keep, scale, out_c, own),
+        flops=1 << 27,
+    )
     (out,) = call(
-        final_kernel,
+        functools.partial(finish_kernel, False),
         [((toks, feat), BF16)],
-        (local_keep, local_send, scale, out_c, own, other),
-        flops=1 << 28,
+        (local_send, scale, out_c, other, kept),
+        flops=1 << 27,
     )
     return out
 

time: 43.9 us -> 43.8 us (level)
    pallas_call x14 -> x15, Pallas kernels: 9.22 us -> 9.33 us  [call(): pl.pallas_call(kernel, out_shape=[jax.ShapeDtypeStruct(s, d) for s, d in...]
  transfers between devices with their start and end apart: 14 -> 14, of which waited for: 11 -> 10; matrix products, arithmetic and copies ran while one was open for 0% -> 0% of each run, Pallas kernels for 13% -> 13%
where the time goes in v7:
time: 43.8 us; the launch traced here: 43.6 us
  starting transfers between devices  17.9 us (41%)
  waiting for transfers between devices  16.2 us (37%)
  Pallas kernels  9.33 us (21%)
    pallas_call x15, Pallas kernels, call(): pl.pallas_call(kernel, out_shape=[jax.ShapeDtypeStruct(s, d) for s, d in...  9.33 us
    ppermute x3, waiting for transfers between devices, hop(): return lax.ppermute(block, 'seq', route)  7.38 us
    ppermute x2, starting transfers between devices, layer(): lax.ppermute(sums, 'head', [(i, i ^ 1 << bit) for i in range(head_count)])  4.17 us
    ppermute x2, waiting for transfers between devices, layer(): lax.ppermute(sums, 'head', [(i, i ^ 1 << bit) for i in range(head_count)])  4.03 us
    ppermute x3, starting transfers between devices, hop(): return lax.ppermute(block, 'seq', route)  3.73 us
    ppermute x1, starting transfers between devices, layer(): old_keep = lax.ppermute(kv_keep, 'seq', onward)  2.97 us
    ppermute x1, starting transfers between devices, layer(): rows = lax.ppermute(attended, 'seq', to_home)  2.8 us
    ppermute x1, starting transfers between devices, layer(): old_k = lax.ppermute(got_k, 'seq', onward)  1.55 us
  transfers between devices with their start and end apart: 14, of which 10 were waited for; matrix products, arithmetic and copies ran while one was open for 0% of the time, Pallas kernels for 13%

profile of v7, /device:TPU:0, one launch (start us, length us, event | category | flops | bytes accessed | tf_op | source)
XLA Modules:
  0.0 43.6 jit_solution(5380714073760190574)
XLA Ops:
  0.0 1.0 %shard_map.91 = (bf16[128,1024]{1,0:T(8,128)(2,1)S(1)}, bf16[128,1024]{1,0:T(8,128)(2,1)S(1)}) custom-call(bf16[2,128,1024]{2,1,0:T(8,128)(2,1)} %q_ref.1), custom_call_target="tpu_custom_call" | custom-call | flops 1 | bytes 1048576 | tf_op jit(solution)/shard_map/pallas_call | solution.py:36
  1.5 0.9 %shard_map.92 = (bf16[128,512]{1,0:T(8,128)(2,1)S(1)}, bf16[128,512]{1,0:T(8,128)(2,1)S(1)}) custom-call(bf16[2,128,256]{2,1,0:T(8,128)(2,1)} %k_ref.1, bf16[2,128,256]{2,1,0:T(8,128)(2,1)} %v_ref.1), custom_call_target="tpu_custom_call" | custom-call | flops 1 | bytes 1048576 | tf_op jit(solution)/shard_map/pallas_call | solution.py:36
  2.5 3.0 %collective-permute-start.2 = (bf16[128,512]{1,0:T(8,128)(2,1)S(1)}, bf16[128,512]{1,0:T(8,128)(2,1)S(1)}, u32[]{:S(2)}, u32[]{:S(2)}) collective-permute-start(bf16[128,512]{1,0:T(8,128)(2,1)S(1)} %get-tuple-element.33.kv_keep_ref), channel_id=1, source_target_pairs={{0,8},{4,12},{8,16},{12,20},{16,24},{20,28},{24,4},{28,0},{1,9},{5... | collective-permute-start | bytes 393224 | tf_op jit(solution)/shard_map/ppermute | solution.py:366
  5.5 1.6 %collective-permute-start.3 = (bf16[128,256]{1,0:T(8,128)(2,1)S(1)}, bf16[128,256]{1,0:T(8,128)(2,1)S(1)}, u32[]{:S(2)}, u32[]{:S(2)}) collective-permute-start(bf16[128,256]{1,0:T(8,128)(2,1)S(1)} %get-tuple-element.35), channel_id=1, source_target_pairs={{0,8},{4,12},{8,16},{12,20},{16,24},{20,28},{24,4},{28,0},{1,9},{5... | collective-permute-start | bytes 196616 | tf_op jit(solution)/shard_map/ppermute | solution.py:368
  7.0 1.5 %collective-permute-start.4 = (bf16[128,256]{1,0:T(8,128)(2,1)S(1)}, bf16[128,256]{1,0:T(8,128)(2,1)S(1)}, u32[]{:S(2)}, u32[]{:S(2)}) collective-permute-start(bf16[128,256]{1,0:T(8,128)(2,1)S(1)} %get-tuple-element.38), channel_id=1, source_target_pairs={{0,8},{4,12},{8,16},{12,20},{16,24},{20,28},{24,4},{28,0},{1,9},{5... | collective-permute-start | bytes 196616 | tf_op jit(solution)/shard_map/ppermute | solution.py:369
  8.5 0.9 %collective-permute-done.2.old_keep_ref = bf16[128,512]{1,0:T(8,128)(2,1)S(1)} collective-permute-done((bf16[128,512]{1,0:T(8,128)(2,1)S(1)}, bf16[128,512]{1,0:T(8,128)(2,1)S(1)}, u32[]{:S(2)}, u32[]{:S(2)}) %collective-permute-start.2) | collective-permute-done | bytes 131104 | tf_op jit(solution)/shard_map/ppermute | solution.py:366
  9.4 1.4 %collective-permute-done.3.old_got_ref = bf16[128,256]{1,0:T(8,128)(2,1)S(1)} collective-permute-done((bf16[128,256]{1,0:T(8,128)(2,1)S(1)}, bf16[128,256]{1,0:T(8,128)(2,1)S(1)}, u32[]{:S(2)}, u32[]{:S(2)}) %collective-permute-start.3) | collective-permute-done | bytes 65568 | tf_op jit(solution)/shard_map/ppermute | solution.py:368
  10.8 1.1 %shard_map.94 = (bf16[4,512,384]{2,1,0:T(8,128)(2,1)S(1)}, f32[4,512,128]{2,1,0:T(8,128)S(1)}) custom-call(bf16[128,1024]{1,0:T(8,128)(2,1)S(1)} %get-tuple-element.31.q_keep_ref, bf16[128,1024]{1,0:T(8,128)(2,1)S(1)} %collective-permute-done.q_got_ref, bf16[128,512]{1,0:T(8,128)(2,1)S(1)} %get-tuple-element.33.kv_keep_ref, ...), custom_call_target="tpu_custom_call" | custom-call | flops 268435456 | bytes 1048576 | tf_op jit(solution)/shard_map/pallas_call | solution.py:36
  12.3 0.7 %shard_map.95 = (bf16[256,1024]{1,0:T(8,128)(2,1)S(1)}, f32[16,128]{1,0:T(8,128)S(1)}) custom-call(bf16[4,512,384]{2,1,0:T(8,128)(2,1)S(1)} %get-tuple-element.36.weight_ref, f32[4,512,128]{2,1,0:T(8,128)S(1)} %get-tuple-element.37.scale_ref, bf16[128,512]{1,0:T(8,128)(2,1)S(1)} %get-tuple-element.33.kv_keep_ref, ...), custom_call_target="tpu_custom_call" | custom-call | flops 268435456 | bytes 1048576 | tf_op jit(solution)/shard_map/pallas_call | solution.py:36
  13.0 2.8 %collective-permute-start.5 = (bf16[256,1024]{1,0:T(8,128)(2,1)S(1)}, bf16[256,1024]{1,0:T(8,128)(2,1)S(1)}, u32[]{:S(2)}, u32[]{:S(2)}) collective-permute-start(bf16[256,1024]{1,0:T(8,128)(2,1)S(1)} %get-tuple-element.39), channel_id=1, source_target_pairs={{0,16},{4,0},{8,20},{12,4},{16,24},{20,8},{24,28},{28,12},{1,17},{... | collective-permute-start | bytes 1572872 | tf_op jit(solution)/shard_map/ppermute | solution.py:400
  15.8 1.6 %collective-permute-start.6 = (f32[16,128]{1,0:T(8,128)S(1)}, f32[16,128]{1,0:T(8,128)S(1)}, u32[]{:S(2)}, u32[]{:S(2)}) collective-permute-start(f32[16,128]{1,0:T(8,128)S(1)} %get-tuple-element.40.a_ref), channel_id=1, source_target_pairs={{0,1},{1,0},{2,3},{3,2},{4,5},{5,4},{6,7},{7,6},{8,9},{9,8},{10,11... | collective-permute-start | bytes 24584 | tf_op jit(solution)/shard_map/ppermute | solution.py:402
  17.4 2.1 %collective-permute-done.6.b_ref = f32[16,128]{1,0:T(8,128)S(1)} collective-permute-done((f32[16,128]{1,0:T(8,128)S(1)}, f32[16,128]{1,0:T(8,128)S(1)}, u32[]{:S(2)}, u32[]{:S(2)}) %collective-permute-start.6) | collective-permute-done | bytes 8224 | tf_op jit(solution)/shard_map/ppermute | solution.py:402
  19.5 2.6 %collective-permute-start.7 = (f32[16,128]{1,0:T(8,128)S(1)}, f32[16,128]{1,0:T(8,128)S(1)}, u32[]{:S(2)}, u32[]{:S(2)}) collective-permute-start(f32[16,128]{1,0:T(8,128)S(1)} %shard_map.96.a_ref), channel_id=1, source_target_pairs={{0,2},{1,3},{2,0},{3,1},{4,6},{5,7},{6,4},{7,5},{8,10},{9,11},{10,... | collective-permute-start | bytes 24584 | tf_op jit(solution)/shard_map/ppermute | solution.py:402
  22.1 2.0 %collective-permute-done.7.b_ref = f32[16,128]{1,0:T(8,128)S(1)} collective-permute-done((f32[16,128]{1,0:T(8,128)S(1)}, f32[16,128]{1,0:T(8,128)S(1)}, u32[]{:S(2)}, u32[]{:S(2)}) %collective-permute-start.7) | collective-permute-done | bytes 8224 | tf_op jit(solution)/shard_map/ppermute | solution.py:402
  24.0 0.6 %collective-permute-start.8 = (f32[16,128]{1,0:T(8,128)S(1)}, f32[16,128]{1,0:T(8,128)S(1)}, u32[]{:S(2)}, u32[]{:S(2)}) collective-permute-start(f32[16,128]{1,0:T(8,128)S(1)} %shard_map.97), channel_id=1, source_target_pairs={{0,16},{4,0},{8,20},{12,4},{16,24},{20,8},{24,28},{28,12},{1,17},{... | collective-permute-start | bytes 24584 | tf_op jit(solution)/shard_map/ppermute | solution.py:404
  24.6 2.4 %shard_map.98 = (bf16[8,256,512]{2,1,0:T(8,128)(2,1)S(1)}, bf16[8,128,512]{2,1,0:T(8,128)(2,1)S(1)}, f32[256,1024]{1,0:T(8,128)S(1)}, f32[1,1024]{1,0:T(1,128)S(1)}, f32[1,1024]{1,0:T(1,128)S(1)}) custom-call(f32[16,256]{1,0:T(8,128)} %refs_0_.1, f32[16,256]{1,0:T(8,128)} %refs_1_.1, bf16[256,128]{1,0:T(8,128)(2,1)} %refs_2_.1, bf16[256,128]{1,0:T(8,128)(2,1)} %c_ref.3, ...), custom_call_target="tpu_custom_call" | custom-call | flops 1073741824 | bytes 1048576 | tf_op jit(solution)/shard_map/pallas_call | solution.py:36
  27.0 0.9 %collective-permute-done.8.sums_ref = f32[16,128]{1,0:T(8,128)S(1)} collective-permute-done((f32[16,128]{1,0:T(8,128)S(1)}, f32[16,128]{1,0:T(8,128)S(1)}, u32[]{:S(2)}, u32[]{:S(2)}) %collective-permute-start.8) | collective-permute-done | bytes 8224 | tf_op jit(solution)/shard_map/ppermute | solution.py:404
  28.9 0.9 %collective-permute-done.9.got_ref = bf16[144,512]{1,0:T(8,128)(2,1)S(1)} collective-permute-done((bf16[144,512]{1,0:T(8,128)(2,1)S(1)}, bf16[144,512]{1,0:T(8,128)(2,1)S(1)}, u32[]{:S(2)}, u32[]{:S(2)}) %collective-permute-start.9) | collective-permute-done | bytes 147488 | tf_op jit(solution)/shard_map/ppermute | solution.py:356
  29.9 2.3 %collective-permute-start.12 = (bf16[144,512]{1,0:T(8,128)(2,1)S(1)}, bf16[144,512]{1,0:T(8,128)(2,1)S(1)}, u32[]{:S(2)}, u32[]{:S(2)}) collective-permute-start(bf16[144,512]{1,0:T(8,128)(2,1)S(1)} %get-tuple-element.51), channel_id=1, source_target_pairs={{0,24},{4,28},{8,0},{12,4},{16,20},{20,16},{24,8},{28,12},{1,25},{... | collective-permute-start | bytes 442376 | tf_op jit(solution)/shard_map/ppermute | solution.py:412
  32.6 1.1 %collective-permute-start.10 = (bf16[144,512]{1,0:T(8,128)(2,1)S(1)}, bf16[144,512]{1,0:T(8,128)(2,1)S(1)}, u32[]{:S(2)}, u32[]{:S(2)}) collective-permute-start(bf16[144,512]{1,0:T(8,128)(2,1)S(1)} %get-tuple-element.51), channel_id=1, source_target_pairs={{0,8},{4,12},{8,16},{12,20},{16,24},{20,28},{24,0},{28,4},{1,9},{5... | collective-permute-start | bytes 442376 | tf_op jit(solution)/shard_map/ppermute | solution.py:412
  33.7 2.9 %collective-permute-done.12.both_ref = bf16[144,512]{1,0:T(8,128)(2,1)S(1)} collective-permute-done((bf16[144,512]{1,0:T(8,128)(2,1)S(1)}, bf16[144,512]{1,0:T(8,128)(2,1)S(1)}, u32[]{:S(2)}, u32[]{:S(2)}) %collective-permute-start.12) | collective-permute-done | bytes 147488 | tf_op jit(solution)/shard_map/ppermute | solution.py:412
  36.5 4.5 %collective-permute-done.11.outer_ref = bf16[144,512]{1,0:T(8,128)(2,1)S(1)} collective-permute-done((bf16[144,512]{1,0:T(8,128)(2,1)S(1)}, bf16[144,512]{1,0:T(8,128)(2,1)S(1)}, u32[]{:S(2)}, u32[]{:S(2)}) %collective-permute-start.11) | collective-permute-done | bytes 147488 | tf_op jit(solution)/shard_map/ppermute | solution.py:412
  41.3 0.7 %shard_map.101 = (f32[256,512]{1,0:T(8,128)S(1)}, f32[256,512]{1,0:T(8,128)S(1)}) custom-call(bf16[256,512]{1,0:T(8,128)(2,1)S(1)} %get-tuple-element.43.x_keep_ref, bf16[256,512]{1,0:T(8,128)(2,1)S(1)} %get-tuple-element.44.x_send_ref, bf16[8,256,512]{2,1,0:T(8,128)(2,1)S(1)} %get-tuple-element.45.mix_ref, f32[1,1024]{1,0:T(1,128)S(1)} %get-tuple-element.46.skip_ref), custom_call_target="tpu_custom_call" | custom-call | flops 536870912 | bytes 1048576 | tf_op jit(solution)/shard_map/pallas_call | solution.py:36
  42.6 1.0 %shard_map.105 = bf16[256,1024]{1,0:T(8,128)(2,1)} custom-call(f32[256,512]{1,0:T(8,128)S(1)} %get-tuple-element.47.local_ref, f32[256,1024]{1,0:T(8,128)S(1)} %get-tuple-element.48.scale_ref, bf16[256,128]{1,0:T(8,128)(2,1)S(1)} %copy-done, bf16[128,512]{1,0:T(8,128)(2,1)S(1)} %collective-permute-done.13.enter_ref, bf16[256,512]{1,0:T(8,128)(2,1)S(1)} %shard_map.104.refs_0_), custom_call_target="tpu_custom_call" | custom-call | flops 134217728 | bytes 1048576 | tf_op jit(solution)/shard_map/pallas_call | solution.py:36
  (23 shorter events, 3.2 us)
Async XLA Ops:
  1.0 9.8 %collective-permute-start = (bf16[128,1024]{1,0:T(8,128)(2,1)S(1)}, bf16[128,1024]{1,0:T(8,128)(2,1)S(1)}, u32[]{:S(2)}, u32[]{:S(2)}) collective-permute-start(bf16[128,1024]{1,0:T(8,128)(2,1)S(1)} %get-tuple-element.32), channel_id=1, source_target_pairs={{0,4},{4,0},{8,12},{12,8},{16,20},{20,16},{24,28},{28,24},{1,5},{5... | collective-permute-start | bytes 786440 | tf_op jit(solution)/shard_map/ppermute | solution.py:356
  2.5 3.0 %collective-permute-start.1 = (bf16[128,512]{1,0:T(8,128)(2,1)S(1)}, bf16[128,512]{1,0:T(8,128)(2,1)S(1)}, u32[]{:S(2)}, u32[]{:S(2)}) collective-permute-start(bf16[128,512]{1,0:T(8,128)(2,1)S(1)} %get-tuple-element.34), channel_id=1, source_target_pairs={{0,4},{4,0},{8,12},{12,8},{16,20},{20,16},{24,28},{28,24},{1,5},{5... | collective-permute-start | bytes 393224 | tf_op jit(solution)/shard_map/ppermute | solution.py:356
  2.5 6.9 %collective-permute-start.2 = (bf16[128,512]{1,0:T(8,128)(2,1)S(1)}, bf16[128,512]{1,0:T(8,128)(2,1)S(1)}, u32[]{:S(2)}, u32[]{:S(2)}) collective-permute-start(bf16[128,512]{1,0:T(8,128)(2,1)S(1)} %get-tuple-element.33.kv_keep_ref), channel_id=1, source_target_pairs={{0,8},{4,12},{8,16},{12,20},{16,24},{20,28},{24,4},{28,0},{1,9},{5... | collective-permute-start | bytes 393224 | tf_op jit(solution)/shard_map/ppermute | solution.py:366
  5.5 5.3 %collective-permute-start.3 = (bf16[128,256]{1,0:T(8,128)(2,1)S(1)}, bf16[128,256]{1,0:T(8,128)(2,1)S(1)}, u32[]{:S(2)}, u32[]{:S(2)}) collective-permute-start(bf16[128,256]{1,0:T(8,128)(2,1)S(1)} %get-tuple-element.35), channel_id=1, source_target_pairs={{0,8},{4,12},{8,16},{12,20},{16,24},{20,28},{24,4},{28,0},{1,9},{5... | collective-permute-start | bytes 196616 | tf_op jit(solution)/shard_map/ppermute | solution.py:368
  7.0 5.3 %collective-permute-start.4 = (bf16[128,256]{1,0:T(8,128)(2,1)S(1)}, bf16[128,256]{1,0:T(8,128)(2,1)S(1)}, u32[]{:S(2)}, u32[]{:S(2)}) collective-permute-start(bf16[128,256]{1,0:T(8,128)(2,1)S(1)} %get-tuple-element.38), channel_id=1, source_target_pairs={{0,8},{4,12},{8,16},{12,20},{16,24},{20,28},{24,4},{28,0},{1,9},{5... | collective-permute-start | bytes 196616 | tf_op jit(solution)/shard_map/ppermute | solution.py:369
  13.0 14.9 %copy-start.1 = (f32[1024]{0:T(1024)S(1)}, f32[1024]{0:T(1024)}, u32[]{:S(2)}) copy-start(f32[1024]{0:T(1024)} %param.12) | copy-start | bytes 12292
  13.0 14.9 %collective-permute-start.5 = (bf16[256,1024]{1,0:T(8,128)(2,1)S(1)}, bf16[256,1024]{1,0:T(8,128)(2,1)S(1)}, u32[]{:S(2)}, u32[]{:S(2)}) collective-permute-start(bf16[256,1024]{1,0:T(8,128)(2,1)S(1)} %get-tuple-element.39), channel_id=1, source_target_pairs={{0,16},{4,0},{8,20},{12,4},{16,24},{20,8},{24,28},{28,12},{1,17},{... | collective-permute-start | bytes 1572872 | tf_op jit(solution)/shard_map/ppermute | solution.py:400
  15.8 3.7 %collective-permute-start.6 = (f32[16,128]{1,0:T(8,128)S(1)}, f32[16,128]{1,0:T(8,128)S(1)}, u32[]{:S(2)}, u32[]{:S(2)}) collective-permute-start(f32[16,128]{1,0:T(8,128)S(1)} %get-tuple-element.40.a_ref), channel_id=1, source_target_pairs={{0,1},{1,0},{2,3},{3,2},{4,5},{5,4},{6,7},{7,6},{8,9},{9,8},{10,11... | collective-permute-start | bytes 24584 | tf_op jit(solution)/shard_map/ppermute | solution.py:402
  19.5 4.5 %collective-permute-start.7 = (f32[16,128]{1,0:T(8,128)S(1)}, f32[16,128]{1,0:T(8,128)S(1)}, u32[]{:S(2)}, u32[]{:S(2)}) collective-permute-start(f32[16,128]{1,0:T(8,128)S(1)} %shard_map.96.a_ref), channel_id=1, source_target_pairs={{0,2},{1,3},{2,0},{3,1},{4,6},{5,7},{6,4},{7,5},{8,10},{9,11},{10,... | collective-permute-start | bytes 24584 | tf_op jit(solution)/shard_map/ppermute | solution.py:402
  24.0 3.9 %collective-permute-start.8 = (f32[16,128]{1,0:T(8,128)S(1)}, f32[16,128]{1,0:T(8,128)S(1)}, u32[]{:S(2)}, u32[]{:S(2)}) collective-permute-start(f32[16,128]{1,0:T(8,128)S(1)} %shard_map.97), channel_id=1, source_target_pairs={{0,16},{4,0},{8,20},{12,4},{16,24},{20,8},{24,28},{28,12},{1,17},{... | collective-permute-start | bytes 24584 | tf_op jit(solution)/shard_map/ppermute | solution.py:404
  28.4 1.4 %collective-permute-start.9 = (bf16[144,512]{1,0:T(8,128)(2,1)S(1)}, bf16[144,512]{1,0:T(8,128)(2,1)S(1)}, u32[]{:S(2)}, u32[]{:S(2)}) collective-permute-start(bf16[144,512]{1,0:T(8,128)(2,1)S(1)} %get-tuple-element.50), channel_id=1, source_target_pairs={{0,4},{4,0},{8,12},{12,8},{16,20},{20,16},{24,28},{28,24},{1,5},{5... | collective-permute-start | bytes 442376 | tf_op jit(solution)/shard_map/ppermute | solution.py:356
  28.9 13.0 %copy-start = (bf16[256,128]{1,0:T(8,128)(2,1)S(1)}, bf16[256,128]{1,0:T(8,128)(2,1)}, u32[]{:S(2)}) copy-start(bf16[256,128]{1,0:T(8,128)(2,1)} %c_ref.3) | copy-start | bytes 196612
  29.9 6.6 %collective-permute-start.12 = (bf16[144,512]{1,0:T(8,128)(2,1)S(1)}, bf16[144,512]{1,0:T(8,128)(2,1)S(1)}, u32[]{:S(2)}, u32[]{:S(2)}) collective-permute-start(bf16[144,512]{1,0:T(8,128)(2,1)S(1)} %get-tuple-element.51), channel_id=1, source_target_pairs={{0,24},{4,28},{8,0},{12,4},{16,20},{20,16},{24,8},{28,12},{1,25},{... | collective-permute-start | bytes 442376 | tf_op jit(solution)/shard_map/ppermute | solution.py:412
  32.3 8.8 %collective-permute-start.11 = (bf16[144,512]{1,0:T(8,128)(2,1)S(1)}, bf16[144,512]{1,0:T(8,128)(2,1)S(1)}, u32[]{:S(2)}, u32[]{:S(2)}) collective-permute-start(bf16[144,512]{1,0:T(8,128)(2,1)S(1)} %get-tuple-element.51), channel_id=1, source_target_pairs={{0,16},{4,20},{8,24},{12,28},{16,0},{20,4},{24,8},{28,12},{1,17},{... | collective-permute-start | bytes 442376 | tf_op jit(solution)/shard_map/ppermute | solution.py:412
  32.6 8.4 %collective-permute-start.10 = (bf16[144,512]{1,0:T(8,128)(2,1)S(1)}, bf16[144,512]{1,0:T(8,128)(2,1)S(1)}, u32[]{:S(2)}, u32[]{:S(2)}) collective-permute-start(bf16[144,512]{1,0:T(8,128)(2,1)S(1)} %get-tuple-element.51), channel_id=1, source_target_pairs={{0,8},{4,12},{8,16},{12,20},{16,24},{20,28},{24,0},{28,4},{1,9},{5... | collective-permute-start | bytes 442376 | tf_op jit(solution)/shard_map/ppermute | solution.py:412
  41.2 1.4 %collective-permute-start.13 = (bf16[128,512]{1,0:T(8,128)(2,1)S(1)}, bf16[128,512]{1,0:T(8,128)(2,1)S(1)}, u32[]{:S(2)}, u32[]{:S(2)}) collective-permute-start(bf16[128,512]{1,0:T(8,128)(2,1)S(1)} %get-tuple-element.54), channel_id=1, source_target_pairs={{0,4},{4,0},{8,12},{12,8},{16,20},{20,16},{24,28},{28,24},{1,5},{5... | collective-permute-start | bytes 393224 | tf_op jit(solution)/shard_map/ppermute | solution.py:356

commit v8 on v7

--- a/solution.py
+++ b/solution.py
@@ -13,7 +13,7 @@
 HDIM = 128
 SDIM = 64
 STATE = 128
-TAIL = 16
+TAIL = 8
 
 F32 = jnp.float32
 BF16 = jnp.bfloat16
@@ -51,19 +51,23 @@
         copy.wait()
 
 
-def part_kernel(kv_ref, k_ref, v_ref):
+def part_kernel(got_ref, keep_v_ref, k_ref, v_ref, both_ref):
     width = k_ref.shape[1]
-    k_ref[...] = kv_ref[:, :width]
-    v_ref[...] = kv_ref[:, width:]
-
-
-def pack_kv_kernel(k_ref, v_ref, keep_ref, send_ref):
+    k_ref[...] = got_ref[:, :width]
+    v_ref[...] = got_ref[:, width:]
+    both_ref[:, :width] = keep_v_ref[...]
+    both_ref[:, width:] = got_ref[:, width:]
+
+
+def pack_kv_kernel(k_ref, v_ref, keep_k_ref, keep_v_ref, send_ref):
     width = k_ref.shape[2]
     mine = lax.axis_index("seq") % 2
-    copies = []
-    for slot, out_ref in ((1 - mine, keep_ref), (mine, send_ref)):
-        copies.append((k_ref.at[slot], out_ref.at[:, :width]))
-        copies.append((v_ref.at[slot], out_ref.at[:, width:]))
+    copies = [
+        (k_ref.at[1 - mine], keep_k_ref),
+        (k_ref.at[mine], send_ref.at[:, :width]),
+        (v_ref.at[mine], send_ref.at[:, width:]),
+        (v_ref.at[1 - mine], keep_v_ref),
+    ]
     pl.run_scoped(functools.partial(gather, copies), pltpu.SemaphoreType.DMA((4,)))
 
 
@@ -157,10 +161,10 @@
 
 
 def score_kernel(
-    q_keep_ref, q_got_ref, kv_keep_ref, kv_got_ref, old_keep_ref, old_got_ref, weight_ref, scale_ref
+    q_keep_ref, q_got_ref, keep_ref, got_ref, old_keep_ref, old_got_ref, weight_ref, scale_ref
 ):
     blk, feat = q_keep_ref.shape
-    kv_local = kv_keep_ref.shape[1] // (2 * HDIM)
+    kv_local = keep_ref.shape[1] // HDIM
     group = feat // HDIM // kv_local
     late, old_late, has_old = places()
     rows = lax.broadcasted_iota(jnp.int32, (group * blk, blk), 0) % blk
@@ -170,7 +174,7 @@
     near_ok = (cols >= 0) & has_old
     factor = math.log2(math.e) / math.sqrt(HDIM)
     for g in range(kv_local):
-        keys = pick(old_keep_ref, old_got_ref, old_late, g) + pick(kv_keep_ref, kv_got_ref, late, g)
+        keys = pick(old_keep_ref, old_got_ref, old_late, g) + pick(keep_ref, got_ref, late, g)
         heads = [pick(q_keep_ref, q_got_ref, late, g * group + i) for i in range(group)]
         for part in range(2):
             query = jnp.concatenate([h[part] for h in heads], 0)
@@ -187,20 +191,28 @@
             scale_ref[2 * g + part] = jnp.broadcast_to(total, (group * blk, HDIM))
 
 
-def value_kernel(
-    weight_ref, scale_ref, kv_keep_ref, kv_got_ref, old_keep_ref, old_got_ref, out_ref, sums_ref
-):
-    blk = kv_keep_ref.shape[0]
-    kv_local = kv_keep_ref.shape[1] // (2 * HDIM)
+def own_value_kernel(weight_ref, keep_ref, got_ref, sum_ref):
+    blk = keep_ref.shape[0]
+    late = places()[0]
+    for g in range(keep_ref.shape[1] // HDIM):
+        vals = pick(keep_ref, got_ref, late, g)
+        for part in range(2):
+            values = jnp.concatenate(vals[: part + 1], 0)
+            sum_ref[2 * g + part] = dot(weight_ref[2 * g + part, :, (2 - part) * blk :], values)
+
+
+def value_kernel(weight_ref, scale_ref, sum_ref, old_ref, out_ref, sums_ref):
+    blk = old_ref.shape[0]
+    kv_local = old_ref.shape[1] // (2 * HDIM)
     group = out_ref.shape[1] // HDIM // kv_local
-    late, old_late, _ = places()
+    old_late = places()[1]
     squares = [jnp.zeros((blk, 1), F32)] * 2
     for g in range(kv_local):
-        c = kv_local + g
-        vals = pick(old_keep_ref, old_got_ref, old_late, c, g) + pick(kv_keep_ref, kv_got_ref, late, c)
+        vals = pick(old_ref, old_ref, old_late, g, kv_local + g)
         for part in range(2):
-            values = jnp.concatenate(vals[part : part + 3], 0)
-            result = dot(weight_ref[2 * g + part], values) * scale_ref[2 * g + part]
+            at = 2 * g + part
+            result = dot(weight_ref[at, :, : (2 - part) * blk], jnp.concatenate(vals[part:], 0))
+            result = (result + sum_ref[at]) * scale_ref[at]
             result = result.astype(BF16)
             wide = result.astype(F32)
             square = jnp.sum(wide * wide, axis=1, keepdims=True)
@@ -356,17 +368,23 @@
         return lax.ppermute(block, "seq", [(i, i ^ (1 << bit)) for i in every])
 
     width = 2 * kv_width
-    kv_keep, kv_send = call(
-        pack_kv_kernel, [((blk, width), BF16)] * 2, (keys, values), spaces=[pltpu.HBM] * 2
+    half_kv = ((blk, kv_width), BF16)
+    keep_k, keep_v, kv_send = call(
+        pack_kv_kernel,
+        [half_kv, half_kv, ((blk, width), BF16)],
+        (keys, values),
+        spaces=[pltpu.HBM] * 2,
     )
     q_keep, q_send = call(pack_q_kernel, [((blk, feat), BF16)] * 2, (query,), spaces=[pltpu.HBM])
     chips = seq_count // 2
     onward = [(i, i + 2) for i in range(seq_count - 2)] + [(seq_count - 2, 1), (seq_count - 1, 0)]
     kv_got = swap(kv_send, 0)
-    old_keep = lax.ppermute(kv_keep, "seq", onward)
-    got_k, got_v = call(part_kernel, [((blk, kv_width), BF16)] * 2, (kv_got,))
+    old_keep = lax.ppermute(keep_k, "seq", onward)
+    got_k, got_v, both_v = call(
+        part_kernel, [half_kv, half_kv, ((blk, width), BF16)], (kv_got, keep_v)
+    )
     old_k = lax.ppermute(got_k, "seq", onward)
-    old_v = lax.ppermute(got_v, "seq", onward)
+    old_v = lax.ppermute(both_v, "seq", onward)
     q_got = swap(q_send, 0)
 
     mix, b_weighted, scale, tot, skip_row = call(
@@ -387,13 +405,19 @@
     weights, scales = call(
         score_kernel,
         [((2 * kv_width // HDIM, rows_at_once, 3 * blk), BF16), ((2 * kv_width // HDIM, rows_at_once, HDIM), F32)],
-        (q_keep, q_got, kv_keep, kv_got, old_keep, old_k),
+        (q_keep, q_got, keep_k, got_k, old_keep, old_k),
         flops=1 << 28,
+    )
+    (own_sum,) = call(
+        own_value_kernel,
+        [((2 * kv_width // HDIM, rows_at_once, HDIM), F32)],
+        (weights, keep_v, got_v),
+        flops=1 << 27,
     )
     attended, sums = call(
         value_kernel,
         [((toks, feat), BF16), ((16, blk), F32)],
-        (weights, scales, kv_keep, kv_got, old_keep, old_v),
+        (weights, scales, own_sum, old_v),
         flops=1 << 28,
     )
     to_home = [(i, i // 2 + (1 - i % 2) * chips) for i in every]

time: 43.8 us -> 45.8 us (1.046)
  waiting for transfers between devices: 16.2 us -> 19.4 us
  starting transfers between devices: 17.9 us -> 16.5 us
    ppermute x2, waiting for transfers between devices: 1.21 us -> 3.07 us  [the longest x1 3.07 us: layer(): old_keep = lax.ppermute(keep_k, 'seq', onward)]
    ppermute x4, waiting for transfers between devices: 1.27 us -> 2.58 us  [swap(): return lax.ppermute(block, 'seq', [(i, i ^ 1 << bit) for i in every])]
    ppermute x1, starting transfers between devices: 2.8 us -> 2.08 us  [layer(): rows = lax.ppermute(attended, 'seq', to_home)]
    pallas_call x15 -> x16, Pallas kernels: 9.33 us -> 9.56 us  [call(): pl.pallas_call(kernel, out_shape=[jax.ShapeDtypeStruct(s, d) for s, d in...]
  transfers between devices with their start and end apart: 14 -> 14, of which waited for: 10 -> 10; matrix products, arithmetic and copies ran while one was open for 0% -> 0% of each run, Pallas kernels for 13% -> 14%
where the time goes in v8:
time: 45.8 us; the launch traced here: 45.6 us
  waiting for transfers between devices  19.4 us (42%)
  starting transfers between devices  16.5 us (36%)
  Pallas kernels  9.56 us (21%)
    pallas_call x16, Pallas kernels, call(): pl.pallas_call(kernel, out_shape=[jax.ShapeDtypeStruct(s, d) for s, d in...  9.56 us
    ppermute x3, waiting for transfers between devices, hop(): return lax.ppermute(block, 'seq', route)  7.04 us
    ppermute x2, starting transfers between devices, layer(): lax.ppermute(sums, 'head', [(i, i ^ 1 << bit) for i in range(head_count)])  4.17 us
    ppermute x2, waiting for transfers between devices, layer(): lax.ppermute(sums, 'head', [(i, i ^ 1 << bit) for i in range(head_count)])  4.03 us
    ppermute x3, starting transfers between devices, hop(): return lax.ppermute(block, 'seq', route)  3.32 us
    ppermute x1, waiting for transfers between devices, layer(): old_keep = lax.ppermute(keep_k, 'seq', onward)  3.07 us
    ppermute x1, starting transfers between devices, layer(): old_v = lax.ppermute(both_v, 'seq', onward)  2.68 us
    ppermute x4, waiting for transfers between devices, swap(): return lax.ppermute(block, 'seq', [(i, i ^ 1 << bit) for i in every])  2.58 us
  transfers between devices with their start and end apart: 14, of which 10 were waited for; matrix products, arithmetic and copies ran while one was open for 0% of the time, Pallas kernels for 14%

profile of v8, /device:TPU:0, one launch (start us, length us, event | category | flops | bytes accessed | tf_op | source)
XLA Modules:
  0.0 45.6 jit_solution(1588740753898580304)
XLA Ops:
  0.0 1.0 %shard_map.91 = (bf16[128,1024]{1,0:T(8,128)(2,1)S(1)}, bf16[128,1024]{1,0:T(8,128)(2,1)S(1)}) custom-call(bf16[2,128,1024]{2,1,0:T(8,128)(2,1)} %q_ref.1), custom_call_target="tpu_custom_call" | custom-call | flops 1 | bytes 1048576 | tf_op jit(solution)/shard_map/pallas_call | solution.py:36
  1.5 0.9 %shard_map.92 = (bf16[128,256]{1,0:T(8,128)(2,1)S(1)}, bf16[128,256]{1,0:T(8,128)(2,1)S(1)}, bf16[128,512]{1,0:T(8,128)(2,1)S(1)}) custom-call(bf16[2,128,256]{2,1,0:T(8,128)(2,1)} %k_ref.1, bf16[2,128,256]{2,1,0:T(8,128)(2,1)} %v_ref.1), custom_call_target="tpu_custom_call" | custom-call | flops 1 | bytes 1048576 | tf_op jit(solution)/shard_map/pallas_call | solution.py:36
  2.5 1.3 %collective-permute-done.1.got_ref = bf16[128,512]{1,0:T(8,128)(2,1)S(1)} collective-permute-done((bf16[128,512]{1,0:T(8,128)(2,1)S(1)}, bf16[128,512]{1,0:T(8,128)(2,1)S(1)}, u32[]{:S(2)}, u32[]{:S(2)}) %collective-permute-start.1) | collective-permute-done | bytes 131104 | tf_op jit(solution)/shard_map/ppermute | solution.py:368
  3.8 2.7 %collective-permute-start.4 = (bf16[128,512]{1,0:T(8,128)(2,1)S(1)}, bf16[128,512]{1,0:T(8,128)(2,1)S(1)}, u32[]{:S(2)}, u32[]{:S(2)}) collective-permute-start(bf16[128,512]{1,0:T(8,128)(2,1)S(1)} %get-tuple-element.42), channel_id=1, source_target_pairs={{0,8},{4,12},{8,16},{12,20},{16,24},{20,28},{24,4},{28,0},{1,9},{5... | collective-permute-start | bytes 393224 | tf_op jit(solution)/shard_map/ppermute | solution.py:387
  6.5 1.5 %collective-permute-start.2 = (bf16[128,256]{1,0:T(8,128)(2,1)S(1)}, bf16[128,256]{1,0:T(8,128)(2,1)S(1)}, u32[]{:S(2)}, u32[]{:S(2)}) collective-permute-start(bf16[128,256]{1,0:T(8,128)(2,1)S(1)} %get-tuple-element.35.keep_ref), channel_id=1, source_target_pairs={{0,8},{4,12},{8,16},{12,20},{16,24},{20,28},{24,4},{28,0},{1,9},{5... | collective-permute-start | bytes 196616 | tf_op jit(solution)/shard_map/ppermute | solution.py:382
  8.0 1.5 %collective-permute-start.3 = (bf16[128,256]{1,0:T(8,128)(2,1)S(1)}, bf16[128,256]{1,0:T(8,128)(2,1)S(1)}, u32[]{:S(2)}, u32[]{:S(2)}) collective-permute-start(bf16[128,256]{1,0:T(8,128)(2,1)S(1)} %get-tuple-element.38.got_ref), channel_id=1, source_target_pairs={{0,8},{4,12},{8,16},{12,20},{16,24},{20,28},{24,4},{28,0},{1,9},{5... | collective-permute-start | bytes 196616 | tf_op jit(solution)/shard_map/ppermute | solution.py:386
  9.5 3.1 %collective-permute-done.2.old_keep_ref = bf16[128,256]{1,0:T(8,128)(2,1)S(1)} collective-permute-done((bf16[128,256]{1,0:T(8,128)(2,1)S(1)}, bf16[128,256]{1,0:T(8,128)(2,1)S(1)}, u32[]{:S(2)}, u32[]{:S(2)}) %collective-permute-start.2) | collective-permute-done | bytes 65568 | tf_op jit(solution)/shard_map/ppermute | solution.py:382
  12.6 1.4 %collective-permute-done.3.old_got_ref = bf16[128,256]{1,0:T(8,128)(2,1)S(1)} collective-permute-done((bf16[128,256]{1,0:T(8,128)(2,1)S(1)}, bf16[128,256]{1,0:T(8,128)(2,1)S(1)}, u32[]{:S(2)}, u32[]{:S(2)}) %collective-permute-start.3) | collective-permute-done | bytes 65568 | tf_op jit(solution)/shard_map/ppermute | solution.py:386
  14.0 1.1 %shard_map.94 = (bf16[4,512,384]{2,1,0:T(8,128)(2,1)S(1)}, f32[4,512,128]{2,1,0:T(8,128)S(1)}) custom-call(bf16[128,1024]{1,0:T(8,128)(2,1)S(1)} %get-tuple-element.33.q_keep_ref, bf16[128,1024]{1,0:T(8,128)(2,1)S(1)} %collective-permute-done.q_got_ref, bf16[128,256]{1,0:T(8,128)(2,1)S(1)} %get-tuple-element.35.keep_ref, ...), custom_call_target="tpu_custom_call" | custom-call | flops 268435456 | bytes 1048576 | tf_op jit(solution)/shard_map/pallas_call | solution.py:36
  16.1 2.1 %collective-permute-start.5 = (bf16[256,1024]{1,0:T(8,128)(2,1)S(1)}, bf16[256,1024]{1,0:T(8,128)(2,1)S(1)}, u32[]{:S(2)}, u32[]{:S(2)}) collective-permute-start(bf16[256,1024]{1,0:T(8,128)(2,1)S(1)} %get-tuple-element.43), channel_id=1, source_target_pairs={{0,16},{4,0},{8,20},{12,4},{16,24},{20,8},{24,28},{28,12},{1,17},{... | collective-permute-start | bytes 1572872 | tf_op jit(solution)/shard_map/ppermute | solution.py:424
  18.1 1.6 %collective-permute-start.6 = (f32[16,128]{1,0:T(8,128)S(1)}, f32[16,128]{1,0:T(8,128)S(1)}, u32[]{:S(2)}, u32[]{:S(2)}) collective-permute-start(f32[16,128]{1,0:T(8,128)S(1)} %get-tuple-element.44.a_ref), channel_id=1, source_target_pairs={{0,1},{1,0},{2,3},{3,2},{4,5},{5,4},{6,7},{7,6},{8,9},{9,8},{10,11... | collective-permute-start | bytes 24584 | tf_op jit(solution)/shard_map/ppermute | solution.py:426
  19.7 2.1 %collective-permute-done.6.b_ref = f32[16,128]{1,0:T(8,128)S(1)} collective-permute-done((f32[16,128]{1,0:T(8,128)S(1)}, f32[16,128]{1,0:T(8,128)S(1)}, u32[]{:S(2)}, u32[]{:S(2)}) %collective-permute-start.6) | collective-permute-done | bytes 8224 | tf_op jit(solution)/shard_map/ppermute | solution.py:426
  21.8 2.6 %collective-permute-start.7 = (f32[16,128]{1,0:T(8,128)S(1)}, f32[16,128]{1,0:T(8,128)S(1)}, u32[]{:S(2)}, u32[]{:S(2)}) collective-permute-start(f32[16,128]{1,0:T(8,128)S(1)} %shard_map.97.a_ref), channel_id=1, source_target_pairs={{0,2},{1,3},{2,0},{3,1},{4,6},{5,7},{6,4},{7,5},{8,10},{9,11},{10,... | collective-permute-start | bytes 24584 | tf_op jit(solution)/shard_map/ppermute | solution.py:426
  24.4 2.0 %collective-permute-done.7.b_ref = f32[16,128]{1,0:T(8,128)S(1)} collective-permute-done((f32[16,128]{1,0:T(8,128)S(1)}, f32[16,128]{1,0:T(8,128)S(1)}, u32[]{:S(2)}, u32[]{:S(2)}) %collective-permute-start.7) | collective-permute-done | bytes 8224 | tf_op jit(solution)/shard_map/ppermute | solution.py:426
  26.9 2.4 %shard_map.99 = (bf16[8,256,512]{2,1,0:T(8,128)(2,1)S(1)}, bf16[8,128,512]{2,1,0:T(8,128)(2,1)S(1)}, f32[256,1024]{1,0:T(8,128)S(1)}, f32[1,1024]{1,0:T(1,128)S(1)}, f32[1,1024]{1,0:T(1,128)S(1)}) custom-call(f32[16,256]{1,0:T(8,128)} %refs_0_.1, f32[16,256]{1,0:T(8,128)} %refs_1_.1, bf16[256,128]{1,0:T(8,128)(2,1)} %refs_2_.1, bf16[256,128]{1,0:T(8,128)(2,1)} %c_ref.3, ...), custom_call_target="tpu_custom_call" | custom-call | flops 1073741824 | bytes 1048576 | tf_op jit(solution)/shard_map/pallas_call | solution.py:36
  29.3 1.3 %collective-permute-done.8.sums_ref = f32[16,128]{1,0:T(8,128)S(1)} collective-permute-done((f32[16,128]{1,0:T(8,128)S(1)}, f32[16,128]{1,0:T(8,128)S(1)}, u32[]{:S(2)}, u32[]{:S(2)}) %collective-permute-start.8) | collective-permute-done | bytes 8224 | tf_op jit(solution)/shard_map/ppermute | solution.py:428
  31.7 0.9 %collective-permute-done.9.got_ref = bf16[136,512]{1,0:T(8,128)(2,1)S(1)} collective-permute-done((bf16[136,512]{1,0:T(8,128)(2,1)S(1)}, bf16[136,512]{1,0:T(8,128)(2,1)S(1)}, u32[]{:S(2)}, u32[]{:S(2)}) %collective-permute-start.9) | collective-permute-done | bytes 139296 | tf_op jit(solution)/shard_map/ppermute | solution.py:368
  32.7 1.9 %collective-permute-start.12 = (bf16[136,512]{1,0:T(8,128)(2,1)S(1)}, bf16[136,512]{1,0:T(8,128)(2,1)S(1)}, u32[]{:S(2)}, u32[]{:S(2)}) collective-permute-start(bf16[136,512]{1,0:T(8,128)(2,1)S(1)} %get-tuple-element.55), channel_id=1, source_target_pairs={{0,24},{4,28},{8,0},{12,4},{16,20},{20,16},{24,8},{28,12},{1,25},{... | collective-permute-start | bytes 417800 | tf_op jit(solution)/shard_map/ppermute | solution.py:436
  34.6 0.8 %collective-permute-start.11 = (bf16[136,512]{1,0:T(8,128)(2,1)S(1)}, bf16[136,512]{1,0:T(8,128)(2,1)S(1)}, u32[]{:S(2)}, u32[]{:S(2)}) collective-permute-start(bf16[136,512]{1,0:T(8,128)(2,1)S(1)} %get-tuple-element.55), channel_id=1, source_target_pairs={{0,16},{4,20},{8,24},{12,28},{16,0},{20,4},{24,8},{28,12},{1,17},{... | collective-permute-start | bytes 417800 | tf_op jit(solution)/shard_map/ppermute | solution.py:436
  35.3 0.6 %collective-permute-start.10 = (bf16[136,512]{1,0:T(8,128)(2,1)S(1)}, bf16[136,512]{1,0:T(8,128)(2,1)S(1)}, u32[]{:S(2)}, u32[]{:S(2)}) collective-permute-start(bf16[136,512]{1,0:T(8,128)(2,1)S(1)} %get-tuple-element.55), channel_id=1, source_target_pairs={{0,8},{4,12},{8,16},{12,20},{16,24},{20,28},{24,0},{28,4},{1,9},{5... | collective-permute-start | bytes 417800 | tf_op jit(solution)/shard_map/ppermute | solution.py:436
  36.0 2.7 %collective-permute-done.12.both_ref = bf16[136,512]{1,0:T(8,128)(2,1)S(1)} collective-permute-done((bf16[136,512]{1,0:T(8,128)(2,1)S(1)}, bf16[136,512]{1,0:T(8,128)(2,1)S(1)}, u32[]{:S(2)}, u32[]{:S(2)}) %collective-permute-start.12) | collective-permute-done | bytes 139296 | tf_op jit(solution)/shard_map/ppermute | solution.py:436
  38.7 4.3 %collective-permute-done.11.outer_ref = bf16[136,512]{1,0:T(8,128)(2,1)S(1)} collective-permute-done((bf16[136,512]{1,0:T(8,128)(2,1)S(1)}, bf16[136,512]{1,0:T(8,128)(2,1)S(1)}, u32[]{:S(2)}, u32[]{:S(2)}) %collective-permute-start.11) | collective-permute-done | bytes 139296 | tf_op jit(solution)/shard_map/ppermute | solution.py:436
  43.2 0.7 %shard_map.102 = (f32[256,512]{1,0:T(8,128)S(1)}, f32[256,512]{1,0:T(8,128)S(1)}) custom-call(bf16[256,512]{1,0:T(8,128)(2,1)S(1)} %get-tuple-element.47.x_keep_ref, bf16[256,512]{1,0:T(8,128)(2,1)S(1)} %get-tuple-element.48.x_send_ref, bf16[8,256,512]{2,1,0:T(8,128)(2,1)S(1)} %get-tuple-element.49.mix_ref, f32[1,1024]{1,0:T(1,128)S(1)} %get-tuple-element.50.skip_ref), custom_call_target="tpu_custom_call" | custom-call | flops 536870912 | bytes 1048576 | tf_op jit(solution)/shard_map/pallas_call | solution.py:36
  44.6 1.0 %shard_map.106 = bf16[256,1024]{1,0:T(8,128)(2,1)} custom-call(f32[256,512]{1,0:T(8,128)S(1)} %get-tuple-element.51.local_ref, f32[256,1024]{1,0:T(8,128)S(1)} %get-tuple-element.52.scale_ref, bf16[256,128]{1,0:T(8,128)(2,1)S(1)} %copy-done, bf16[128,512]{1,0:T(8,128)(2,1)S(1)} %collective-permute-done.13.enter_ref, bf16[256,512]{1,0:T(8,128)(2,1)S(1)} %shard_map.105.refs_0_), custom_call_target="tpu_custom_call" | custom-call | flops 134217728 | bytes 1048576 | tf_op jit(solution)/shard_map/pallas_call | solution.py:36
  (24 shorter events, 4.0 us)
Async XLA Ops:
  1.0 12.9 %collective-permute-start = (bf16[128,1024]{1,0:T(8,128)(2,1)S(1)}, bf16[128,1024]{1,0:T(8,128)(2,1)S(1)}, u32[]{:S(2)}, u32[]{:S(2)}) collective-permute-start(bf16[128,1024]{1,0:T(8,128)(2,1)S(1)} %get-tuple-element.34), channel_id=1, source_target_pairs={{0,4},{4,0},{8,12},{12,8},{16,20},{20,16},{24,28},{28,24},{1,5},{5... | collective-permute-start | bytes 786440 | tf_op jit(solution)/shard_map/ppermute | solution.py:368
  2.5 1.3 %collective-permute-start.1 = (bf16[128,512]{1,0:T(8,128)(2,1)S(1)}, bf16[128,512]{1,0:T(8,128)(2,1)S(1)}, u32[]{:S(2)}, u32[]{:S(2)}) collective-permute-start(bf16[128,512]{1,0:T(8,128)(2,1)S(1)} %get-tuple-element.36), channel_id=1, source_target_pairs={{0,4},{4,0},{8,12},{12,8},{16,20},{20,16},{24,28},{28,24},{1,5},{5... | collective-permute-start | bytes 393224 | tf_op jit(solution)/shard_map/ppermute | solution.py:368
  3.8 11.7 %collective-permute-start.4 = (bf16[128,512]{1,0:T(8,128)(2,1)S(1)}, bf16[128,512]{1,0:T(8,128)(2,1)S(1)}, u32[]{:S(2)}, u32[]{:S(2)}) collective-permute-start(bf16[128,512]{1,0:T(8,128)(2,1)S(1)} %get-tuple-element.42), channel_id=1, source_target_pairs={{0,8},{4,12},{8,16},{12,20},{16,24},{20,28},{24,4},{28,0},{1,9},{5... | collective-permute-start | bytes 393224 | tf_op jit(solution)/shard_map/ppermute | solution.py:387
  6.5 6.1 %collective-permute-start.2 = (bf16[128,256]{1,0:T(8,128)(2,1)S(1)}, bf16[128,256]{1,0:T(8,128)(2,1)S(1)}, u32[]{:S(2)}, u32[]{:S(2)}) collective-permute-start(bf16[128,256]{1,0:T(8,128)(2,1)S(1)} %get-tuple-element.35.keep_ref), channel_id=1, source_target_pairs={{0,8},{4,12},{8,16},{12,20},{16,24},{20,28},{24,4},{28,0},{1,9},{5... | collective-permute-start | bytes 196616 | tf_op jit(solution)/shard_map/ppermute | solution.py:382
  8.0 6.0 %collective-permute-start.3 = (bf16[128,256]{1,0:T(8,128)(2,1)S(1)}, bf16[128,256]{1,0:T(8,128)(2,1)S(1)}, u32[]{:S(2)}, u32[]{:S(2)}) collective-permute-start(bf16[128,256]{1,0:T(8,128)(2,1)S(1)} %get-tuple-element.38.got_ref), channel_id=1, source_target_pairs={{0,8},{4,12},{8,16},{12,20},{16,24},{20,28},{24,4},{28,0},{1,9},{5... | collective-permute-start | bytes 196616 | tf_op jit(solution)/shard_map/ppermute | solution.py:386
  16.1 14.6 %copy-start.1 = (f32[1024]{0:T(1024)S(1)}, f32[1024]{0:T(1024)}, u32[]{:S(2)}) copy-start(f32[1024]{0:T(1024)} %param.12) | copy-start | bytes 12292
  16.1 14.6 %collective-permute-start.5 = (bf16[256,1024]{1,0:T(8,128)(2,1)S(1)}, bf16[256,1024]{1,0:T(8,128)(2,1)S(1)}, u32[]{:S(2)}, u32[]{:S(2)}) collective-permute-start(bf16[256,1024]{1,0:T(8,128)(2,1)S(1)} %get-tuple-element.43), channel_id=1, source_target_pairs={{0,16},{4,0},{8,20},{12,4},{16,24},{20,8},{24,28},{28,12},{1,17},{... | collective-permute-start | bytes 1572872 | tf_op jit(solution)/shard_map/ppermute | solution.py:424
  18.1 3.7 %collective-permute-start.6 = (f32[16,128]{1,0:T(8,128)S(1)}, f32[16,128]{1,0:T(8,128)S(1)}, u32[]{:S(2)}, u32[]{:S(2)}) collective-permute-start(f32[16,128]{1,0:T(8,128)S(1)} %get-tuple-element.44.a_ref), channel_id=1, source_target_pairs={{0,1},{1,0},{2,3},{3,2},{4,5},{5,4},{6,7},{7,6},{8,9},{9,8},{10,11... | collective-permute-start | bytes 24584 | tf_op jit(solution)/shard_map/ppermute | solution.py:426
  21.8 4.5 %collective-permute-start.7 = (f32[16,128]{1,0:T(8,128)S(1)}, f32[16,128]{1,0:T(8,128)S(1)}, u32[]{:S(2)}, u32[]{:S(2)}) collective-permute-start(f32[16,128]{1,0:T(8,128)S(1)} %shard_map.97.a_ref), channel_id=1, source_target_pairs={{0,2},{1,3},{2,0},{3,1},{4,6},{5,7},{6,4},{7,5},{8,10},{9,11},{10,... | collective-permute-start | bytes 24584 | tf_op jit(solution)/shard_map/ppermute | solution.py:426
  26.4 4.3 %collective-permute-start.8 = (f32[16,128]{1,0:T(8,128)S(1)}, f32[16,128]{1,0:T(8,128)S(1)}, u32[]{:S(2)}, u32[]{:S(2)}) collective-permute-start(f32[16,128]{1,0:T(8,128)S(1)} %shard_map.98), channel_id=1, source_target_pairs={{0,16},{4,0},{8,20},{12,4},{16,24},{20,8},{24,28},{28,12},{1,17},{... | collective-permute-start | bytes 24584 | tf_op jit(solution)/shard_map/ppermute | solution.py:428
  31.1 1.4 %collective-permute-start.9 = (bf16[136,512]{1,0:T(8,128)(2,1)S(1)}, bf16[136,512]{1,0:T(8,128)(2,1)S(1)}, u32[]{:S(2)}, u32[]{:S(2)}) collective-permute-start(bf16[136,512]{1,0:T(8,128)(2,1)S(1)} %get-tuple-element.54), channel_id=1, source_target_pairs={{0,4},{4,0},{8,12},{12,8},{16,20},{20,16},{24,28},{28,24},{1,5},{5... | collective-permute-start | bytes 417800 | tf_op jit(solution)/shard_map/ppermute | solution.py:368
  31.7 12.3 %copy-start = (bf16[256,128]{1,0:T(8,128)(2,1)S(1)}, bf16[256,128]{1,0:T(8,128)(2,1)}, u32[]{:S(2)}) copy-start(bf16[256,128]{1,0:T(8,128)(2,1)} %c_ref.3) | copy-start | bytes 196612
  32.7 6.0 %collective-permute-start.12 = (bf16[136,512]{1,0:T(8,128)(2,1)S(1)}, bf16[136,512]{1,0:T(8,128)(2,1)S(1)}, u32[]{:S(2)}, u32[]{:S(2)}) collective-permute-start(bf16[136,512]{1,0:T(8,128)(2,1)S(1)} %get-tuple-element.55), channel_id=1, source_target_pairs={{0,24},{4,28},{8,0},{12,4},{16,20},{20,16},{24,8},{28,12},{1,25},{... | collective-permute-start | bytes 417800 | tf_op jit(solution)/shard_map/ppermute | solution.py:436
  34.6 8.4 %collective-permute-start.11 = (bf16[136,512]{1,0:T(8,128)(2,1)S(1)}, bf16[136,512]{1,0:T(8,128)(2,1)S(1)}, u32[]{:S(2)}, u32[]{:S(2)}) collective-permute-start(bf16[136,512]{1,0:T(8,128)(2,1)S(1)} %get-tuple-element.55), channel_id=1, source_target_pairs={{0,16},{4,20},{8,24},{12,28},{16,0},{20,4},{24,8},{28,12},{1,17},{... | collective-permute-start | bytes 417800 | tf_op jit(solution)/shard_map/ppermute | solution.py:436
  35.3 7.7 %collective-permute-start.10 = (bf16[136,512]{1,0:T(8,128)(2,1)S(1)}, bf16[136,512]{1,0:T(8,128)(2,1)S(1)}, u32[]{:S(2)}, u32[]{:S(2)}) collective-permute-start(bf16[136,512]{1,0:T(8,128)(2,1)S(1)} %get-tuple-element.55), channel_id=1, source_target_pairs={{0,8},{4,12},{8,16},{12,20},{16,24},{20,28},{24,0},{28,4},{1,9},{5... | collective-permute-start | bytes 417800 | tf_op jit(solution)/shard_map/ppermute | solution.py:436
  43.2 1.4 %collective-permute-start.13 = (bf16[128,512]{1,0:T(8,128)(2,1)S(1)}, bf16[128,512]{1,0:T(8,128)(2,1)S(1)}, u32[]{:S(2)}, u32[]{:S(2)}) collective-permute-start(bf16[128,512]{1,0:T(8,128)(2,1)S(1)} %get-tuple-element.58), channel_id=1, source_target_pairs={{0,4},{4,0},{8,12},{12,8},{16,20},{20,16},{24,28},{28,24},{1,5},{5... | collective-permute-start | bytes 393224 | tf_op jit(solution)/shard_map/ppermute | solution.py:368

commit v9 on v8

--- a/solution.py
+++ b/solution.py
@@ -201,27 +201,28 @@
             sum_ref[2 * g + part] = dot(weight_ref[2 * g + part, :, (2 - part) * blk :], values)
 
 
-def value_kernel(weight_ref, scale_ref, sum_ref, old_ref, out_ref, sums_ref):
+def value_kernel(weight_ref, scale_ref, sum_ref, old_ref, out_ref):
     blk = old_ref.shape[0]
     kv_local = old_ref.shape[1] // (2 * HDIM)
     group = out_ref.shape[1] // HDIM // kv_local
     old_late = places()[1]
-    squares = [jnp.zeros((blk, 1), F32)] * 2
     for g in range(kv_local):
         vals = pick(old_ref, old_ref, old_late, g, kv_local + g)
         for part in range(2):
             at = 2 * g + part
             result = dot(weight_ref[at, :, : (2 - part) * blk], jnp.concatenate(vals[part:], 0))
-            result = (result + sum_ref[at]) * scale_ref[at]
-            result = result.astype(BF16)
-            wide = result.astype(F32)
-            square = jnp.sum(wide * wide, axis=1, keepdims=True)
+            result = ((result + sum_ref[at]) * scale_ref[at]).astype(BF16)
             for i in range(group):
-                at = slice((g * group + i) * HDIM, (g * group + i + 1) * HDIM)
-                out_ref[part * blk : (part + 1) * blk, at] = result[i * blk : (i + 1) * blk]
-                squares[part] = squares[part] + square[i * blk : (i + 1) * blk]
+                lanes = slice((g * group + i) * HDIM, (g * group + i + 1) * HDIM)
+                out_ref[part * blk : (part + 1) * blk, lanes] = result[i * blk : (i + 1) * blk]
+
+
+def square_kernel(rows_ref, sums_ref):
+    blk = rows_ref.shape[0] // 2
     for part in range(2):
-        turned = jnp.transpose(jnp.broadcast_to(squares[part], (blk, blk)))
+        rows = rows_ref[part * blk : (part + 1) * blk].astype(F32)
+        total = jnp.sum(rows * rows, axis=1, keepdims=True)
+        turned = jnp.transpose(jnp.broadcast_to(total, (blk, blk)))
         sums_ref[part * 8 : part * 8 + 8] = turned[:8]
 
 
@@ -254,9 +255,12 @@
     for part in range(2):
         at = slice(part * blk, (part + 1) * blk)
         sums = sums_ref[part * 8 : part * 8 + 1]
-        mean = jnp.transpose(jnp.broadcast_to(sums, (blk, blk))) / (HEADS * HDIM)
-        inv = lax.rsqrt(mean + 1e-06)[:, :1]
-        x_ref[at, :] = (rows_ref[at, lanes].astype(F32) * gain * inv).astype(BF16)
+        mean = jnp.transpose(jnp.broadcast_to(sums, (HDIM, blk))) / (HEADS * HDIM)
+        inv = lax.rsqrt(mean + 1e-06)
+        rows = rows_ref[at, lanes].astype(F32) * gain
+        for p in range(pairs):
+            tile = slice(p * HDIM, (p + 1) * HDIM)
+            x_ref[at, tile] = (rows[:, tile] * inv).astype(BF16)
     for p in range(pairs):
         at = slice(p * HDIM, (p + 1) * HDIM)
         state = dot(bw_ref[side * pairs + p], spread(x_ref[:, at]))
@@ -414,12 +418,10 @@
         (weights, keep_v, got_v),
         flops=1 << 27,
     )
-    attended, sums = call(
-        value_kernel,
-        [((toks, feat), BF16), ((16, blk), F32)],
-        (weights, scales, own_sum, old_v),
-        flops=1 << 28,
-    )
+    (attended,) = call(
+        value_kernel, [((toks, feat), BF16)], (weights, scales, own_sum, old_v), flops=1 << 28
+    )
+    (sums,) = call(square_kernel, [((16, blk), F32)], (attended,), flops=1 << 22)
     to_home = [(i, i // 2 + (1 - i % 2) * chips) for i in every]
     rows = lax.ppermute(attended, "seq", to_home)
     for bit in range(head_count.bit_length() - 1):

time: 45.8 us -> 45.6 us (level)
    pallas_call x16 -> x17, Pallas kernels: 9.56 us -> 9.49 us  [call(): pl.pallas_call(kernel, out_shape=[jax.ShapeDtypeStruct(s, d) for s, d in...]
where the time goes in v9:
time: 45.6 us; the launch traced here: 45.4 us
  waiting for transfers between devices  19.2 us (42%)
  starting transfers between devices  16.5 us (36%)
  Pallas kernels  9.49 us (21%)
    pallas_call x17, Pallas kernels, call(): pl.pallas_call(kernel, out_shape=[jax.ShapeDtypeStruct(s, d) for s, d in...  9.49 us
    ppermute x3, waiting for transfers between devices, hop(): return lax.ppermute(block, 'seq', route)  7.04 us
    ppermute x2, starting transfers between devices, layer(): lax.ppermute(sums, 'head', [(i, i ^ 1 << bit) for i in range(head_count)])  4.22 us
    ppermute x2, waiting for transfers between devices, layer(): lax.ppermute(sums, 'head', [(i, i ^ 1 << bit) for i in range(head_count)])  4.03 us
    ppermute x3, starting transfers between devices, hop(): return lax.ppermute(block, 'seq', route)  3.32 us
    ppermute x1, waiting for transfers between devices, layer(): old_keep = lax.ppermute(keep_k, 'seq', onward)  3.07 us
    ppermute x1, starting transfers between devices, layer(): old_v = lax.ppermute(both_v, 'seq', onward)  2.68 us
    ppermute x4, waiting for transfers between devices, swap(): return lax.ppermute(block, 'seq', [(i, i ^ 1 << bit) for i in every])  2.64 us
  transfers between devices with their start and end apart: 14, of which 10 were waited for; matrix products, arithmetic and copies ran while one was open for 0% of the time, Pallas kernels for 14%

profile of v9, /device:TPU:0, one launch (start us, length us, event | category | flops | bytes accessed | tf_op | source)
XLA Modules:
  0.0 45.4 jit_solution(16470372147164942661)
XLA Ops:
  0.0 1.0 %shard_map.91 = (bf16[128,1024]{1,0:T(8,128)(2,1)S(1)}, bf16[128,1024]{1,0:T(8,128)(2,1)S(1)}) custom-call(bf16[2,128,1024]{2,1,0:T(8,128)(2,1)} %q_ref.1), custom_call_target="tpu_custom_call" | custom-call | flops 1 | bytes 1048576 | tf_op jit(solution)/shard_map/pallas_call | solution.py:36
  1.5 0.9 %shard_map.92 = (bf16[128,256]{1,0:T(8,128)(2,1)S(1)}, bf16[128,256]{1,0:T(8,128)(2,1)S(1)}, bf16[128,512]{1,0:T(8,128)(2,1)S(1)}) custom-call(bf16[2,128,256]{2,1,0:T(8,128)(2,1)} %k_ref.1, bf16[2,128,256]{2,1,0:T(8,128)(2,1)} %v_ref.1), custom_call_target="tpu_custom_call" | custom-call | flops 1 | bytes 1048576 | tf_op jit(solution)/shard_map/pallas_call | solution.py:36
  2.5 1.3 %collective-permute-done.1.got_ref = bf16[128,512]{1,0:T(8,128)(2,1)S(1)} collective-permute-done((bf16[128,512]{1,0:T(8,128)(2,1)S(1)}, bf16[128,512]{1,0:T(8,128)(2,1)S(1)}, u32[]{:S(2)}, u32[]{:S(2)}) %collective-permute-start.1) | collective-permute-done | bytes 131104 | tf_op jit(solution)/shard_map/ppermute | solution.py:372
  3.8 2.7 %collective-permute-start.4 = (bf16[128,512]{1,0:T(8,128)(2,1)S(1)}, bf16[128,512]{1,0:T(8,128)(2,1)S(1)}, u32[]{:S(2)}, u32[]{:S(2)}) collective-permute-start(bf16[128,512]{1,0:T(8,128)(2,1)S(1)} %get-tuple-element.40), channel_id=1, source_target_pairs={{0,8},{4,12},{8,16},{12,20},{16,24},{20,28},{24,4},{28,0},{1,9},{5... | collective-permute-start | bytes 393224 | tf_op jit(solution)/shard_map/ppermute | solution.py:391
  6.5 1.5 %collective-permute-start.2 = (bf16[128,256]{1,0:T(8,128)(2,1)S(1)}, bf16[128,256]{1,0:T(8,128)(2,1)S(1)}, u32[]{:S(2)}, u32[]{:S(2)}) collective-permute-start(bf16[128,256]{1,0:T(8,128)(2,1)S(1)} %get-tuple-element.33.keep_ref), channel_id=1, source_target_pairs={{0,8},{4,12},{8,16},{12,20},{16,24},{20,28},{24,4},{28,0},{1,9},{5... | collective-permute-start | bytes 196616 | tf_op jit(solution)/shard_map/ppermute | solution.py:386
  8.0 1.5 %collective-permute-start.3 = (bf16[128,256]{1,0:T(8,128)(2,1)S(1)}, bf16[128,256]{1,0:T(8,128)(2,1)S(1)}, u32[]{:S(2)}, u32[]{:S(2)}) collective-permute-start(bf16[128,256]{1,0:T(8,128)(2,1)S(1)} %get-tuple-element.36.got_ref), channel_id=1, source_target_pairs={{0,8},{4,12},{8,16},{12,20},{16,24},{20,28},{24,4},{28,0},{1,9},{5... | collective-permute-start | bytes 196616 | tf_op jit(solution)/shard_map/ppermute | solution.py:390
  9.5 3.1 %collective-permute-done.2.old_keep_ref = bf16[128,256]{1,0:T(8,128)(2,1)S(1)} collective-permute-done((bf16[128,256]{1,0:T(8,128)(2,1)S(1)}, bf16[128,256]{1,0:T(8,128)(2,1)S(1)}, u32[]{:S(2)}, u32[]{:S(2)}) %collective-permute-start.2) | collective-permute-done | bytes 65568 | tf_op jit(solution)/shard_map/ppermute | solution.py:386
  12.6 1.4 %collective-permute-done.3.old_got_ref = bf16[128,256]{1,0:T(8,128)(2,1)S(1)} collective-permute-done((bf16[128,256]{1,0:T(8,128)(2,1)S(1)}, bf16[128,256]{1,0:T(8,128)(2,1)S(1)}, u32[]{:S(2)}, u32[]{:S(2)}) %collective-permute-start.3) | collective-permute-done | bytes 65568 | tf_op jit(solution)/shard_map/ppermute | solution.py:390
  14.0 1.2 %shard_map.94 = (bf16[4,512,384]{2,1,0:T(8,128)(2,1)S(1)}, f32[4,512,128]{2,1,0:T(8,128)S(1)}) custom-call(bf16[128,1024]{1,0:T(8,128)(2,1)S(1)} %get-tuple-element.31.q_keep_ref, bf16[128,1024]{1,0:T(8,128)(2,1)S(1)} %collective-permute-done.q_got_ref, bf16[128,256]{1,0:T(8,128)(2,1)S(1)} %get-tuple-element.33.keep_ref, ...), custom_call_target="tpu_custom_call" | custom-call | flops 268435456 | bytes 1048576 | tf_op jit(solution)/shard_map/pallas_call | solution.py:36
  15.9 2.1 %collective-permute-start.5 = (bf16[256,1024]{1,0:T(8,128)(2,1)S(1)}, bf16[256,1024]{1,0:T(8,128)(2,1)S(1)}, u32[]{:S(2)}, u32[]{:S(2)}) collective-permute-start(bf16[256,1024]{1,0:T(8,128)(2,1)S(1)} %shard_map.96.rows_ref), channel_id=1, source_target_pairs={{0,16},{4,0},{8,20},{12,4},{16,24},{20,8},{24,28},{28,12},{1,17},{... | collective-permute-start | bytes 1572872 | tf_op jit(solution)/shard_map/ppermute | solution.py:426
  18.2 1.6 %collective-permute-start.6 = (f32[16,128]{1,0:T(8,128)S(1)}, f32[16,128]{1,0:T(8,128)S(1)}, u32[]{:S(2)}, u32[]{:S(2)}) collective-permute-start(f32[16,128]{1,0:T(8,128)S(1)} %shard_map.97.a_ref), channel_id=1, source_target_pairs={{0,1},{1,0},{2,3},{3,2},{4,5},{5,4},{6,7},{7,6},{8,9},{9,8},{10,11... | collective-permute-start | bytes 24584 | tf_op jit(solution)/shard_map/ppermute | solution.py:428
  19.8 2.1 %collective-permute-done.6.b_ref = f32[16,128]{1,0:T(8,128)S(1)} collective-permute-done((f32[16,128]{1,0:T(8,128)S(1)}, f32[16,128]{1,0:T(8,128)S(1)}, u32[]{:S(2)}, u32[]{:S(2)}) %collective-permute-start.6) | collective-permute-done | bytes 8224 | tf_op jit(solution)/shard_map/ppermute | solution.py:428
  21.9 2.6 %collective-permute-start.7 = (f32[16,128]{1,0:T(8,128)S(1)}, f32[16,128]{1,0:T(8,128)S(1)}, u32[]{:S(2)}, u32[]{:S(2)}) collective-permute-start(f32[16,128]{1,0:T(8,128)S(1)} %shard_map.98.a_ref), channel_id=1, source_target_pairs={{0,2},{1,3},{2,0},{3,1},{4,6},{5,7},{6,4},{7,5},{8,10},{9,11},{10,... | collective-permute-start | bytes 24584 | tf_op jit(solution)/shard_map/ppermute | solution.py:428
  24.5 2.0 %collective-permute-done.7.b_ref = f32[16,128]{1,0:T(8,128)S(1)} collective-permute-done((f32[16,128]{1,0:T(8,128)S(1)}, f32[16,128]{1,0:T(8,128)S(1)}, u32[]{:S(2)}, u32[]{:S(2)}) %collective-permute-start.7) | collective-permute-done | bytes 8224 | tf_op jit(solution)/shard_map/ppermute | solution.py:428
  27.1 2.4 %shard_map.100 = (bf16[8,256,512]{2,1,0:T(8,128)(2,1)S(1)}, bf16[8,128,512]{2,1,0:T(8,128)(2,1)S(1)}, f32[256,1024]{1,0:T(8,128)S(1)}, f32[1,1024]{1,0:T(1,128)S(1)}, f32[1,1024]{1,0:T(1,128)S(1)}) custom-call(f32[16,256]{1,0:T(8,128)} %refs_0_.1, f32[16,256]{1,0:T(8,128)} %refs_1_.1, bf16[256,128]{1,0:T(8,128)(2,1)} %refs_2_.1, bf16[256,128]{1,0:T(8,128)(2,1)} %c_ref.3, ...), custom_call_target="tpu_custom_call" | custom-call | flops 1073741824 | bytes 1048576 | tf_op jit(solution)/shard_map/pallas_call | solution.py:36
  29.5 1.0 %collective-permute-done.8.sums_ref = f32[16,128]{1,0:T(8,128)S(1)} collective-permute-done((f32[16,128]{1,0:T(8,128)S(1)}, f32[16,128]{1,0:T(8,128)S(1)}, u32[]{:S(2)}, u32[]{:S(2)}) %collective-permute-start.8) | collective-permute-done | bytes 8224 | tf_op jit(solution)/shard_map/ppermute | solution.py:430
  31.4 0.9 %collective-permute-done.9.got_ref = bf16[136,512]{1,0:T(8,128)(2,1)S(1)} collective-permute-done((bf16[136,512]{1,0:T(8,128)(2,1)S(1)}, bf16[136,512]{1,0:T(8,128)(2,1)S(1)}, u32[]{:S(2)}, u32[]{:S(2)}) %collective-permute-start.9) | collective-permute-done | bytes 139296 | tf_op jit(solution)/shard_map/ppermute | solution.py:372
  32.5 1.9 %collective-permute-start.12 = (bf16[136,512]{1,0:T(8,128)(2,1)S(1)}, bf16[136,512]{1,0:T(8,128)(2,1)S(1)}, u32[]{:S(2)}, u32[]{:S(2)}) collective-permute-start(bf16[136,512]{1,0:T(8,128)(2,1)S(1)} %get-tuple-element.51), channel_id=1, source_target_pairs={{0,24},{4,28},{8,0},{12,4},{16,20},{20,16},{24,8},{28,12},{1,25},{... | collective-permute-start | bytes 417800 | tf_op jit(solution)/shard_map/ppermute | solution.py:438
  34.4 0.8 %collective-permute-start.11 = (bf16[136,512]{1,0:T(8,128)(2,1)S(1)}, bf16[136,512]{1,0:T(8,128)(2,1)S(1)}, u32[]{:S(2)}, u32[]{:S(2)}) collective-permute-start(bf16[136,512]{1,0:T(8,128)(2,1)S(1)} %get-tuple-element.51), channel_id=1, source_target_pairs={{0,16},{4,20},{8,24},{12,28},{16,0},{20,4},{24,8},{28,12},{1,17},{... | collective-permute-start | bytes 417800 | tf_op jit(solution)/shard_map/ppermute | solution.py:438
  35.2 0.6 %collective-permute-start.10 = (bf16[136,512]{1,0:T(8,128)(2,1)S(1)}, bf16[136,512]{1,0:T(8,128)(2,1)S(1)}, u32[]{:S(2)}, u32[]{:S(2)}) collective-permute-start(bf16[136,512]{1,0:T(8,128)(2,1)S(1)} %get-tuple-element.51), channel_id=1, source_target_pairs={{0,8},{4,12},{8,16},{12,20},{16,24},{20,28},{24,0},{28,4},{1,9},{5... | collective-permute-start | bytes 417800 | tf_op jit(solution)/shard_map/ppermute | solution.py:438
  35.8 2.7 %collective-permute-done.12.both_ref = bf16[136,512]{1,0:T(8,128)(2,1)S(1)} collective-permute-done((bf16[136,512]{1,0:T(8,128)(2,1)S(1)}, bf16[136,512]{1,0:T(8,128)(2,1)S(1)}, u32[]{:S(2)}, u32[]{:S(2)}) %collective-permute-start.12) | collective-permute-done | bytes 139296 | tf_op jit(solution)/shard_map/ppermute | solution.py:438
  38.5 4.3 %collective-permute-done.11.outer_ref = bf16[136,512]{1,0:T(8,128)(2,1)S(1)} collective-permute-done((bf16[136,512]{1,0:T(8,128)(2,1)S(1)}, bf16[136,512]{1,0:T(8,128)(2,1)S(1)}, u32[]{:S(2)}, u32[]{:S(2)}) %collective-permute-start.11) | collective-permute-done | bytes 139296 | tf_op jit(solution)/shard_map/ppermute | solution.py:438
  43.1 0.7 %shard_map.103 = (f32[256,512]{1,0:T(8,128)S(1)}, f32[256,512]{1,0:T(8,128)S(1)}) custom-call(bf16[256,512]{1,0:T(8,128)(2,1)S(1)} %get-tuple-element.43.x_keep_ref, bf16[256,512]{1,0:T(8,128)(2,1)S(1)} %get-tuple-element.44.x_send_ref, bf16[8,256,512]{2,1,0:T(8,128)(2,1)S(1)} %get-tuple-element.45.mix_ref, f32[1,1024]{1,0:T(1,128)S(1)} %get-tuple-element.46.skip_ref), custom_call_target="tpu_custom_call" | custom-call | flops 536870912 | bytes 1048576 | tf_op jit(solution)/shard_map/pallas_call | solution.py:36
  44.4 1.0 %shard_map.107 = bf16[256,1024]{1,0:T(8,128)(2,1)} custom-call(f32[256,512]{1,0:T(8,128)S(1)} %get-tuple-element.47.local_ref, f32[256,1024]{1,0:T(8,128)S(1)} %get-tuple-element.48.scale_ref, bf16[256,128]{1,0:T(8,128)(2,1)S(1)} %copy-done, bf16[128,512]{1,0:T(8,128)(2,1)S(1)} %collective-permute-done.13.enter_ref, bf16[256,512]{1,0:T(8,128)(2,1)S(1)} %shard_map.106.refs_0_), custom_call_target="tpu_custom_call" | custom-call | flops 134217728 | bytes 1048576 | tf_op jit(solution)/shard_map/pallas_call | solution.py:36
  (25 shorter events, 3.9 us)
Async XLA Ops:
  1.0 12.9 %collective-permute-start = (bf16[128,1024]{1,0:T(8,128)(2,1)S(1)}, bf16[128,1024]{1,0:T(8,128)(2,1)S(1)}, u32[]{:S(2)}, u32[]{:S(2)}) collective-permute-start(bf16[128,1024]{1,0:T(8,128)(2,1)S(1)} %get-tuple-element.32), channel_id=1, source_target_pairs={{0,4},{4,0},{8,12},{12,8},{16,20},{20,16},{24,28},{28,24},{1,5},{5... | collective-permute-start | bytes 786440 | tf_op jit(solution)/shard_map/ppermute | solution.py:372
  2.5 1.3 %collective-permute-start.1 = (bf16[128,512]{1,0:T(8,128)(2,1)S(1)}, bf16[128,512]{1,0:T(8,128)(2,1)S(1)}, u32[]{:S(2)}, u32[]{:S(2)}) collective-permute-start(bf16[128,512]{1,0:T(8,128)(2,1)S(1)} %get-tuple-element.34), channel_id=1, source_target_pairs={{0,4},{4,0},{8,12},{12,8},{16,20},{20,16},{24,28},{28,24},{1,5},{5... | collective-permute-start | bytes 393224 | tf_op jit(solution)/shard_map/ppermute | solution.py:372
  3.8 11.7 %collective-permute-start.4 = (bf16[128,512]{1,0:T(8,128)(2,1)S(1)}, bf16[128,512]{1,0:T(8,128)(2,1)S(1)}, u32[]{:S(2)}, u32[]{:S(2)}) collective-permute-start(bf16[128,512]{1,0:T(8,128)(2,1)S(1)} %get-tuple-element.40), channel_id=1, source_target_pairs={{0,8},{4,12},{8,16},{12,20},{16,24},{20,28},{24,4},{28,0},{1,9},{5... | collective-permute-start | bytes 393224 | tf_op jit(solution)/shard_map/ppermute | solution.py:391
  6.5 6.1 %collective-permute-start.2 = (bf16[128,256]{1,0:T(8,128)(2,1)S(1)}, bf16[128,256]{1,0:T(8,128)(2,1)S(1)}, u32[]{:S(2)}, u32[]{:S(2)}) collective-permute-start(bf16[128,256]{1,0:T(8,128)(2,1)S(1)} %get-tuple-element.33.keep_ref), channel_id=1, source_target_pairs={{0,8},{4,12},{8,16},{12,20},{16,24},{20,28},{24,4},{28,0},{1,9},{5... | collective-permute-start | bytes 196616 | tf_op jit(solution)/shard_map/ppermute | solution.py:386
  8.0 6.0 %collective-permute-start.3 = (bf16[128,256]{1,0:T(8,128)(2,1)S(1)}, bf16[128,256]{1,0:T(8,128)(2,1)S(1)}, u32[]{:S(2)}, u32[]{:S(2)}) collective-permute-start(bf16[128,256]{1,0:T(8,128)(2,1)S(1)} %get-tuple-element.36.got_ref), channel_id=1, source_target_pairs={{0,8},{4,12},{8,16},{12,20},{16,24},{20,28},{24,4},{28,0},{1,9},{5... | collective-permute-start | bytes 196616 | tf_op jit(solution)/shard_map/ppermute | solution.py:390
  15.9 14.6 %collective-permute-start.5 = (bf16[256,1024]{1,0:T(8,128)(2,1)S(1)}, bf16[256,1024]{1,0:T(8,128)(2,1)S(1)}, u32[]{:S(2)}, u32[]{:S(2)}) collective-permute-start(bf16[256,1024]{1,0:T(8,128)(2,1)S(1)} %shard_map.96.rows_ref), channel_id=1, source_target_pairs={{0,16},{4,0},{8,20},{12,4},{16,24},{20,8},{24,28},{28,12},{1,17},{... | collective-permute-start | bytes 1572872 | tf_op jit(solution)/shard_map/ppermute | solution.py:426
  18.2 12.3 %copy-start.1 = (f32[1024]{0:T(1024)S(1)}, f32[1024]{0:T(1024)}, u32[]{:S(2)}) copy-start(f32[1024]{0:T(1024)} %param.12) | copy-start | bytes 12292
  18.2 3.7 %collective-permute-start.6 = (f32[16,128]{1,0:T(8,128)S(1)}, f32[16,128]{1,0:T(8,128)S(1)}, u32[]{:S(2)}, u32[]{:S(2)}) collective-permute-start(f32[16,128]{1,0:T(8,128)S(1)} %shard_map.97.a_ref), channel_id=1, source_target_pairs={{0,1},{1,0},{2,3},{3,2},{4,5},{5,4},{6,7},{7,6},{8,9},{9,8},{10,11... | collective-permute-start | bytes 24584 | tf_op jit(solution)/shard_map/ppermute | solution.py:428
  21.9 4.5 %collective-permute-start.7 = (f32[16,128]{1,0:T(8,128)S(1)}, f32[16,128]{1,0:T(8,128)S(1)}, u32[]{:S(2)}, u32[]{:S(2)}) collective-permute-start(f32[16,128]{1,0:T(8,128)S(1)} %shard_map.98.a_ref), channel_id=1, source_target_pairs={{0,2},{1,3},{2,0},{3,1},{4,6},{5,7},{6,4},{7,5},{8,10},{9,11},{10,... | collective-permute-start | bytes 24584 | tf_op jit(solution)/shard_map/ppermute | solution.py:428
  26.5 4.0 %collective-permute-start.8 = (f32[16,128]{1,0:T(8,128)S(1)}, f32[16,128]{1,0:T(8,128)S(1)}, u32[]{:S(2)}, u32[]{:S(2)}) collective-permute-start(f32[16,128]{1,0:T(8,128)S(1)} %shard_map.99), channel_id=1, source_target_pairs={{0,16},{4,0},{8,20},{12,4},{16,24},{20,8},{24,28},{28,12},{1,17},{... | collective-permute-start | bytes 24584 | tf_op jit(solution)/shard_map/ppermute | solution.py:430
  30.9 1.4 %collective-permute-start.9 = (bf16[136,512]{1,0:T(8,128)(2,1)S(1)}, bf16[136,512]{1,0:T(8,128)(2,1)S(1)}, u32[]{:S(2)}, u32[]{:S(2)}) collective-permute-start(bf16[136,512]{1,0:T(8,128)(2,1)S(1)} %get-tuple-element.50), channel_id=1, source_target_pairs={{0,4},{4,0},{8,12},{12,8},{16,20},{20,16},{24,28},{28,24},{1,5},{5... | collective-permute-start | bytes 417800 | tf_op jit(solution)/shard_map/ppermute | solution.py:372
  31.4 12.3 %copy-start = (bf16[256,128]{1,0:T(8,128)(2,1)S(1)}, bf16[256,128]{1,0:T(8,128)(2,1)}, u32[]{:S(2)}) copy-start(bf16[256,128]{1,0:T(8,128)(2,1)} %c_ref.3) | copy-start | bytes 196612
  32.5 6.0 %collective-permute-start.12 = (bf16[136,512]{1,0:T(8,128)(2,1)S(1)}, bf16[136,512]{1,0:T(8,128)(2,1)S(1)}, u32[]{:S(2)}, u32[]{:S(2)}) collective-permute-start(bf16[136,512]{1,0:T(8,128)(2,1)S(1)} %get-tuple-element.51), channel_id=1, source_target_pairs={{0,24},{4,28},{8,0},{12,4},{16,20},{20,16},{24,8},{28,12},{1,25},{... | collective-permute-start | bytes 417800 | tf_op jit(solution)/shard_map/ppermute | solution.py:438
  34.4 8.4 %collective-permute-start.11 = (bf16[136,512]{1,0:T(8,128)(2,1)S(1)}, bf16[136,512]{1,0:T(8,128)(2,1)S(1)}, u32[]{:S(2)}, u32[]{:S(2)}) collective-permute-start(bf16[136,512]{1,0:T(8,128)(2,1)S(1)} %get-tuple-element.51), channel_id=1, source_target_pairs={{0,16},{4,20},{8,24},{12,28},{16,0},{20,4},{24,8},{28,12},{1,17},{... | collective-permute-start | bytes 417800 | tf_op jit(solution)/shard_map/ppermute | solution.py:438
  35.2 7.7 %collective-permute-start.10 = (bf16[136,512]{1,0:T(8,128)(2,1)S(1)}, bf16[136,512]{1,0:T(8,128)(2,1)S(1)}, u32[]{:S(2)}, u32[]{:S(2)}) collective-permute-start(bf16[136,512]{1,0:T(8,128)(2,1)S(1)} %get-tuple-element.51), channel_id=1, source_target_pairs={{0,8},{4,12},{8,16},{12,20},{16,24},{20,28},{24,0},{28,4},{1,9},{5... | collective-permute-start | bytes 417800 | tf_op jit(solution)/shard_map/ppermute | solution.py:438
  43.0 1.4 %collective-permute-start.13 = (bf16[128,512]{1,0:T(8,128)(2,1)S(1)}, bf16[128,512]{1,0:T(8,128)(2,1)S(1)}, u32[]{:S(2)}, u32[]{:S(2)}) collective-permute-start(bf16[128,512]{1,0:T(8,128)(2,1)S(1)} %get-tuple-element.54), channel_id=1, source_target_pairs={{0,4},{4,0},{8,12},{12,8},{16,20},{20,16},{24,28},{28,24},{1,5},{5... | collective-permute-start | bytes 393224 | tf_op jit(solution)/shard_map/ppermute | solution.py:372

commit v10 on v9

--- a/solution.py
+++ b/solution.py
@@ -306,7 +306,7 @@
     return ref[:, pl.ds(pl.multiple_of(side * half, half), half)]
 
 
-def chip_kernel(keep_ref, got_ref, tot_ref, early_ref, ahead_ref, low_ref, *refs):
+def chip_kernel(keep_ref, got_ref, tot_ref, early_ref, ahead_ref, low_ref, plain_ref, *refs):
     mine = lax.axis_index("seq") % 2
     late = mine == 1
     keep, here = keep_ref[...], half_of(tot_ref, mine)
@@ -316,6 +316,7 @@
     early_ref[...] = early
     ahead_ref[...] = jnp.where(late, there, here)
     pack_state(low_ref, total, here * there)
+    plain_ref[...] = total.astype(BF16)
     if refs:
         refs[0][...] = total
         refs[1][...] = here * there
@@ -323,7 +324,7 @@
 
 def stage_kernel(bit, first, total_ref, mine_ref, theirs_ref, *refs):
     upper = (lax.axis_index("seq") >> bit) % 2 == 1
-    enter_ref, carried_ref, low_ref, next_ref, running_ref = refs[-5:]
+    enter_ref, carried_ref, low_ref, plain_ref, next_ref, running_ref = refs[-6:]
     theirs, decay = unpack_state(theirs_ref)
     total, mine = total_ref[...], mine_ref[...]
     if first:
@@ -335,6 +336,7 @@
         carried_ref[...] = jnp.where(upper, carried * decay, carried)
     total = jnp.where(upper, mine * theirs + total, decay * total + theirs)
     pack_state(low_ref, total, mine * decay)
+    plain_ref[...] = total.astype(BF16)
     next_ref[...] = total
     running_ref[...] = mine * decay
 
@@ -345,7 +347,7 @@
     quarter, late = me >> shift, me % 2 == 1
     beside, by_inner = unpack_state(inner_ref)
     across, by_outer = unpack_state(outer_ref)
-    diagonal, _ = unpack_state(both_ref)
+    diagonal = both_ref[...].astype(F32)
     third, fourth = quarter == 2, quarter == 3
     one, zero = jnp.ones_like(by_inner), jnp.zeros_like(by_inner)
     enter = jnp.where(quarter > 0, one, zero) * beside
@@ -456,19 +458,20 @@
     )
     got = swap(send, 0)
     stages = range(1, bits - 2)
-    early, ahead, low, *held = call(
-        chip_kernel, [state, row, packed] + [state, row] * bool(stages), (keep, got, tot)
+    plain_state = ((STATE, half), BF16)
+    early, ahead, low, plain, *held = call(
+        chip_kernel, [state, row, packed, plain_state] + [state, row] * bool(stages), (keep, got, tot)
     )
     entered = ()
     for bit in stages:
         theirs = swap(low, bit)
-        *entered, low, total, running = call(
+        *entered, low, plain, total, running = call(
             functools.partial(stage_kernel, bit, bit == 1),
-            [state, row, packed, state, row],
+            [state, row, packed, plain_state, state, row],
             (*held, theirs, *entered),
         )
         held = (total, running)
-    both = hop(low, (3, 0, None, 1))
+    both = hop(plain, (3, 0, None, 1))
     inner = hop(low, (1, 2, 3, 0))
     outer = hop(low, (2, 3, 0, 1))
     own, give = call(

time: 45.6 us -> 45.9 us (level)
  starting transfers between devices: 16.5 us -> 18.7 us
  waiting for transfers between devices: 19.2 us -> 17.4 us
    ppermute x3, starting transfers between devices: 3.32 us -> 5.48 us  [hop(): return lax.ppermute(block, 'seq', route)]
    ppermute x3, waiting for transfers between devices: 7.04 us -> 5.16 us  [hop(): return lax.ppermute(block, 'seq', route)]
  transfers between devices with their start and end apart: 14 -> 14, of which waited for: 10 -> 9; matrix products, arithmetic and copies ran while one was open for 0% -> 0% of each run, Pallas kernels for 14% -> 14%
where the time goes in v10:
time: 45.9 us; the launch traced here: 45.7 us
  starting transfers between devices  18.7 us (41%)
  waiting for transfers between devices  17.4 us (38%)
  Pallas kernels  9.48 us (21%)
    pallas_call x17, Pallas kernels, call(): pl.pallas_call(kernel, out_shape=[jax.ShapeDtypeStruct(s, d) for s, d in...  9.48 us
    ppermute x3, starting transfers between devices, hop(): return lax.ppermute(block, 'seq', route)  5.48 us
    ppermute x3, waiting for transfers between devices, hop(): return lax.ppermute(block, 'seq', route)  5.16 us
    ppermute x2, starting transfers between devices, layer(): lax.ppermute(sums, 'head', [(i, i ^ 1 << bit) for i in range(head_count)])  4.22 us
    ppermute x2, waiting for transfers between devices, layer(): lax.ppermute(sums, 'head', [(i, i ^ 1 << bit) for i in range(head_count)])  4.03 us
    ppermute x1, waiting for transfers between devices, layer(): old_keep = lax.ppermute(keep_k, 'seq', onward)  3.07 us
    ppermute x1, starting transfers between devices, layer(): old_v = lax.ppermute(both_v, 'seq', onward)  2.68 us
    ppermute x4, waiting for transfers between devices, swap(): return lax.ppermute(block, 'seq', [(i, i ^ 1 << bit) for i in every])  2.64 us
  transfers between devices with their start and end apart: 14, of which 9 were waited for; matrix products, arithmetic and copies ran while one was open for 0% of the time, Pallas kernels for 14%

profile of v10, /device:TPU:0, one launch (start us, length us, event | category | flops | bytes accessed | tf_op | source)
XLA Modules:
  0.0 45.7 jit_solution(475802413895053422)
XLA Ops:
  0.0 1.0 %shard_map.91 = (bf16[128,1024]{1,0:T(8,128)(2,1)S(1)}, bf16[128,1024]{1,0:T(8,128)(2,1)S(1)}) custom-call(bf16[2,128,1024]{2,1,0:T(8,128)(2,1)} %q_ref.1), custom_call_target="tpu_custom_call" | custom-call | flops 1 | bytes 1048576 | tf_op jit(solution)/shard_map/pallas_call | solution.py:36
  1.0 0.5 %collective-permute-start = (bf16[128,1024]{1,0:T(8,128)(2,1)S(1)}, bf16[128,1024]{1,0:T(8,128)(2,1)S(1)}, u32[]{:S(2)}, u32[]{:S(2)}) collective-permute-start(bf16[128,1024]{1,0:T(8,128)(2,1)S(1)} %get-tuple-element.33), channel_id=1, source_target_pairs={{0,4},{4,0},{8,12},{12,8},{16,20},{20,16},{24,28},{28,24},{1,5},{5... | collective-permute-start | bytes 786440 | tf_op jit(solution)/shard_map/ppermute | solution.py:374
  1.5 0.9 %shard_map.92 = (bf16[128,256]{1,0:T(8,128)(2,1)S(1)}, bf16[128,256]{1,0:T(8,128)(2,1)S(1)}, bf16[128,512]{1,0:T(8,128)(2,1)S(1)}) custom-call(bf16[2,128,256]{2,1,0:T(8,128)(2,1)} %k_ref.1, bf16[2,128,256]{2,1,0:T(8,128)(2,1)} %v_ref.1), custom_call_target="tpu_custom_call" | custom-call | flops 1 | bytes 1048576 | tf_op jit(solution)/shard_map/pallas_call | solution.py:36
  2.5 1.3 %collective-permute-done.1.got_ref = bf16[128,512]{1,0:T(8,128)(2,1)S(1)} collective-permute-done((bf16[128,512]{1,0:T(8,128)(2,1)S(1)}, bf16[128,512]{1,0:T(8,128)(2,1)S(1)}, u32[]{:S(2)}, u32[]{:S(2)}) %collective-permute-start.1) | collective-permute-done | bytes 131104 | tf_op jit(solution)/shard_map/ppermute | solution.py:374
  3.8 2.7 %collective-permute-start.4 = (bf16[128,512]{1,0:T(8,128)(2,1)S(1)}, bf16[128,512]{1,0:T(8,128)(2,1)S(1)}, u32[]{:S(2)}, u32[]{:S(2)}) collective-permute-start(bf16[128,512]{1,0:T(8,128)(2,1)S(1)} %get-tuple-element.41), channel_id=1, source_target_pairs={{0,8},{4,12},{8,16},{12,20},{16,24},{20,28},{24,4},{28,0},{1,9},{5... | collective-permute-start | bytes 393224 | tf_op jit(solution)/shard_map/ppermute | solution.py:393
  6.5 1.5 %collective-permute-start.2 = (bf16[128,256]{1,0:T(8,128)(2,1)S(1)}, bf16[128,256]{1,0:T(8,128)(2,1)S(1)}, u32[]{:S(2)}, u32[]{:S(2)}) collective-permute-start(bf16[128,256]{1,0:T(8,128)(2,1)S(1)} %get-tuple-element.34.keep_ref), channel_id=1, source_target_pairs={{0,8},{4,12},{8,16},{12,20},{16,24},{20,28},{24,4},{28,0},{1,9},{5... | collective-permute-start | bytes 196616 | tf_op jit(solution)/shard_map/ppermute | solution.py:388
  8.0 1.5 %collective-permute-start.3 = (bf16[128,256]{1,0:T(8,128)(2,1)S(1)}, bf16[128,256]{1,0:T(8,128)(2,1)S(1)}, u32[]{:S(2)}, u32[]{:S(2)}) collective-permute-start(bf16[128,256]{1,0:T(8,128)(2,1)S(1)} %get-tuple-element.37.got_ref), channel_id=1, source_target_pairs={{0,8},{4,12},{8,16},{12,20},{16,24},{20,28},{24,4},{28,0},{1,9},{5... | collective-permute-start | bytes 196616 | tf_op jit(solution)/shard_map/ppermute | solution.py:392
  9.5 3.1 %collective-permute-done.2.old_keep_ref = bf16[128,256]{1,0:T(8,128)(2,1)S(1)} collective-permute-done((bf16[128,256]{1,0:T(8,128)(2,1)S(1)}, bf16[128,256]{1,0:T(8,128)(2,1)S(1)}, u32[]{:S(2)}, u32[]{:S(2)}) %collective-permute-start.2) | collective-permute-done | bytes 65568 | tf_op jit(solution)/shard_map/ppermute | solution.py:388
  12.6 1.4 %collective-permute-done.3.old_got_ref = bf16[128,256]{1,0:T(8,128)(2,1)S(1)} collective-permute-done((bf16[128,256]{1,0:T(8,128)(2,1)S(1)}, bf16[128,256]{1,0:T(8,128)(2,1)S(1)}, u32[]{:S(2)}, u32[]{:S(2)}) %collective-permute-start.3) | collective-permute-done | bytes 65568 | tf_op jit(solution)/shard_map/ppermute | solution.py:392
  14.0 1.2 %shard_map.94 = (bf16[4,512,384]{2,1,0:T(8,128)(2,1)S(1)}, f32[4,512,128]{2,1,0:T(8,128)S(1)}) custom-call(bf16[128,1024]{1,0:T(8,128)(2,1)S(1)} %get-tuple-element.32.q_keep_ref, bf16[128,1024]{1,0:T(8,128)(2,1)S(1)} %collective-permute-done.q_got_ref, bf16[128,256]{1,0:T(8,128)(2,1)S(1)} %get-tuple-element.34.keep_ref, ...), custom_call_target="tpu_custom_call" | custom-call | flops 268435456 | bytes 1048576 | tf_op jit(solution)/shard_map/pallas_call | solution.py:36
  15.9 2.1 %collective-permute-start.5 = (bf16[256,1024]{1,0:T(8,128)(2,1)S(1)}, bf16[256,1024]{1,0:T(8,128)(2,1)S(1)}, u32[]{:S(2)}, u32[]{:S(2)}) collective-permute-start(bf16[256,1024]{1,0:T(8,128)(2,1)S(1)} %shard_map.96.rows_ref), channel_id=1, source_target_pairs={{0,16},{4,0},{8,20},{12,4},{16,24},{20,8},{24,28},{28,12},{1,17},{... | collective-permute-start | bytes 1572872 | tf_op jit(solution)/shard_map/ppermute | solution.py:428
  18.2 1.6 %collective-permute-start.6 = (f32[16,128]{1,0:T(8,128)S(1)}, f32[16,128]{1,0:T(8,128)S(1)}, u32[]{:S(2)}, u32[]{:S(2)}) collective-permute-start(f32[16,128]{1,0:T(8,128)S(1)} %shard_map.97.a_ref), channel_id=1, source_target_pairs={{0,1},{1,0},{2,3},{3,2},{4,5},{5,4},{6,7},{7,6},{8,9},{9,8},{10,11... | collective-permute-start | bytes 24584 | tf_op jit(solution)/shard_map/ppermute | solution.py:430
  19.8 2.1 %collective-permute-done.6.b_ref = f32[16,128]{1,0:T(8,128)S(1)} collective-permute-done((f32[16,128]{1,0:T(8,128)S(1)}, f32[16,128]{1,0:T(8,128)S(1)}, u32[]{:S(2)}, u32[]{:S(2)}) %collective-permute-start.6) | collective-permute-done | bytes 8224 | tf_op jit(solution)/shard_map/ppermute | solution.py:430
  21.9 2.6 %collective-permute-start.7 = (f32[16,128]{1,0:T(8,128)S(1)}, f32[16,128]{1,0:T(8,128)S(1)}, u32[]{:S(2)}, u32[]{:S(2)}) collective-permute-start(f32[16,128]{1,0:T(8,128)S(1)} %shard_map.98.a_ref), channel_id=1, source_target_pairs={{0,2},{1,3},{2,0},{3,1},{4,6},{5,7},{6,4},{7,5},{8,10},{9,11},{10,... | collective-permute-start | bytes 24584 | tf_op jit(solution)/shard_map/ppermute | solution.py:430
  24.5 2.0 %collective-permute-done.7.b_ref = f32[16,128]{1,0:T(8,128)S(1)} collective-permute-done((f32[16,128]{1,0:T(8,128)S(1)}, f32[16,128]{1,0:T(8,128)S(1)}, u32[]{:S(2)}, u32[]{:S(2)}) %collective-permute-start.7) | collective-permute-done | bytes 8224 | tf_op jit(solution)/shard_map/ppermute | solution.py:430
  26.5 0.6 %collective-permute-start.8 = (f32[16,128]{1,0:T(8,128)S(1)}, f32[16,128]{1,0:T(8,128)S(1)}, u32[]{:S(2)}, u32[]{:S(2)}) collective-permute-start(f32[16,128]{1,0:T(8,128)S(1)} %shard_map.99), channel_id=1, source_target_pairs={{0,16},{4,0},{8,20},{12,4},{16,24},{20,8},{24,28},{28,12},{1,17},{... | collective-permute-start | bytes 24584 | tf_op jit(solution)/shard_map/ppermute | solution.py:432
  27.1 2.4 %shard_map.100 = (bf16[8,256,512]{2,1,0:T(8,128)(2,1)S(1)}, bf16[8,128,512]{2,1,0:T(8,128)(2,1)S(1)}, f32[256,1024]{1,0:T(8,128)S(1)}, f32[1,1024]{1,0:T(1,128)S(1)}, f32[1,1024]{1,0:T(1,128)S(1)}) custom-call(f32[16,256]{1,0:T(8,128)} %refs_0_.1, f32[16,256]{1,0:T(8,128)} %refs_1_.1, bf16[256,128]{1,0:T(8,128)(2,1)} %refs_2_.1, bf16[256,128]{1,0:T(8,128)(2,1)} %c_ref.3, ...), custom_call_target="tpu_custom_call" | custom-call | flops 1073741824 | bytes 1048576 | tf_op jit(solution)/shard_map/pallas_call | solution.py:36
  29.5 1.0 %collective-permute-done.8.sums_ref = f32[16,128]{1,0:T(8,128)S(1)} collective-permute-done((f32[16,128]{1,0:T(8,128)S(1)}, f32[16,128]{1,0:T(8,128)S(1)}, u32[]{:S(2)}, u32[]{:S(2)}) %collective-permute-start.8) | collective-permute-done | bytes 8224 | tf_op jit(solution)/shard_map/ppermute | solution.py:432
  31.4 0.9 %collective-permute-done.9.got_ref = bf16[136,512]{1,0:T(8,128)(2,1)S(1)} collective-permute-done((bf16[136,512]{1,0:T(8,128)(2,1)S(1)}, bf16[136,512]{1,0:T(8,128)(2,1)S(1)}, u32[]{:S(2)}, u32[]{:S(2)}) %collective-permute-start.9) | collective-permute-done | bytes 139296 | tf_op jit(solution)/shard_map/ppermute | solution.py:374
  32.5 2.6 %collective-permute-start.11 = (bf16[136,512]{1,0:T(8,128)(2,1)S(1)}, bf16[136,512]{1,0:T(8,128)(2,1)S(1)}, u32[]{:S(2)}, u32[]{:S(2)}) collective-permute-start(bf16[136,512]{1,0:T(8,128)(2,1)S(1)} %get-tuple-element.52), channel_id=1, source_target_pairs={{0,16},{4,20},{8,24},{12,28},{16,0},{20,4},{24,8},{28,12},{1,17},{... | collective-permute-start | bytes 417800 | tf_op jit(solution)/shard_map/ppermute | solution.py:440
  35.0 2.9 %collective-permute-start.12 = (bf16[128,512]{1,0:T(8,128)(2,1)S(1)}, bf16[128,512]{1,0:T(8,128)(2,1)S(1)}, u32[]{:S(2)}, u32[]{:S(2)}) collective-permute-start(bf16[128,512]{1,0:T(8,128)(2,1)S(1)} %get-tuple-element.53), channel_id=1, source_target_pairs={{0,24},{4,28},{8,0},{12,4},{16,20},{20,16},{24,8},{28,12},{1,25},{... | collective-permute-start | bytes 393224 | tf_op jit(solution)/shard_map/ppermute | solution.py:440
  37.9 5.2 %collective-permute-done.12.both_ref = bf16[128,512]{1,0:T(8,128)(2,1)S(1)} collective-permute-done((bf16[128,512]{1,0:T(8,128)(2,1)S(1)}, bf16[128,512]{1,0:T(8,128)(2,1)S(1)}, u32[]{:S(2)}, u32[]{:S(2)}) %collective-permute-start.12) | collective-permute-done | bytes 131104 | tf_op jit(solution)/shard_map/ppermute | solution.py:440
  43.3 0.7 %shard_map.103 = (f32[256,512]{1,0:T(8,128)S(1)}, f32[256,512]{1,0:T(8,128)S(1)}) custom-call(bf16[256,512]{1,0:T(8,128)(2,1)S(1)} %get-tuple-element.44.x_keep_ref, bf16[256,512]{1,0:T(8,128)(2,1)S(1)} %get-tuple-element.45.x_send_ref, bf16[8,256,512]{2,1,0:T(8,128)(2,1)S(1)} %get-tuple-element.46.mix_ref, f32[1,1024]{1,0:T(1,128)S(1)} %get-tuple-element.47.skip_ref), custom_call_target="tpu_custom_call" | custom-call | flops 536870912 | bytes 1048576 | tf_op jit(solution)/shard_map/pallas_call | solution.py:36
  44.7 1.0 %shard_map.107 = bf16[256,1024]{1,0:T(8,128)(2,1)} custom-call(f32[256,512]{1,0:T(8,128)S(1)} %get-tuple-element.48.local_ref, f32[256,1024]{1,0:T(8,128)S(1)} %get-tuple-element.49.scale_ref, bf16[256,128]{1,0:T(8,128)(2,1)S(1)} %copy-done, bf16[128,512]{1,0:T(8,128)(2,1)S(1)} %collective-permute-done.13.enter_ref, bf16[256,512]{1,0:T(8,128)(2,1)S(1)} %shard_map.106.refs_0_), custom_call_target="tpu_custom_call" | custom-call | flops 134217728 | bytes 1048576 | tf_op jit(solution)/shard_map/pallas_call | solution.py:36
  (25 shorter events, 2.8 us)
Async XLA Ops:
  1.0 12.9 %collective-permute-start = (bf16[128,1024]{1,0:T(8,128)(2,1)S(1)}, bf16[128,1024]{1,0:T(8,128)(2,1)S(1)}, u32[]{:S(2)}, u32[]{:S(2)}) collective-permute-start(bf16[128,1024]{1,0:T(8,128)(2,1)S(1)} %get-tuple-element.33), channel_id=1, source_target_pairs={{0,4},{4,0},{8,12},{12,8},{16,20},{20,16},{24,28},{28,24},{1,5},{5... | collective-permute-start | bytes 786440 | tf_op jit(solution)/shard_map/ppermute | solution.py:374
  2.5 1.3 %collective-permute-start.1 = (bf16[128,512]{1,0:T(8,128)(2,1)S(1)}, bf16[128,512]{1,0:T(8,128)(2,1)S(1)}, u32[]{:S(2)}, u32[]{:S(2)}) collective-permute-start(bf16[128,512]{1,0:T(8,128)(2,1)S(1)} %get-tuple-element.35), channel_id=1, source_target_pairs={{0,4},{4,0},{8,12},{12,8},{16,20},{20,16},{24,28},{28,24},{1,5},{5... | collective-permute-start | bytes 393224 | tf_op jit(solution)/shard_map/ppermute | solution.py:374
  3.8 11.7 %collective-permute-start.4 = (bf16[128,512]{1,0:T(8,128)(2,1)S(1)}, bf16[128,512]{1,0:T(8,128)(2,1)S(1)}, u32[]{:S(2)}, u32[]{:S(2)}) collective-permute-start(bf16[128,512]{1,0:T(8,128)(2,1)S(1)} %get-tuple-element.41), channel_id=1, source_target_pairs={{0,8},{4,12},{8,16},{12,20},{16,24},{20,28},{24,4},{28,0},{1,9},{5... | collective-permute-start | bytes 393224 | tf_op jit(solution)/shard_map/ppermute | solution.py:393
  6.5 6.1 %collective-permute-start.2 = (bf16[128,256]{1,0:T(8,128)(2,1)S(1)}, bf16[128,256]{1,0:T(8,128)(2,1)S(1)}, u32[]{:S(2)}, u32[]{:S(2)}) collective-permute-start(bf16[128,256]{1,0:T(8,128)(2,1)S(1)} %get-tuple-element.34.keep_ref), channel_id=1, source_target_pairs={{0,8},{4,12},{8,16},{12,20},{16,24},{20,28},{24,4},{28,0},{1,9},{5... | collective-permute-start | bytes 196616 | tf_op jit(solution)/shard_map/ppermute | solution.py:388
  8.0 6.0 %collective-permute-start.3 = (bf16[128,256]{1,0:T(8,128)(2,1)S(1)}, bf16[128,256]{1,0:T(8,128)(2,1)S(1)}, u32[]{:S(2)}, u32[]{:S(2)}) collective-permute-start(bf16[128,256]{1,0:T(8,128)(2,1)S(1)} %get-tuple-element.37.got_ref), channel_id=1, source_target_pairs={{0,8},{4,12},{8,16},{12,20},{16,24},{20,28},{24,4},{28,0},{1,9},{5... | collective-permute-start | bytes 196616 | tf_op jit(solution)/shard_map/ppermute | solution.py:392
  15.9 14.6 %collective-permute-start.5 = (bf16[256,1024]{1,0:T(8,128)(2,1)S(1)}, bf16[256,1024]{1,0:T(8,128)(2,1)S(1)}, u32[]{:S(2)}, u32[]{:S(2)}) collective-permute-start(bf16[256,1024]{1,0:T(8,128)(2,1)S(1)} %shard_map.96.rows_ref), channel_id=1, source_target_pairs={{0,16},{4,0},{8,20},{12,4},{16,24},{20,8},{24,28},{28,12},{1,17},{... | collective-permute-start | bytes 1572872 | tf_op jit(solution)/shard_map/ppermute | solution.py:428
  18.2 12.3 %copy-start.1 = (f32[1024]{0:T(1024)S(1)}, f32[1024]{0:T(1024)}, u32[]{:S(2)}) copy-start(f32[1024]{0:T(1024)} %param.12) | copy-start | bytes 12292
  18.2 3.7 %collective-permute-start.6 = (f32[16,128]{1,0:T(8,128)S(1)}, f32[16,128]{1,0:T(8,128)S(1)}, u32[]{:S(2)}, u32[]{:S(2)}) collective-permute-start(f32[16,128]{1,0:T(8,128)S(1)} %shard_map.97.a_ref), channel_id=1, source_target_pairs={{0,1},{1,0},{2,3},{3,2},{4,5},{5,4},{6,7},{7,6},{8,9},{9,8},{10,11... | collective-permute-start | bytes 24584 | tf_op jit(solution)/shard_map/ppermute | solution.py:430
  21.9 4.5 %collective-permute-start.7 = (f32[16,128]{1,0:T(8,128)S(1)}, f32[16,128]{1,0:T(8,128)S(1)}, u32[]{:S(2)}, u32[]{:S(2)}) collective-permute-start(f32[16,128]{1,0:T(8,128)S(1)} %shard_map.98.a_ref), channel_id=1, source_target_pairs={{0,2},{1,3},{2,0},{3,1},{4,6},{5,7},{6,4},{7,5},{8,10},{9,11},{10,... | collective-permute-start | bytes 24584 | tf_op jit(solution)/shard_map/ppermute | solution.py:430
  26.5 4.0 %collective-permute-start.8 = (f32[16,128]{1,0:T(8,128)S(1)}, f32[16,128]{1,0:T(8,128)S(1)}, u32[]{:S(2)}, u32[]{:S(2)}) collective-permute-start(f32[16,128]{1,0:T(8,128)S(1)} %shard_map.99), channel_id=1, source_target_pairs={{0,16},{4,0},{8,20},{12,4},{16,24},{20,8},{24,28},{28,12},{1,17},{... | collective-permute-start | bytes 24584 | tf_op jit(solution)/shard_map/ppermute | solution.py:432
  30.9 1.4 %collective-permute-start.9 = (bf16[136,512]{1,0:T(8,128)(2,1)S(1)}, bf16[136,512]{1,0:T(8,128)(2,1)S(1)}, u32[]{:S(2)}, u32[]{:S(2)}) collective-permute-start(bf16[136,512]{1,0:T(8,128)(2,1)S(1)} %get-tuple-element.51), channel_id=1, source_target_pairs={{0,4},{4,0},{8,12},{12,8},{16,20},{20,16},{24,28},{28,24},{1,5},{5... | collective-permute-start | bytes 417800 | tf_op jit(solution)/shard_map/ppermute | solution.py:374
  31.4 12.6 %copy-start = (bf16[256,128]{1,0:T(8,128)(2,1)S(1)}, bf16[256,128]{1,0:T(8,128)(2,1)}, u32[]{:S(2)}) copy-start(bf16[256,128]{1,0:T(8,128)(2,1)} %c_ref.3) | copy-start | bytes 196612
  32.5 10.6 %collective-permute-start.11 = (bf16[136,512]{1,0:T(8,128)(2,1)S(1)}, bf16[136,512]{1,0:T(8,128)(2,1)S(1)}, u32[]{:S(2)}, u32[]{:S(2)}) collective-permute-start(bf16[136,512]{1,0:T(8,128)(2,1)S(1)} %get-tuple-element.52), channel_id=1, source_target_pairs={{0,16},{4,20},{8,24},{12,28},{16,0},{20,4},{24,8},{28,12},{1,17},{... | collective-permute-start | bytes 417800 | tf_op jit(solution)/shard_map/ppermute | solution.py:440
  35.0 8.1 %collective-permute-start.10 = (bf16[136,512]{1,0:T(8,128)(2,1)S(1)}, bf16[136,512]{1,0:T(8,128)(2,1)S(1)}, u32[]{:S(2)}, u32[]{:S(2)}) collective-permute-start(bf16[136,512]{1,0:T(8,128)(2,1)S(1)} %get-tuple-element.52), channel_id=1, source_target_pairs={{0,8},{4,12},{8,16},{12,20},{16,24},{20,28},{24,0},{28,4},{1,9},{5... | collective-permute-start | bytes 417800 | tf_op jit(solution)/shard_map/ppermute | solution.py:440
  35.0 8.1 %collective-permute-start.12 = (bf16[128,512]{1,0:T(8,128)(2,1)S(1)}, bf16[128,512]{1,0:T(8,128)(2,1)S(1)}, u32[]{:S(2)}, u32[]{:S(2)}) collective-permute-start(bf16[128,512]{1,0:T(8,128)(2,1)S(1)} %get-tuple-element.53), channel_id=1, source_target_pairs={{0,24},{4,28},{8,0},{12,4},{16,20},{20,16},{24,8},{28,12},{1,25},{... | collective-permute-start | bytes 393224 | tf_op jit(solution)/shard_map/ppermute | solution.py:440
  43.2 1.4 %collective-permute-start.13 = (bf16[128,512]{1,0:T(8,128)(2,1)S(1)}, bf16[128,512]{1,0:T(8,128)(2,1)S(1)}, u32[]{:S(2)}, u32[]{:S(2)}) collective-permute-start(bf16[128,512]{1,0:T(8,128)(2,1)S(1)} %get-tuple-element.56), channel_id=1, source_target_pairs={{0,4},{4,0},{8,12},{12,8},{16,20},{20,16},{24,28},{28,24},{1,5},{5... | collective-permute-start | bytes 393224 | tf_op jit(solution)/shard_map/ppermute | solution.py:374
